TPU v7x, 256 devices: a whole 4x4x8 slice. The times are simulated.
256 devices in a mesh: tm: 32 (over z, y), grid: 8 (over x, core).
Axes of the slice: x: 4, y: 4, z: 8, core: 2. Of those that a mesh axis runs over, the one named last changes fastest.
Arguments:
- departure: float32 [64, 128, 3, 1024], P('tm', 'grid'), may hold values from -6 to 6
- obs_weight: float32 [64, 128], P('tm', 'grid'), may hold values from 0.2 to 2
- obs_block: int32 [64, 128], P('tm', 'grid'), may hold values from 0 to 7
- coarse_decay: float32 [3, 64, 1024], P(None, 'grid'), may hold values from 0.95 to 1
Outputs:
- adjoint: float32 [64, 3, 64, 1024], P('tm', None, 'grid')
- misfit: float32 [], replicated
- changes: float32 [3], replicated
Inputs may be any that keep to these rules, and one draw needn't show every extreme that they name: `obs_block`: several observations may name the same block.
All inputs are finite; a program needn't handle non-finite values.
Results may differ from a plain program's by a relative error of at most 0.0003.
Values sent between devices are 32-bit elements; how exact they have to be, the bound alone decides.
No kernel may reach another device: no remote copies, remote signals or barrier semaphores. Data moves between devices by JAX's collectives and lax.ppermute only.
A program may use at most 64 MiB of HBM per device.

v0:
```python
import functools

import jax
import jax.numpy as jnp
from jax import lax
from jax.sharding import Mesh
from jax.sharding import PartitionSpec as P

STEPS = 4
ITERS = 3
TILE_ROWS = 8
TILE_COLS = 128
GRID = ("grid_0", "grid_1")
TM = ("tm_0", "tm_1")
TM_GRID = ("tm_0", "tm_1", "grid_0", "grid_1")


wave_coef = 0.6
diffusion = 0.05
coriolis = 0.1
epsilon = 1e-06


def padded_2(value, sides, width):
    for axis, dim in sides:
        devices, length = (lax.axis_size(axis), value.shape[dim])
        up = [(i, (i + 1) % devices) for i in range(devices - 1)]
        down = [(j, i) for i, j in up]
        last = lax.slice_in_dim(value, length - width, length, axis=dim)
        first = lax.slice_in_dim(value, 0, width, axis=dim)
        before = lax.ppermute(last, axis, up)
        after = lax.ppermute(first, axis, down)
        value = jnp.concatenate([before, value, after], axis=dim)
    return value


def nothing_yet(value, identity):
    return jax.tree.map(
        lambda part, zero: jnp.zeros_like(part) + jnp.asarray(zero, part.dtype), value, identity
    )


def carried_in(value, axes, combine, identity):
    before = start = nothing_yet(value, identity)
    so_far = value
    for axis in reversed(axes):
        devices, here = (lax.axis_size(axis), lax.axis_index(axis))
        pieces = jax.tree.map(lambda part: lax.all_gather(part, axis), so_far)
        inside, so_far = (start, start)
        for k in reversed(range(devices)):
            passed = k > here
            so_far = combine(so_far, jax.tree.map(lambda part: part[k], pieces))
            inside = jax.tree.map(lambda new, old: jnp.where(passed, new, old), so_far, inside)
        before = combine(inside, before)
    return before


def shifted(value, axis, by):
    devices = lax.axis_size(axis)
    pairs = [(i, i + by) for i in range(devices) if 0 <= i + by < devices]
    return lax.ppermute(value, axis, pairs)


def over_axes(value, axes):
    return functools.reduce(lax.psum, axes, value)


def along_lon(values):
    return 0.5 * (jnp.roll(values, -1, -1) - jnp.roll(values, 1, -1))


def pad_rows(values):
    return jnp.pad(values, ((0, 0), (1, 1), (0, 0)))


def along_lat(values):
    padded = pad_rows(values)
    return 0.5 * (padded[:, 2:] - padded[:, :-2])


def laplace(values):
    padded = pad_rows(values)
    return (
        padded[:, 2:]
        + padded[:, :-2]
        + jnp.roll(values, -1, -1)
        + jnp.roll(values, 1, -1)
        - 4.0 * values
    )


def sweep_once(fields, inside):
    height, zonal, merid = (fields[:, 0], fields[:, 1], fields[:, 2])
    weight = inside[None, :, None]
    height_new = (
        height + wave_coef * (along_lon(zonal) + along_lat(merid)) + diffusion * laplace(height)
    ) * weight
    zonal_new = (
        zonal + wave_coef * along_lon(height_new) + coriolis * merid + diffusion * laplace(zonal)
    ) * weight
    merid_new = (
        merid + wave_coef * along_lat(height_new) - coriolis * zonal + diffusion * laplace(merid)
    ) * weight
    return jnp.stack([height_new, zonal_new, merid_new], axis=1)


def spread_tiles(scaled, blocks, row_count, lon_count):
    tile_rows_n = row_count // TILE_ROWS
    tile_cols_n = lon_count // TILE_COLS
    choose = (blocks[..., None] == jnp.arange(tile_rows_n * tile_cols_n, dtype=jnp.int32)).astype(
        jnp.float32
    )
    tiles = jnp.einsum("sob,soct->sbct", choose, scaled, precision=lax.Precision.HIGHEST)
    leading = scaled.shape[0]
    tiles = tiles.reshape(leading, tile_rows_n, tile_cols_n, 3, TILE_ROWS, TILE_COLS).transpose(
        0, 3, 1, 4, 2, 5
    )
    return tiles.reshape(leading, 3, row_count, lon_count)


def inside_rows(row_count, margin):
    band_index = lax.axis_index(GRID)
    band_count = lax.axis_size(GRID)
    global_row = band_index * row_count - margin + jnp.arange(row_count + 2 * margin)
    return ((global_row >= 0) & (global_row < row_count * band_count)).astype(jnp.float32)


def propagate(fields):
    row_count = fields.shape[2]
    margin = 2 * STEPS
    extended = padded_2(fields, ((GRID, 2),), margin)
    inside = inside_rows(row_count, margin)
    for repeat in range(STEPS):
        extended = sweep_once(extended, inside)[:, :, 2:-2]
        inside = inside[2:-2]
    return extended


def run_chain(correction, coarse_decay, start):
    values = []
    current = start
    for offset in reversed(range(correction.shape[0])):
        current = coarse_decay * current + correction[offset]
        values.append(current)
    return jnp.stack(values[::-1], axis=0)


def compose_pair(earlier, later):
    return (later[0] * earlier[0], later[0] * earlier[1] + later[1])


def per_device(departure, obs_weight, obs_block, coarse_decay):
    sub_count = departure.shape[0]
    row_count = coarse_decay.shape[1]
    lon_count = coarse_decay.shape[2]
    window_total = lax.axis_size(TM) * sub_count
    window_first = lax.axis_index(TM) * sub_count
    position = (window_first + jnp.arange(sub_count)).astype(jnp.float32)
    emphasis = 1.0 + 2.0 * position / (window_total - 1)
    local_misfit = 0.5 * jnp.sum(
        emphasis[:, None] * obs_weight * jnp.sum(departure * departure, axis=(2, 3))
    )
    scaled = departure * (emphasis[:, None] * obs_weight)[:, :, None, None]
    forcing = spread_tiles(scaled, obs_block, row_count, lon_count)
    factor_here = coarse_decay**sub_count
    zeros_field = jnp.zeros_like(coarse_decay)

    def backward(correction):
        offset_here = run_chain(correction, coarse_decay, zeros_field)[0]
        composed = carried_in(
            (factor_here, offset_here), TM, compose_pair, (jnp.ones_like(factor_here), zeros_field)
        )
        start = composed[1]
        return run_chain(correction, coarse_decay, start)

    adjoint = backward(forcing)
    changes = []
    sizes = []
    for iteration in range(ITERS):
        following = shifted(adjoint[:1], TM, -1)
        above = jnp.concatenate([adjoint[1:], following], axis=0)
        correction = propagate(above) - coarse_decay * above + forcing
        renewed = backward(correction)
        weights = emphasis[:, None, None, None]
        local_change = jnp.sum(weights * (renewed - adjoint) ** 2)
        local_size = jnp.sum(weights * renewed**2)
        changes.append(local_change)
        sizes.append(local_size)
        adjoint = renewed
    misfit, change_sums, size_sums = (
        over_axes(local_misfit, TM_GRID),
        over_axes(jnp.stack(changes), TM_GRID),
        over_axes(jnp.stack(sizes), TM_GRID),
    )
    change_totals = change_sums / (size_sums + epsilon)
    return (adjoint, misfit, change_totals)


def solution(mesh):
    split = Mesh(mesh.devices.reshape(8, 4, 4, 2), ("tm_0", "tm_1", "grid_0", "grid_1"))
    return jax.shard_map(
        per_device,
        mesh=split,
        in_specs=(P(TM, GRID, None, None), P(TM, GRID), P(TM, GRID), P(None, GRID, None)),
        out_specs=(P(TM, None, GRID, None), P(), P()),
        check_vma=False,
    )
```

profile of v0, /device:TPU:1, one launch (start us, length us, event | category | flops | bytes accessed | tf_op | source)
XLA Modules:
  0.0 322.6 jit_solution(13516847098785530859)
XLA Ops:
  4.5 12.1 %all-gather = f32[12,8,1024]{2,1,0:T(8,128)S(1)} all-gather(f32[3,8,1024]{2,1,0:T(8,128)S(1)} %get-tuple-element.140), channel_id=2, replica_groups=mesh['tm_0'=8,'tm_1'=4,'grid_0'=4,'grid_1'=2] {'tm_1'}, dimensions={0}, use_global_device_ids=true | all-gather | bytes 491520 | tf_op jit(solution)/shard_map/all_gather | solution.py:48
  16.6 9.8 %all-gather.1 = f32[12,8,1024]{2,1,0:T(8,128)S(1)} all-gather(f32[3,8,1024]{2,1,0:T(8,128)S(1)} %get-tuple-element.139), channel_id=3, replica_groups=mesh['tm_0'=8,'tm_1'=4,'grid_0'=4,'grid_1'=2] {'tm_1'}, dimensions={0}, use_global_device_ids=true | all-gather | bytes 491520 | tf_op jit(solution)/shard_map/all_gather | solution.py:48
  26.5 24.0 %all_gather.24 = f32[8,3,8,1024]{3,2,1,0:T(8,128)S(1)} all-gather(f32[1,3,8,1024]{3,2,1,0:T(8,128)S(1)} %get-tuple-element.41), channel_id=1, replica_groups=mesh['tm_0'=8,'tm_1'=4,'grid_0'=4,'grid_1'=2] {'tm_0'}, dimensions={0}, use_global_device_ids=true | all-gather | bytes 884736 | tf_op jit(solution)/shard_map/all_gather | solution.py:48
  50.5 20.9 %all_gather.26 = f32[8,3,8,1024]{3,2,1,0:T(8,128)S(1)} all-gather(f32[1,3,8,1024]{3,2,1,0:T(8,128)S(1)} %get-tuple-element.42), channel_id=1, replica_groups=mesh['tm_0'=8,'tm_1'=4,'grid_0'=4,'grid_1'=2] {'tm_0'}, dimensions={0}, use_global_device_ids=true | all-gather | bytes 884736 | tf_op jit(solution)/shard_map/all_gather | solution.py:48
  72.9 4.4 %collective-permute-done = f32[1,3,8,1024]{3,2,1,0:T(8,128)S(1)} collective-permute-done((f32[1,3,8,1024]{3,2,1,0:T(8,128)S(1)}, f32[1,3,8,1024]{3,2,1,0:T(8,128)S(1)}, u32[]{:S(2)}, u32[]{:S(2)}) %collective-permute-start) | collective-permute-done | bytes 98336 | tf_op jit(solution)/shard_map/ppermute | solution.py:61
  77.3 19.9 %collective-permute-start.1 = (f32[2,3,8,1024]{3,2,0,1:T(8,128)S(1)}, f32[2,3,8,1024]{3,2,0,1:T(8,128)S(1)}, u32[]{:S(2)}, u32[]{:S(2)}) collective-permute-start(f32[2,3,8,1024]{3,2,0,1:T(8,128)S(1)} %copy.20), channel_id=1, source_target_pairs={{0,1},{1,2},{2,3},{3,4},{4,5},{5,6},{6,7},{8,9},{9,10},{10,11},{11... | collective-permute-start | bytes 589832 | tf_op jit(solution)/shard_map/ppermute | solution.py:31
  99.9 4.6 %collective-permute-done.2 = f32[2,3,8,1024]{3,2,0,1:T(8,128)S(1)} collective-permute-done((f32[2,3,8,1024]{3,2,0,1:T(8,128)S(1)}, f32[2,3,8,1024]{3,2,0,1:T(8,128)S(1)}, u32[]{:S(2)}, u32[]{:S(2)}) %collective-permute-start.2) | collective-permute-done | bytes 196640 | tf_op jit(solution)/shard_map/ppermute | solution.py:32
  109.8 11.9 %all-gather.2 = f32[12,8,1024]{2,1,0:T(8,128)S(1)} all-gather(f32[3,8,1024]{2,1,0:T(8,128)S(1)} %multiply_add_fusion.3), channel_id=4, replica_groups=mesh['tm_0'=8,'tm_1'=4,'grid_0'=4,'grid_1'=2] {'tm_1'}, dimensions={0}, use_global_device_ids=true | all-gather | bytes 491520 | tf_op jit(solution)/shard_map/all_gather | solution.py:48
  121.8 20.8 %all_gather.56 = f32[8,3,8,1024]{3,2,1,0:T(8,128)S(1)} all-gather(f32[1,3,8,1024]{3,2,1,0:T(8,128)S(1)} %bitcast_add_fusion.8), channel_id=1, replica_groups=mesh['tm_0'=8,'tm_1'=4,'grid_0'=4,'grid_1'=2] {'tm_0'}, dimensions={0}, use_global_device_ids=true | all-gather | bytes 884736 | tf_op jit(solution)/shard_map/all_gather | solution.py:48
  144.2 4.6 %collective-permute-done.3 = f32[1,3,8,1024]{3,2,1,0:T(8,128)S(1)} collective-permute-done((f32[1,3,8,1024]{3,2,1,0:T(8,128)S(1)}, f32[1,3,8,1024]{3,2,1,0:T(8,128)S(1)}, u32[]{:S(2)}, u32[]{:S(2)}) %collective-permute-start.3) | collective-permute-done | bytes 98336 | tf_op jit(solution)/shard_map/ppermute | solution.py:61
  148.8 11.0 %collective-permute-start.4 = (f32[2,3,8,1024]{3,2,0,1:T(8,128)S(1)}, f32[2,3,8,1024]{3,2,0,1:T(8,128)S(1)}, u32[]{:S(2)}, u32[]{:S(2)}) collective-permute-start(f32[2,3,8,1024]{3,2,0,1:T(8,128)S(1)} %copy.25), channel_id=1, source_target_pairs={{0,1},{1,2},{2,3},{3,4},{4,5},{5,6},{6,7},{8,9},{9,10},{10,11},{11... | collective-permute-start | bytes 589832 | tf_op jit(solution)/shard_map/ppermute | solution.py:31
  162.4 4.4 %collective-permute-done.5 = f32[2,3,8,1024]{3,2,0,1:T(8,128)S(1)} collective-permute-done((f32[2,3,8,1024]{3,2,0,1:T(8,128)S(1)}, f32[2,3,8,1024]{3,2,0,1:T(8,128)S(1)}, u32[]{:S(2)}, u32[]{:S(2)}) %collective-permute-start.5) | collective-permute-done | bytes 196640 | tf_op jit(solution)/shard_map/ppermute | solution.py:32
  172.2 12.1 %all-gather.3 = f32[12,8,1024]{2,1,0:T(8,128)S(1)} all-gather(f32[3,8,1024]{2,1,0:T(8,128)S(1)} %multiply_add_fusion.2), channel_id=5, replica_groups=mesh['tm_0'=8,'tm_1'=4,'grid_0'=4,'grid_1'=2] {'tm_1'}, dimensions={0}, use_global_device_ids=true | all-gather | bytes 491520 | tf_op jit(solution)/shard_map/all_gather | solution.py:48
  184.4 20.7 %all_gather.58 = f32[8,3,8,1024]{3,2,1,0:T(8,128)S(1)} all-gather(f32[1,3,8,1024]{3,2,1,0:T(8,128)S(1)} %bitcast_add_fusion.4), channel_id=1, replica_groups=mesh['tm_0'=8,'tm_1'=4,'grid_0'=4,'grid_1'=2] {'tm_0'}, dimensions={0}, use_global_device_ids=true | all-gather | bytes 884736 | tf_op jit(solution)/shard_map/all_gather | solution.py:48
  206.7 4.6 %collective-permute-done.6 = f32[1,3,8,1024]{3,2,0,1:T(8,128)S(1)} collective-permute-done((f32[1,3,8,1024]{3,2,0,1:T(8,128)S(1)}, f32[1,3,8,1024]{3,2,0,1:T(8,128)S(1)}, u32[]{:S(2)}, u32[]{:S(2)}) %collective-permute-start.6) | collective-permute-done | bytes 98336 | tf_op jit(solution)/shard_map/ppermute | solution.py:61
  211.3 11.1 %collective-permute-start.7 = (f32[2,3,8,1024]{3,2,0,1:T(8,128)S(1)}, f32[2,3,8,1024]{3,2,0,1:T(8,128)S(1)}, u32[]{:S(2)}, u32[]{:S(2)}) collective-permute-start(f32[2,3,8,1024]{3,2,0,1:T(8,128)S(1)} %pad_maximum_fusion.17), channel_id=1, source_target_pairs={{0,1},{1,2},{2,3},{3,4},{4,5},{5,6},{6,7},{8,9},{9,10},{10,11},{11... | collective-permute-start | bytes 589832 | tf_op jit(solution)/shard_map/ppermute | solution.py:31
  222.4 2.1 collective-permute-start.8
  225.2 4.2 %collective-permute-done.8 = f32[2,3,8,1024]{3,2,0,1:T(8,128)S(1)} collective-permute-done((f32[2,3,8,1024]{3,2,0,1:T(8,128)S(1)}, f32[2,3,8,1024]{3,2,0,1:T(8,128)S(1)}, u32[]{:S(2)}, u32[]{:S(2)}) %collective-permute-start.8) | collective-permute-done | bytes 196640 | tf_op jit(solution)/shard_map/ppermute | solution.py:32
  234.9 12.1 %all-gather.4 = f32[12,8,1024]{2,1,0:T(8,128)S(1)} all-gather(f32[3,8,1024]{2,1,0:T(8,128)S(1)} %multiply_add_fusion), channel_id=6, replica_groups=mesh['tm_0'=8,'tm_1'=4,'grid_0'=4,'grid_1'=2] {'tm_1'}, dimensions={0}, use_global_device_ids=true | all-gather | bytes 491520 | tf_op jit(solution)/shard_map/all_gather | solution.py:48
  247.0 21.5 %all_gather.60 = f32[8,3,8,1024]{3,2,1,0:T(8,128)S(1)} all-gather(f32[1,3,8,1024]{3,2,1,0:T(8,128)S(1)} %bitcast_add_fusion), channel_id=1, replica_groups=mesh['tm_0'=8,'tm_1'=4,'grid_0'=4,'grid_1'=2] {'tm_0'}, dimensions={0}, use_global_device_ids=true | all-gather | bytes 884736 | tf_op jit(solution)/shard_map/all_gather | solution.py:48
  274.1 13.0 %all-reduce.48 = (f32[]{:T(128)}, f32[3]{0:T(128)S(1)}, f32[3]{0:T(128)S(1)}) all-reduce(f32[]{:T(128)S(6)} %mul.1346, f32[3]{0:T(128)S(1)} %pad_maximum_fusion.37, f32[3]{0:T(128)S(1)} %pad_maximum_fusion.38), channel_id=1, replica_groups=mesh['tm_0'=8,'tm_1'=4,'grid_0'=4,'grid_1'=2] {'tm_0'}, use_global_device_ids=true, to_apply=%region_2.3 | all-reduce | flops 7 | bytes 56 | tf_op jit(solution)/shard_map/psum | solution.py:65
  287.2 10.1 %all-reduce.50 = (f32[]{:T(128)}, f32[3]{0:T(128)S(1)}, f32[3]{0:T(128)S(1)}) all-reduce(f32[]{:T(128)} %get-tuple-element.9, f32[3]{0:T(128)S(1)} %get-tuple-element.10, f32[3]{0:T(128)S(1)} %get-tuple-element.11), channel_id=1, replica_groups=mesh['tm_0'=8,'tm_1'=4,'grid_0'=4,'grid_1'=2] {'tm_1'}, use_global_device_ids=true, to_apply=%region_3.4 | all-reduce | flops 7 | bytes 56 | tf_op jit(solution)/shard_map/psum | solution.py:65
  297.3 8.3 %all-reduce.49 = (f32[]{:T(128)}, f32[3]{0:T(128)S(1)}, f32[3]{0:T(128)S(1)}) all-reduce(f32[]{:T(128)} %get-tuple-element.15, f32[3]{0:T(128)S(1)} %get-tuple-element.16, f32[3]{0:T(128)S(1)} %get-tuple-element.17), channel_id=1, replica_groups=mesh['tm_0'=8,'tm_1'=4,'grid_0'=4,'grid_1'=2] {'grid_0'}, use_global_device_ids=true, to_apply=%region_4.5 | all-reduce | flops 7 | bytes 56 | tf_op jit(solution)/shard_map/psum | solution.py:65
  305.5 16.6 %all-reduce.51 = (f32[]{:T(128)}, f32[3]{0:T(128)S(1)}, f32[3]{0:T(128)S(1)}) all-reduce(f32[]{:T(128)} %get-tuple-element.12, f32[3]{0:T(128)S(1)} %get-tuple-element.13, f32[3]{0:T(128)S(1)} %get-tuple-element.14), channel_id=1, replica_groups=mesh['tm_0'=8,'tm_1'=4,'grid_0'=4,'grid_1'=2] {'grid_1'}, use_global_device_ids=true, to_apply=%region_5.6 | all-reduce | flops 7 | bytes 56 | tf_op jit(solution)/shard_map/psum | solution.py:65
  (220 shorter events, 35.5 us)
Async XLA Ops:
  0.6 1.9 copy-start.1
  0.7 1.2 copy-start.3
  2.5 0.7 copy-start.2
  3.6 0.9 copy-start
  71.6 5.7 %collective-permute-start = (f32[1,3,8,1024]{3,2,1,0:T(8,128)S(1)}, f32[1,3,8,1024]{3,2,1,0:T(8,128)S(1)}, u32[]{:S(2)}, u32[]{:S(2)}) collective-permute-start(f32[1,3,8,1024]{3,2,1,0:T(8,128)S(1)} %get-tuple-element.30), channel_id=1, source_target_pairs={{8,0},{16,8},{24,16},{32,24},{40,32},{48,40},{56,48},{64,56},{72,6... | collective-permute-start | bytes 294920 | tf_op jit(solution)/shard_map/ppermute | solution.py:61
  77.3 22.6 %collective-permute-start.1 = (f32[2,3,8,1024]{3,2,0,1:T(8,128)S(1)}, f32[2,3,8,1024]{3,2,0,1:T(8,128)S(1)}, u32[]{:S(2)}, u32[]{:S(2)}) collective-permute-start(f32[2,3,8,1024]{3,2,0,1:T(8,128)S(1)} %copy.20), channel_id=1, source_target_pairs={{0,1},{1,2},{2,3},{3,4},{4,5},{5,6},{6,7},{8,9},{9,10},{10,11},{11... | collective-permute-start | bytes 589832 | tf_op jit(solution)/shard_map/ppermute | solution.py:31
  97.5 7.0 %collective-permute-start.2 = (f32[2,3,8,1024]{3,2,0,1:T(8,128)S(1)}, f32[2,3,8,1024]{3,2,0,1:T(8,128)S(1)}, u32[]{:S(2)}, u32[]{:S(2)}) collective-permute-start(f32[2,3,8,1024]{3,2,0,1:T(8,128)S(1)} %copy.20), channel_id=1, source_target_pairs={{1,0},{2,1},{3,2},{4,3},{5,4},{6,5},{7,6},{9,8},{10,9},{11,10},{12... | collective-permute-start | bytes 589832 | tf_op jit(solution)/shard_map/ppermute | solution.py:32
  142.9 5.9 %collective-permute-start.3 = (f32[1,3,8,1024]{3,2,1,0:T(8,128)S(1)}, f32[1,3,8,1024]{3,2,1,0:T(8,128)S(1)}, u32[]{:S(2)}, u32[]{:S(2)}) collective-permute-start(f32[1,3,8,1024]{3,2,1,0:T(8,128)S(1)} %get-tuple-element.28), channel_id=1, source_target_pairs={{8,0},{16,8},{24,16},{32,24},{40,32},{48,40},{56,48},{64,56},{72,6... | collective-permute-start | bytes 294920 | tf_op jit(solution)/shard_map/ppermute | solution.py:61
  148.8 13.6 %collective-permute-start.4 = (f32[2,3,8,1024]{3,2,0,1:T(8,128)S(1)}, f32[2,3,8,1024]{3,2,0,1:T(8,128)S(1)}, u32[]{:S(2)}, u32[]{:S(2)}) collective-permute-start(f32[2,3,8,1024]{3,2,0,1:T(8,128)S(1)} %copy.25), channel_id=1, source_target_pairs={{0,1},{1,2},{2,3},{3,4},{4,5},{5,6},{6,7},{8,9},{9,10},{10,11},{11... | collective-permute-start | bytes 589832 | tf_op jit(solution)/shard_map/ppermute | solution.py:31
  159.7 7.0 %collective-permute-start.5 = (f32[2,3,8,1024]{3,2,0,1:T(8,128)S(1)}, f32[2,3,8,1024]{3,2,0,1:T(8,128)S(1)}, u32[]{:S(2)}, u32[]{:S(2)}) collective-permute-start(f32[2,3,8,1024]{3,2,0,1:T(8,128)S(1)} %copy.25), channel_id=1, source_target_pairs={{1,0},{2,1},{3,2},{4,3},{5,4},{6,5},{7,6},{9,8},{10,9},{11,10},{12... | collective-permute-start | bytes 589832 | tf_op jit(solution)/shard_map/ppermute | solution.py:32
  205.4 5.9 %collective-permute-start.6 = (f32[1,3,8,1024]{3,2,0,1:T(8,128)S(1)}, f32[1,3,8,1024]{3,2,0,1:T(8,128)S(1)}, u32[]{:S(2)}, u32[]{:S(2)}) collective-permute-start(f32[1,3,8,1024]{3,2,0,1:T(8,128)S(1)} %fusion.320), channel_id=1, source_target_pairs={{8,0},{16,8},{24,16},{32,24},{40,32},{48,40},{56,48},{64,56},{72,6... | collective-permute-start | bytes 294920 | tf_op jit(solution)/shard_map/ppermute | solution.py:61
  211.3 13.9 %collective-permute-start.7 = (f32[2,3,8,1024]{3,2,0,1:T(8,128)S(1)}, f32[2,3,8,1024]{3,2,0,1:T(8,128)S(1)}, u32[]{:S(2)}, u32[]{:S(2)}) collective-permute-start(f32[2,3,8,1024]{3,2,0,1:T(8,128)S(1)} %pad_maximum_fusion.17), channel_id=1, source_target_pairs={{0,1},{1,2},{2,3},{3,4},{4,5},{5,6},{6,7},{8,9},{9,10},{10,11},{11... | collective-permute-start | bytes 589832 | tf_op jit(solution)/shard_map/ppermute | solution.py:31
  222.4 7.0 %collective-permute-start.8 = (f32[2,3,8,1024]{3,2,0,1:T(8,128)S(1)}, f32[2,3,8,1024]{3,2,0,1:T(8,128)S(1)}, u32[]{:S(2)}, u32[]{:S(2)}) collective-permute-start(f32[2,3,8,1024]{3,2,0,1:T(8,128)S(1)} %pad_maximum_fusion.17), channel_id=1, source_target_pairs={{1,0},{2,1},{3,2},{4,3},{5,4},{6,5},{7,6},{9,8},{10,9},{11,10},{12... | collective-permute-start | bytes 589832 | tf_op jit(solution)/shard_map/ppermute | solution.py:32
where the time goes:
time: 323 us
  blocking collectives  214 us (66%)
  starting transfers between devices  51.9 us (16%)
  waiting for transfers between devices  27.8 us (9%)
  other arithmetic  15.5 us (5%)
  local copies, waits for them, and re-layouts  10.8 us (3%)
    all_gather x10, blocking collectives, carried_in(): pieces = jax.tree.map(lambda part: lax.all_gather(part, axis), so_far)  166 us
    psum x4, blocking collectives, over_axes(): return functools.reduce(lax.psum, axes, value)  48 us
    ppermute x3, starting transfers between devices, padded_2(): before = lax.ppermute(last, axis, up)  42 us
    ppermute x3, waiting for transfers between devices, shifted(): return lax.ppermute(value, axis, pairs)  13.5 us
    ppermute x3, waiting for transfers between devices, padded_2(): after = lax.ppermute(first, axis, down)  13.2 us
  transfers between devices with their start and end apart: 9, of which 8 were waited for; matrix products, arithmetic and copies ran while one was open for 0% of the time, Pallas kernels for 0%

commit v1 on v0

v1 whole, which is shorter than its diff:
```python
import functools

import jax
import jax.numpy as jnp
from jax import lax
from jax.experimental import pallas as pl
from jax.experimental.pallas import tpu as pltpu
from jax.sharding import Mesh
from jax.sharding import PartitionSpec as P

STEPS = 4
ITERS = 3
NZ, NY, NX = 8, 4, 4
CHIPS = NZ * NY * NX
LONS = 8
FIELDS = 3
TM = ("z", "y")
GRID = ("x", "c")
ZYX = ("z", "y", "x")

wave_coef = 0.6
diffusion = 0.05
coriolis = 0.1
epsilon = 1e-06


def chip_of(tile):
    z, place = divmod(tile, NY * NX)
    if z % 2:
        place = NY * NX - 1 - place
    y, x = divmod(place, NX)
    if y % 2:
        x = NX - 1 - x
    return (z * NY + y) * NX + x


def swap_pairs(first):
    pairs = []
    for tile in range(first, CHIPS, 2):
        a, b = chip_of(tile), chip_of((tile + 1) % CHIPS)
        pairs += [(a, b), (b, a)]
    return pairs


SIBLING = [(0, 1), (1, 0)]


def shape(*dims):
    return jax.ShapeDtypeStruct(dims, jnp.float32)


def call(kernel, outs, scalars, *operands, scratch=()):
    vmem = pl.BlockSpec(memory_space=pltpu.VMEM)
    smem = pl.BlockSpec(memory_space=pltpu.SMEM)
    return pl.pallas_call(
        kernel,
        out_shape=outs,
        in_specs=[smem] * len(scalars) + [vmem] * len(operands),
        out_specs=jax.tree.map(lambda _: vmem, outs),
        scratch_shapes=list(scratch),
    )(*scalars, *operands)


def iota(dim):
    return lax.broadcasted_iota(jnp.int32, (8, 128), dim)


def pack_kernel(odd_ref, tiles_ref, decay_ref, out_ref, rows_ref):
    odd = odd_ref[0] == 1
    for j in range(2):
        for f in range(FIELDS):
            for r in range(8):
                rows_ref[pl.ds(24 * j + 8 * f + r, 8, stride=64), :] = tiles_ref[
                    j, f, :, 128 * r : 128 * r + 128
                ]
    for b in range(8):
        span = slice(128 * b, 128 * b + 128)
        rows_ref[64 * b + 48 : 64 * b + 56, :] = jnp.where(
            odd, decay_ref[2, :, span], decay_ref[0, :, span]
        )
        rows_ref[64 * b + 56 : 64 * b + 64, :] = decay_ref[1, :, span]
    for b in range(8):
        block = rows_ref[64 * b : 64 * b + 64, :]
        both = jnp.concatenate([block, pltpu.roll(block, 124, 1)], axis=0)
        turned = both.T
        for i in range(16):
            to = 4 * chip_of(16 * b + i)
            out_ref[to : to + 4, :] = turned[8 * i : 8 * i + 4, :]


def later(value, groups):
    return pltpu.roll(value, 128 - 8 * groups, value.ndim - 1)


def scan_pairs(u, square, pair):
    factor = square
    for groups in (1, 2, 4, 8):
        u = u + jnp.where(pair < 16 - groups, factor, 0.0) * later(u, groups)
        factor = factor * factor
    return u


def chain_here(c0, c1, decay, pair, first_ref, second_ref, carry_ref, at):
    square = decay * decay
    value = scan_pairs(c0 + decay * c1, square, pair)
    first_ref[at] = value
    second_ref[at] = c1 + decay * jnp.where(pair < 15, later(value, 1), 0.0)
    spread = jnp.where(pair < 1, value, 0.0)
    for groups in (1, 2, 4, 8):
        spread = spread + pltpu.roll(spread, 8 * groups, spread.ndim - 1)
    carry_ref[at] = spread


def open_kernel(
    core_ref, mine_ref, other_ref, first_ref, second_ref, carry_ref, decay_ref, power_ref, turn_ref
):
    low = core_ref[0] == 0
    lane = iota(1)
    pair = lane // 8
    even = (pair & 1) == 0
    for s in range(4):
        below = mine_ref[pl.ds(s, 64, stride=4), :]
        above = mine_ref[pl.ds(256 + s, 64, stride=4), :]
        kept = jnp.where(low, below, above)
        got = other_ref[pl.ds(s, 64, stride=4), :]
        turn_ref[pl.ds(0, 64, stride=2), :] = jnp.where(low, kept, got)
        turn_ref[pl.ds(1, 64, stride=2), :] = jnp.where(low, got, kept)
        turned = turn_ref[...].T
        for half in range(2):
            at = 64 * half
            col = s + 4 * half
            mixed = turned[at + 48 : at + 56, :]
            decays = (
                jnp.where(even, mixed, pltpu.roll(mixed, 8, 1)),
                turned[at + 56 : at + 64, :],
                jnp.where(even, pltpu.roll(mixed, 120, 1), mixed),
            )
            for f in range(FIELDS):
                decay = decays[f]
                c0 = turned[at + 8 * f : at + 8 * f + 8, :]
                c1 = turned[at + 24 + 8 * f : at + 32 + 8 * f, :]
                decay_ref[f, col] = decay
                chain_here(c0, c1, decay, pair, first_ref, second_ref, carry_ref, (f, col))
                power = decay * decay
                for groups in (1, 2, 4, 8):
                    power = power * jnp.where(pair < 16 - groups, later(power, groups), 1.0)
                power_ref[0, f, col] = power
                power_ref[1, f, col] = decay * jnp.where(pair < 15, later(power, 1), 1.0)


def close_kernel(core_ref, first_ref, second_ref, carry_ref, power_ref, zero_ref, above_ref):
    low = core_ref[0] == 0
    pair = iota(1) // 8
    for f in range(FIELDS):
        for col in range(LONS):
            carry = jnp.where(low, carry_ref[f, col], 0.0)
            value = first_ref[f, col] + power_ref[0, f, col] * carry
            zero_ref[f, col] = value
            above_ref[0, f, col] = second_ref[f, col] + power_ref[1, f, col] * carry
            above_ref[1, f, col] = jnp.where(pair < 15, later(value, 1), carry)


def fine_kernel(
    odd_ref, own_ref, even_ref, odd_side_ref, decay_ref, first_ref, second_ref, carry_ref, state_ref
):
    odd = odd_ref[0] == 1
    row = iota(0)[None]
    lane = iota(1)[None]
    band = lane % 8
    pair = lane // 8
    at_top = row == 0
    at_end = row == 7
    not_first = band > 0
    not_last = band < 7

    def next_row(v):
        inner = pltpu.roll(v, 7, 1)
        edge = jnp.where(not_last, pltpu.roll(inner, 127, 2), 0.0)
        return jnp.where(at_end, edge, inner)

    def last_row(v):
        inner = pltpu.roll(v, 1, 1)
        edge = jnp.where(not_first, pltpu.roll(inner, 1, 2), 0.0)
        return jnp.where(at_top, edge, inner)

    corrections = []
    for j in range(2):
        for f in range(FIELDS):
            one, two = even_ref[j, f], odd_side_ref[j, f]
            state_ref[f, 0:8] = jnp.where(odd, one, two)
            state_ref[f, 8:16] = own_ref[j, f]
            state_ref[f, 16:24] = jnp.where(odd, two, one)
        p, q, r = state_ref[0], state_ref[1], state_ref[2]
        keep = 1.0 - 4.0 * diffusion
        wave = 0.5 * wave_coef
        for step in range(STEPS):
            n = p.shape[0]
            inside = slice(1, n - 1)
            pc, rc = p[inside], r[inside]
            p1 = (
                keep * pc
                + diffusion * (p[: n - 2] + p[2:])
                + wave * (q[2:] - q[: n - 2])
                + next_row(diffusion * pc + wave * rc)
                + last_row(diffusion * pc - wave * rc)
            )
            m = n - 2
            q2, r2, p2 = q[inside], rc, p1
            qc, rcc, pcc = q2[1 : m - 1], r2[1 : m - 1], p2[1 : m - 1]
            scaled = diffusion * qc
            q1 = (
                keep * qc
                + diffusion * (q2[: m - 2] + q2[2:])
                + wave * (p2[2:] - p2[: m - 2])
                + coriolis * rcc
                + next_row(scaled)
                + last_row(scaled)
            )
            r1 = (
                keep * rcc
                + diffusion * (r2[: m - 2] + r2[2:])
                - coriolis * qc
                + next_row(diffusion * rcc + wave * pcc)
                + last_row(diffusion * rcc - wave * pcc)
            )
            p, q, r = pcc, q1, r1
        corrections.append([v - decay_ref[f] * own_ref[j, f] for f, v in enumerate((p, q, r))])
    for f in range(FIELDS):
        chain_here(
            corrections[0][f], corrections[1][f], decay_ref[f], pair, first_ref, second_ref, carry_ref, f
        )


def finish_kernel(core_ref, *refs):
    zeros = refs[0:3]
    aboves = refs[3:6]
    first_ref, second_ref, carry_ref, power_ref, misfit_ref, ones_ref = refs[6:12]
    mine_ref, other_ref, turn_ref = refs[12:]
    low = core_ref[0] == 0
    pair = iota(1) // 8
    subwindow = (2 * (pair + jnp.where(low, 0, 16))).astype(jnp.float32)
    emphasis = [1.0 + 2.0 * (subwindow + j) / 63.0 for j in range(2)]
    sums = [jnp.zeros((8, 128), jnp.float32) for _ in range(2 * ITERS)]
    result = {}
    for f in range(FIELDS):
        for col in range(LONS):
            carry = jnp.where(low, carry_ref[f, col], 0.0)
            last = (
                first_ref[f, col] + power_ref[0, f, col] * carry,
                second_ref[f, col] + power_ref[1, f, col] * carry,
            )
            for j in range(2):
                so_far = zeros[0][f, col] if j == 0 else aboves[0][0, f, col]
                for n in range(ITERS):
                    if n == ITERS - 1:
                        change = last[j]
                    else:
                        change = zeros[n + 1][f, col] if j == 0 else aboves[n + 1][0, f, col]
                    so_far = so_far + change
                    sums[n] = sums[n] + emphasis[j] * (change * change)
                    sums[ITERS + n] = sums[ITERS + n] + emphasis[j] * (so_far * so_far)
                result[j, f, col] = so_far
    parts = jnp.concatenate(sums + [misfit_ref[...], jnp.zeros((8, 128), jnp.float32)], axis=0)
    totals = jnp.dot(parts, ones_ref[...], precision=lax.Precision.HIGHEST)
    for s in range(4):
        for half in range(2):
            at = 64 * half
            for j in range(2):
                for f in range(FIELDS):
                    to = at + 24 * j + 8 * f
                    turn_ref[to : to + 8, :] = result[j, f, s + 4 * half]
            if s < 2:
                which = 4 * half + 2 * s
                turn_ref[at + 48 : at + 64, :] = totals[8 * which : 8 * which + 16, :]
        back = turn_ref[...].T
        turn_ref[...] = back
        evens = turn_ref[pl.ds(0, 64, stride=2), :]
        odds = turn_ref[pl.ds(1, 64, stride=2), :]
        mine_ref[pl.ds(s, 64, stride=4), :] = jnp.where(low, evens, odds)
        other_ref[pl.ds(s, 64, stride=4), :] = jnp.where(low, odds, evens)


def join_kernel(core_ref, mine_ref, got_ref, out_ref):
    low = core_ref[0] == 0
    lane = lax.broadcasted_iota(jnp.int32, (256, 128), 1)
    counted = (lane & 63) >= 48
    mine, got = mine_ref[...], got_ref[...]
    total = mine + got
    out_ref[0:256, :] = jnp.where(counted, total, jnp.where(low, mine, got))
    out_ref[256:512, :] = jnp.where(counted, total, jnp.where(low, got, mine))


def unpack_kernel(in_ref, out_ref, sums_ref, rows_ref):
    total = in_ref[0:8, :]
    for v in range(1, 64):
        total = total + in_ref[8 * v : 8 * v + 8, :]
    sums_ref[...] = total
    second = (lax.broadcasted_iota(jnp.int32, (128, 128), 0) & 7) >= 4
    for b in range(8):
        for i in range(16):
            at = 4 * chip_of(16 * b + i)
            piece = in_ref[at : at + 4, :]
            rows_ref[8 * i : 8 * i + 4, :] = piece
            rows_ref[8 * i + 4 : 8 * i + 8, :] = piece
        block = rows_ref[...]
        turned = jnp.where(second, pltpu.roll(block, 64, 1), block).T
        for j in range(2):
            for f in range(FIELDS):
                at = 24 * j + 8 * f
                out_ref[j, f, :, 128 * b : 128 * b + 128] = turned[at : at + 8, :]


def per_device(departure, obs_weight, obs_block, coarse_decay):
    z, y, x, core = (lax.axis_index(name) for name in ("z", "y", "x", "c"))
    core_arg = core.astype(jnp.int32).reshape(1)
    tile_odd = ((x + y + z) % 2).astype(jnp.int32).reshape(1)
    pair_odd = (y % 2).astype(jnp.int32).reshape(1)

    position = ((z * NY + y) * 2 + jnp.arange(2)).astype(jnp.float32)
    emphasis = 1.0 + 2.0 * position / 63.0
    strength = emphasis[:, None] * obs_weight
    misfit_part = 0.5 * jnp.sum(
        strength[:, :, None, None] * departure * departure, axis=(0, 1, 2)
    ).reshape(8, 128)
    choose = jnp.where(
        obs_block[:, :, None] == jnp.arange(8, dtype=jnp.int32), strength[:, :, None], 0.0
    )
    tiles = jnp.einsum("sob,soct->scbt", choose, departure, precision=lax.Precision.HIGHEST)

    sent = call(
        pack_kernel,
        shape(512, 128),
        (pair_odd,),
        tiles,
        coarse_decay,
        scratch=[pltpu.VMEM((512, 128), jnp.float32)],
    )
    got = lax.all_to_all(sent.reshape(CHIPS, 4, 128), ZYX, 0, 0).reshape(512, 128)
    away = lax.dynamic_slice_in_dim(got, 256 * (1 - core), 256)
    other = lax.ppermute(away, "c", SIBLING)

    field = shape(FIELDS, LONS, 8, 128)
    both = shape(2, FIELDS, LONS, 8, 128)
    square = pltpu.VMEM((128, 128), jnp.float32)
    first, second, carry, decay, power = call(
        open_kernel, (field, field, field, field, both), (core_arg,), got, other, scratch=[square]
    )
    zeros, aboves = [], []
    for _ in range(ITERS):
        carry = lax.ppermute(carry, "c", SIBLING)
        zero, above = call(
            close_kernel, (field, both), (core_arg,), first, second, carry, power
        )
        zeros.append(zero)
        aboves.append(above)
        side_even = lax.ppermute(above, ZYX, swap_pairs(0))
        side_odd = lax.ppermute(above, ZYX, swap_pairs(1))
        first, second, carry = call(
            fine_kernel,
            (field, field, field),
            (tile_odd,),
            above,
            side_even,
            side_odd,
            decay,
            scratch=[pltpu.VMEM((FIELDS, 24, 8, 128), jnp.float32)],
        )
    carry = lax.ppermute(carry, "c", SIBLING)
    mine, away = call(
        finish_kernel,
        (shape(256, 128), shape(256, 128)),
        (core_arg,),
        *zeros,
        *aboves,
        first,
        second,
        carry,
        power,
        misfit_part,
        jnp.ones((128, 128), jnp.float32),
        scratch=[square],
    )
    other = lax.ppermute(away, "c", SIBLING)
    back = call(join_kernel, shape(512, 128), (core_arg,), mine, other)
    home = lax.all_to_all(back.reshape(CHIPS, 4, 128), ZYX, 0, 0).reshape(512, 128)
    adjoint, sums = call(
        unpack_kernel,
        (shape(2, FIELDS, 8, 1024), shape(8, 128)),
        (),
        home,
        scratch=[square],
    )
    counted = jnp.sum(sums.reshape(2, 4, 2, 64)[:, :2, :, 48:].reshape(2, 2, 2, 2, 8), axis=(0, 4))
    totals = counted.transpose(1, 0, 2).reshape(8)
    changes = totals[:ITERS] / (totals[ITERS : 2 * ITERS] + epsilon)
    return adjoint, totals[2 * ITERS], changes


def solution(mesh):
    split = Mesh(mesh.devices.reshape(NZ, NY, NX, 2), ("z", "y", "x", "c"))
    return jax.shard_map(
        per_device,
        mesh=split,
        in_specs=(P(TM, GRID, None, None), P(TM, GRID), P(TM, GRID), P(None, GRID, None)),
        out_specs=(P(TM, None, GRID, None), P(), P()),
        check_vma=False,
    )
```

time: 323 us -> 128 us (0.40)
  blocking collectives: 214 us -> 21 us
  Pallas kernels: 0 us -> 27.6 us
  starting transfers between devices: 51.9 us -> 24.9 us
  other arithmetic: 15.5 us -> 1.55 us
  waiting for transfers between devices: 27.8 us -> 41.2 us
    all_gather x10 -> x0, blocking collectives: 166 us -> none  [carried_in(): pieces = jax.tree.map(lambda part: lax.all_gather(part, axis), so_far)]
    psum x4 -> x0, blocking collectives: 48 us -> none  [over_axes(): return functools.reduce(lax.psum, axes, value)]
    ppermute x9 -> x12, starting transfers between devices: 51.9 us -> 8.54 us  [the longest x4 4.83 us: per_device(): carry = lax.ppermute(carry, 'c', SIBLING)]
    pallas_call x0 -> x11, Pallas kernels: none -> 27.6 us  [call(): pl.pallas_call(kernel, out_shape=outs, in_specs=[smem] * len(scalars) + [...]
    all_to_all x0 -> x1, blocking collectives: none -> 21 us  [per_device(): lax.all_to_all(back.reshape(CHIPS, 4, 128), ZYX, 0, 0).reshape(512, 128)]
    all_to_all x0 -> x1, starting transfers between devices: none -> 16.3 us  [per_device(): lax.all_to_all(sent.reshape(CHIPS, 4, 128), ZYX, 0, 0).reshape(512, 128)]
    all_to_all x0 -> x1, waiting for transfers between devices: none -> 13.4 us  [per_device(): lax.all_to_all(sent.reshape(CHIPS, 4, 128), ZYX, 0, 0).reshape(512, 128)]
    another operation x31 -> x0, other arithmetic: 8.98 us -> none  [the longest x24 4.08 us: sweep_once(): return jnp.stack([height_new, zonal_new, merid_new], axis=1)]
  transfers between devices with their start and end apart: 9 -> 13, of which waited for: 8 -> 13; matrix products, arithmetic and copies ran while one was open for 0% -> 1% of each run, Pallas kernels for 0% -> 0%
where the time goes in v1:
time: 128 us
  waiting for transfers between devices  41.2 us (32%)
  Pallas kernels  27.6 us (22%)
  starting transfers between devices  24.9 us (19%)
  blocking collectives  21 us (16%)
  local copies, waits for them, and re-layouts  8.75 us (7%)
  matrix products  2 us (2%)
  other arithmetic  1.55 us (1%)
    pallas_call x11, Pallas kernels, call(): pl.pallas_call(kernel, out_shape=outs, in_specs=[smem] * len(scalars) + [...  27.6 us
    all_to_all x1, blocking collectives, per_device(): lax.all_to_all(back.reshape(CHIPS, 4, 128), ZYX, 0, 0).reshape(512, 128)  21 us
    ppermute x3, waiting for transfers between devices, per_device(): side_even = lax.ppermute(above, ZYX, swap_pairs(0))  18.2 us
    all_to_all x1, starting transfers between devices, per_device(): lax.all_to_all(sent.reshape(CHIPS, 4, 128), ZYX, 0, 0).reshape(512, 128)  16.3 us
    all_to_all x1, waiting for transfers between devices, per_device(): lax.all_to_all(sent.reshape(CHIPS, 4, 128), ZYX, 0, 0).reshape(512, 128)  13.4 us
    unnamed x32, local copies, waits for them, and re-layouts  6.56 us
    ppermute x4, starting transfers between devices, per_device(): carry = lax.ppermute(carry, 'c', SIBLING)  4.83 us
    ppermute x4, waiting for transfers between devices, per_device(): carry = lax.ppermute(carry, 'c', SIBLING)  4.03 us
  transfers between devices with their start and end apart: 13, of which 13 were waited for; matrix products, arithmetic and copies ran while one was open for 1% of the time, Pallas kernels for 0%

profile of v1, /device:TPU:1, one launch (start us, length us, event | category | flops | bytes accessed | tf_op | source)
XLA Modules:
  0.0 127.7 jit_solution(16051449851762612967)
XLA Ops:
  2.0 2.0 %convolution_bitcast_fusion.tiles_ref = f32[2,3,8,1024]{3,2,1,0:T(8,128)} fusion(f32[2,16,3,1024]{3,1,2,0:T(8,128)} %param.4, f32[2,16]{1,0:T(2,128)S(1)} %broadcast_multiply_fusion, s32[2,16]{1,0:T(2,128)S(1)} %copy-done.14), kind=kOutput, calls=%fused_computation | convolution fusion | flops 9437696 | bytes 590080 | tf_op jit(solution)/shard_map/sob,soct->scbt/dot_general | solution.py:328
  4.0 2.1 %shard_map.67 = f32[512,128]{1,0:T(8,128)} custom-call(s32[1]{0:T(128)} %bitcast.1.odd_ref, f32[2,3,8,1024]{3,2,1,0:T(8,128)} %convolution_bitcast_fusion.tiles_ref, f32[3,8,1024]{2,1,0:T(8,128)} %decay_ref.1), custom_call_target="tpu_custom_call" | custom-call | tf_op jit(solution)/shard_map/pallas_call | solution.py:55
  6.1 16.3 %all-to-all-start = ((f32[128,4,128]{2,1,0:T(4,128)}), f32[128,4,128]{2,1,0:T(4,128)S(1)}, u32[]{:S(2)}, u32[]{:S(2)}) async-start(f32[128,4,128]{2,1,0:T(4,128)} %bitcast.21), calls=%async_computation | async-start | bytes 524288 | tf_op jit(solution)/shard_map/all_to_all | solution.py:338
  22.4 13.4 %all-to-all-done = f32[128,4,128]{2,1,0:T(4,128)S(1)} async-done(((f32[128,4,128]{2,1,0:T(4,128)}), f32[128,4,128]{2,1,0:T(4,128)S(1)}, u32[]{:S(2)}, u32[]{:S(2)}) %all-to-all-start) | async-done | bytes 262176 | tf_op jit(solution)/shard_map/all_to_all | solution.py:338
  35.9 2.8 %collective-permute-start = (f32[256,128]{1,0:T(8,128)S(1)}, f32[256,128]{1,0:T(8,128)S(1)}, u32[]{:S(2)}, u32[]{:S(2)}) collective-permute-start(f32[256,128]{1,0:T(8,128)S(1)} %constant_dynamic-slice_fusion), channel_id=1, source_target_pairs={{0,1},{1,0},{2,3},{3,2},{4,5},{5,4},{6,7},{7,6},{8,9},{9,8},{10,11... | collective-permute-start | bytes 393224 | tf_op jit(solution)/shard_map/ppermute | solution.py:340
  40.3 2.8 %shard_map.68 = (f32[3,8,8,128]{3,2,1,0:T(8,128)}, f32[3,8,8,128]{3,2,1,0:T(8,128)}, f32[3,8,8,128]{3,2,1,0:T(8,128)}, f32[3,8,8,128]{3,2,1,0:T(8,128)}, f32[2,3,8,8,128]{4,3,2,1,0:T(8,128)}) custom-call(s32[1]{0:T(128)} %bitcast.core_ref, f32[512,128]{1,0:T(8,128)} %bitcast.20, f32[256,128]{1,0:T(8,128)} %copy-done.9), custom_call_target="tpu_custom_call" | custom-call | tf_op jit(solution)/shard_map/pallas_call | solution.py:55
  45.3 1.8 %shard_map.69 = (f32[3,8,8,128]{3,2,1,0:T(8,128)}, f32[2,3,8,8,128]{4,3,2,1,0:T(8,128)}) custom-call(s32[1]{0:T(128)} %bitcast.core_ref, f32[3,8,8,128]{3,2,1,0:T(8,128)} %get-tuple-element.27.first_ref, f32[3,8,8,128]{3,2,1,0:T(8,128)} %get-tuple-element.28.second_ref, f32[3,8,8,128]{3,2,1,0:T(8,128)} %copy-done.12, ...), custom_call_target="tpu_custom_call" | custom-call | tf_op jit(solution)/shard_map/pallas_call | solution.py:55
  47.4 6.0 %collective-permute-done.2.even_ref = f32[2,3,8,8,128]{4,3,2,1,0:T(8,128)S(1)} collective-permute-done((f32[2,3,8,8,128]{4,3,2,1,0:T(8,128)}, f32[2,3,8,8,128]{4,3,2,1,0:T(8,128)S(1)}, u32[]{:S(2)}, u32[]{:S(2)}) %collective-permute-start.2) | collective-permute-done | bytes 196640 | tf_op jit(solution)/shard_map/ppermute | solution.py:356
  53.4 1.2 collective-permute-done.3.odd_side_ref
  55.3 3.6 %shard_map.70 = (f32[3,8,8,128]{3,2,1,0:T(8,128)}, f32[3,8,8,128]{3,2,1,0:T(8,128)}, f32[3,8,8,128]{3,2,1,0:T(8,128)}) custom-call(s32[1]{0:T(128)} %bitcast.7.odd_ref, f32[2,3,8,8,128]{4,3,2,1,0:T(8,128)} %get-tuple-element.32.own_ref.refs_3_, f32[2,3,8,8,128]{4,3,2,1,0:T(8,128)} %copy-done.2, f32[2,3,8,8,128]{4,3,2,1,0:T(8,128)} %copy-done.3, ...), custom_call_target="tpu_custom_call" | custom-call | tf_op jit(solution)/shard_map/pallas_call | solution.py:55
  58.9 1.5 %collective-permute-start.4 = (f32[3,8,8,128]{3,2,1,0:T(8,128)}, f32[3,8,8,128]{3,2,1,0:T(8,128)S(1)}, u32[]{:S(2)}, u32[]{:S(2)}) collective-permute-start(f32[3,8,8,128]{3,2,1,0:T(8,128)} %get-tuple-element.36), channel_id=1, source_target_pairs={{0,1},{1,0},{2,3},{3,2},{4,5},{5,4},{6,7},{7,6},{8,9},{9,8},{10,11... | collective-permute-start | bytes 294920 | tf_op jit(solution)/shard_map/ppermute | solution.py:350
  62.1 1.8 %shard_map.71 = (f32[3,8,8,128]{3,2,1,0:T(8,128)}, f32[2,3,8,8,128]{4,3,2,1,0:T(8,128)}) custom-call(s32[1]{0:T(128)} %bitcast.core_ref, f32[3,8,8,128]{3,2,1,0:T(8,128)} %get-tuple-element.34.first_ref, f32[3,8,8,128]{3,2,1,0:T(8,128)} %get-tuple-element.35.second_ref, f32[3,8,8,128]{3,2,1,0:T(8,128)} %copy-done.10, ...), custom_call_target="tpu_custom_call" | custom-call | tf_op jit(solution)/shard_map/pallas_call | solution.py:55
  64.0 6.3 %collective-permute-done.5.even_ref = f32[2,3,8,8,128]{4,3,2,1,0:T(8,128)S(1)} collective-permute-done((f32[2,3,8,8,128]{4,3,2,1,0:T(8,128)}, f32[2,3,8,8,128]{4,3,2,1,0:T(8,128)S(1)}, u32[]{:S(2)}, u32[]{:S(2)}) %collective-permute-start.5) | collective-permute-done | bytes 196640 | tf_op jit(solution)/shard_map/ppermute | solution.py:356
  71.9 3.6 %shard_map.72 = (f32[3,8,8,128]{3,2,1,0:T(8,128)}, f32[3,8,8,128]{3,2,1,0:T(8,128)}, f32[3,8,8,128]{3,2,1,0:T(8,128)}) custom-call(s32[1]{0:T(128)} %bitcast.7.odd_ref, f32[2,3,8,8,128]{4,3,2,1,0:T(8,128)} %get-tuple-element.38.own_ref.refs_4_, f32[2,3,8,8,128]{4,3,2,1,0:T(8,128)} %copy-done.6, f32[2,3,8,8,128]{4,3,2,1,0:T(8,128)} %copy-done.7, ...), custom_call_target="tpu_custom_call" | custom-call | tf_op jit(solution)/shard_map/pallas_call | solution.py:55
  75.5 1.5 %collective-permute-start.7 = (f32[3,8,8,128]{3,2,1,0:T(8,128)}, f32[3,8,8,128]{3,2,1,0:T(8,128)S(1)}, u32[]{:S(2)}, u32[]{:S(2)}) collective-permute-start(f32[3,8,8,128]{3,2,1,0:T(8,128)} %get-tuple-element.41), channel_id=1, source_target_pairs={{0,1},{1,0},{2,3},{3,2},{4,5},{5,4},{6,7},{7,6},{8,9},{9,8},{10,11... | collective-permute-start | bytes 294920 | tf_op jit(solution)/shard_map/ppermute | solution.py:350
  78.8 1.8 %shard_map.73 = (f32[3,8,8,128]{3,2,1,0:T(8,128)}, f32[2,3,8,8,128]{4,3,2,1,0:T(8,128)}) custom-call(s32[1]{0:T(128)} %bitcast.core_ref, f32[3,8,8,128]{3,2,1,0:T(8,128)} %get-tuple-element.39.first_ref, f32[3,8,8,128]{3,2,1,0:T(8,128)} %get-tuple-element.40.second_ref, f32[3,8,8,128]{3,2,1,0:T(8,128)} %copy-done.11, ...), custom_call_target="tpu_custom_call" | custom-call | tf_op jit(solution)/shard_map/pallas_call | solution.py:55
  81.0 5.9 %collective-permute-done.8.even_ref = f32[2,3,8,8,128]{4,3,2,1,0:T(8,128)S(1)} collective-permute-done((f32[2,3,8,8,128]{4,3,2,1,0:T(8,128)}, f32[2,3,8,8,128]{4,3,2,1,0:T(8,128)S(1)}, u32[]{:S(2)}, u32[]{:S(2)}) %collective-permute-start.8) | collective-permute-done | bytes 196640 | tf_op jit(solution)/shard_map/ppermute | solution.py:356
  88.8 3.6 %shard_map.74 = (f32[3,8,8,128]{3,2,1,0:T(8,128)}, f32[3,8,8,128]{3,2,1,0:T(8,128)}, f32[3,8,8,128]{3,2,1,0:T(8,128)}) custom-call(s32[1]{0:T(128)} %bitcast.7.odd_ref, f32[2,3,8,8,128]{4,3,2,1,0:T(8,128)} %get-tuple-element.43.own_ref.refs_5_, f32[2,3,8,8,128]{4,3,2,1,0:T(8,128)} %copy-done.4, f32[2,3,8,8,128]{4,3,2,1,0:T(8,128)} %copy-done.5, ...), custom_call_target="tpu_custom_call" | custom-call | tf_op jit(solution)/shard_map/pallas_call | solution.py:55
  92.4 1.5 %collective-permute-start.10 = (f32[3,8,8,128]{3,2,1,0:T(8,128)}, f32[3,8,8,128]{3,2,1,0:T(8,128)S(1)}, u32[]{:S(2)}, u32[]{:S(2)}) collective-permute-start(f32[3,8,8,128]{3,2,1,0:T(8,128)} %get-tuple-element.46), channel_id=1, source_target_pairs={{0,1},{1,0},{2,3},{3,2},{4,5},{5,4},{6,7},{7,6},{8,9},{9,8},{10,11... | collective-permute-start | bytes 294920 | tf_op jit(solution)/shard_map/ppermute | solution.py:368
  95.7 2.7 %shard_map.75 = (f32[256,128]{1,0:T(8,128)}, f32[256,128]{1,0:T(8,128)}) custom-call(s32[1]{0:T(128)} %bitcast.core_ref, f32[3,8,8,128]{3,2,1,0:T(8,128)} %get-tuple-element.31.refs_0_, f32[3,8,8,128]{3,2,1,0:T(8,128)} %get-tuple-element.37.refs_1_, f32[3,8,8,128]{3,2,1,0:T(8,128)} %get-tuple-element.42.refs_2_, ...), custom_call_target="tpu_custom_call" | custom-call | tf_op jit(solution)/shard_map/pallas_call | solution.py:55
  98.8 1.2 collective-permute-done.11.got_ref
  100.6 1.7 %shard_map.76 = f32[512,128]{1,0:T(8,128)} custom-call(s32[1]{0:T(128)} %bitcast.core_ref, f32[256,128]{1,0:T(8,128)} %get-tuple-element.47.mine_ref, f32[256,128]{1,0:T(8,128)} %copy-done.8), custom_call_target="tpu_custom_call" | custom-call | tf_op jit(solution)/shard_map/pallas_call | solution.py:55
  102.4 21.0 %all_to_all.10 = f32[128,4,128]{2,1,0:T(4,128)} all-to-all(f32[128,4,128]{2,1,0:T(4,128)} %bitcast.22), channel_id=1, replica_groups=mesh['z'=8,'y'=4,'x'=4,'c'=2] {'z','y','x'}, dimensions={0} | all-to-all | bytes 524288 | tf_op jit(solution)/shard_map/all_to_all | solution.py:385
  123.4 2.0 %shard_map.77 = (f32[2,3,8,1024]{3,2,1,0:T(8,128)}, f32[8,128]{1,0:T(8,128)}) custom-call(f32[512,128]{1,0:T(8,128)} %bitcast.23), custom_call_target="tpu_custom_call" | custom-call | tf_op jit(solution)/shard_map/pallas_call | solution.py:55
  (61 shorter events, 18.8 us)
Async XLA Ops:
  0.7 0.7 copy-start.15
  1.3 0.7 copy-start.14
  6.1 29.8 %all-to-all-start = ((f32[128,4,128]{2,1,0:T(4,128)}), f32[128,4,128]{2,1,0:T(4,128)S(1)}, u32[]{:S(2)}, u32[]{:S(2)}) async-start(f32[128,4,128]{2,1,0:T(4,128)} %bitcast.21), calls=%async_computation | async-start | bytes 524288 | tf_op jit(solution)/shard_map/all_to_all | solution.py:338
  35.9 3.8 %copy-start = (f32[128,4,128]{2,1,0:T(4,128)}, f32[128,4,128]{2,1,0:T(4,128)S(1)}, u32[]{:S(2)}) copy-start(f32[128,4,128]{2,1,0:T(4,128)S(1)} %all-to-all-done) | copy-start | bytes 786436
  35.9 3.7 %collective-permute-start = (f32[256,128]{1,0:T(8,128)S(1)}, f32[256,128]{1,0:T(8,128)S(1)}, u32[]{:S(2)}, u32[]{:S(2)}) collective-permute-start(f32[256,128]{1,0:T(8,128)S(1)} %constant_dynamic-slice_fusion), channel_id=1, source_target_pairs={{0,1},{1,0},{2,3},{3,2},{4,5},{5,4},{6,7},{7,6},{8,9},{9,8},{10,11... | collective-permute-start | bytes 393224 | tf_op jit(solution)/shard_map/ppermute | solution.py:340
  43.1 1.5 %collective-permute-start.1 = (f32[3,8,8,128]{3,2,1,0:T(8,128)}, f32[3,8,8,128]{3,2,1,0:T(8,128)S(1)}, u32[]{:S(2)}, u32[]{:S(2)}) collective-permute-start(f32[3,8,8,128]{3,2,1,0:T(8,128)} %get-tuple-element.29), channel_id=1, source_target_pairs={{0,1},{1,0},{2,3},{3,2},{4,5},{5,4},{6,7},{7,6},{8,9},{9,8},{10,11... | collective-permute-start | bytes 294920 | tf_op jit(solution)/shard_map/ppermute | solution.py:350
  47.1 6.3 %collective-permute-start.2 = (f32[2,3,8,8,128]{4,3,2,1,0:T(8,128)}, f32[2,3,8,8,128]{4,3,2,1,0:T(8,128)S(1)}, u32[]{:S(2)}, u32[]{:S(2)}) collective-permute-start(f32[2,3,8,8,128]{4,3,2,1,0:T(8,128)} %get-tuple-element.32.own_ref.refs_3_), channel_id=1, source_target_pairs={{0,2},{2,0},{4,6},{6,4},{14,12},{12,14},{10,8},{8,10},{16,18},{18,... | collective-permute-start | bytes 589832 | tf_op jit(solution)/shard_map/ppermute | solution.py:356
  47.4 7.2 %collective-permute-start.3 = (f32[2,3,8,8,128]{4,3,2,1,0:T(8,128)}, f32[2,3,8,8,128]{4,3,2,1,0:T(8,128)S(1)}, u32[]{:S(2)}, u32[]{:S(2)}) collective-permute-start(f32[2,3,8,8,128]{4,3,2,1,0:T(8,128)} %get-tuple-element.32.own_ref.refs_3_), channel_id=1, source_target_pairs={{2,4},{4,2},{6,14},{14,6},{12,10},{10,12},{8,16},{16,8},{18,20},{2... | collective-permute-start | bytes 589832 | tf_op jit(solution)/shard_map/ppermute | solution.py:357
  53.4 1.2 copy-start.2
  54.6 0.7 copy-start.3
  58.9 2.7 %collective-permute-start.4 = (f32[3,8,8,128]{3,2,1,0:T(8,128)}, f32[3,8,8,128]{3,2,1,0:T(8,128)S(1)}, u32[]{:S(2)}, u32[]{:S(2)}) collective-permute-start(f32[3,8,8,128]{3,2,1,0:T(8,128)} %get-tuple-element.36), channel_id=1, source_target_pairs={{0,1},{1,0},{2,3},{3,2},{4,5},{5,4},{6,7},{7,6},{8,9},{9,8},{10,11... | collective-permute-start | bytes 294920 | tf_op jit(solution)/shard_map/ppermute | solution.py:350
  64.0 6.3 %collective-permute-start.5 = (f32[2,3,8,8,128]{4,3,2,1,0:T(8,128)}, f32[2,3,8,8,128]{4,3,2,1,0:T(8,128)S(1)}, u32[]{:S(2)}, u32[]{:S(2)}) collective-permute-start(f32[2,3,8,8,128]{4,3,2,1,0:T(8,128)} %get-tuple-element.38.own_ref.refs_4_), channel_id=1, source_target_pairs={{0,2},{2,0},{4,6},{6,4},{14,12},{12,14},{10,8},{8,10},{16,18},{18,... | collective-permute-start | bytes 589832 | tf_op jit(solution)/shard_map/ppermute | solution.py:356
  64.0 7.3 %collective-permute-start.6 = (f32[2,3,8,8,128]{4,3,2,1,0:T(8,128)}, f32[2,3,8,8,128]{4,3,2,1,0:T(8,128)S(1)}, u32[]{:S(2)}, u32[]{:S(2)}) collective-permute-start(f32[2,3,8,8,128]{4,3,2,1,0:T(8,128)} %get-tuple-element.38.own_ref.refs_4_), channel_id=1, source_target_pairs={{2,4},{4,2},{6,14},{14,6},{12,10},{10,12},{8,16},{16,8},{18,20},{2... | collective-permute-start | bytes 589832 | tf_op jit(solution)/shard_map/ppermute | solution.py:357
  70.3 1.0 copy-start.6
  71.3 0.7 copy-start.7
  75.5 5.4 %copy-start.1 = (f32[2,16,3,1024]{3,1,2,0:T(8,128)S(1)}, f32[2,16,3,1024]{3,1,2,0:T(8,128)}, u32[]{:S(2)}) copy-start(f32[2,16,3,1024]{3,1,2,0:T(8,128)} %param.4) | copy-start | bytes 1179652
  75.5 2.6 %collective-permute-start.7 = (f32[3,8,8,128]{3,2,1,0:T(8,128)}, f32[3,8,8,128]{3,2,1,0:T(8,128)S(1)}, u32[]{:S(2)}, u32[]{:S(2)}) collective-permute-start(f32[3,8,8,128]{3,2,1,0:T(8,128)} %get-tuple-element.41), channel_id=1, source_target_pairs={{0,1},{1,0},{2,3},{3,2},{4,5},{5,4},{6,7},{7,6},{8,9},{9,8},{10,11... | collective-permute-start | bytes 294920 | tf_op jit(solution)/shard_map/ppermute | solution.py:350
  80.6 6.3 %collective-permute-start.8 = (f32[2,3,8,8,128]{4,3,2,1,0:T(8,128)}, f32[2,3,8,8,128]{4,3,2,1,0:T(8,128)S(1)}, u32[]{:S(2)}, u32[]{:S(2)}) collective-permute-start(f32[2,3,8,8,128]{4,3,2,1,0:T(8,128)} %get-tuple-element.43.own_ref.refs_5_), channel_id=1, source_target_pairs={{0,2},{2,0},{4,6},{6,4},{14,12},{12,14},{10,8},{8,10},{16,18},{18,... | collective-permute-start | bytes 589832 | tf_op jit(solution)/shard_map/ppermute | solution.py:356
  80.9 7.2 %collective-permute-start.9 = (f32[2,3,8,8,128]{4,3,2,1,0:T(8,128)}, f32[2,3,8,8,128]{4,3,2,1,0:T(8,128)S(1)}, u32[]{:S(2)}, u32[]{:S(2)}) collective-permute-start(f32[2,3,8,8,128]{4,3,2,1,0:T(8,128)} %get-tuple-element.43.own_ref.refs_5_), channel_id=1, source_target_pairs={{2,4},{4,2},{6,14},{14,6},{12,10},{10,12},{8,16},{16,8},{18,20},{2... | collective-permute-start | bytes 589832 | tf_op jit(solution)/shard_map/ppermute | solution.py:357
  86.9 1.2 copy-start.4
  88.1 0.7 copy-start.5
  92.4 2.7 %collective-permute-start.10 = (f32[3,8,8,128]{3,2,1,0:T(8,128)}, f32[3,8,8,128]{3,2,1,0:T(8,128)S(1)}, u32[]{:S(2)}, u32[]{:S(2)}) collective-permute-start(f32[3,8,8,128]{3,2,1,0:T(8,128)} %get-tuple-element.46), channel_id=1, source_target_pairs={{0,1},{1,0},{2,3},{3,2},{4,5},{5,4},{6,7},{7,6},{8,9},{9,8},{10,11... | collective-permute-start | bytes 294920 | tf_op jit(solution)/shard_map/ppermute | solution.py:368
  95.0 0.7 copy-start.13
  98.4 1.6 %collective-permute-start.11 = (f32[256,128]{1,0:T(8,128)}, f32[256,128]{1,0:T(8,128)S(1)}, u32[]{:S(2)}, u32[]{:S(2)}) collective-permute-start(f32[256,128]{1,0:T(8,128)} %get-tuple-element.48), channel_id=1, source_target_pairs={{0,1},{1,0},{2,3},{3,2},{4,5},{5,4},{6,7},{7,6},{8,9},{9,8},{10,11... | collective-permute-start | bytes 393224 | tf_op jit(solution)/shard_map/ppermute | solution.py:383
  (5 other events, 3.2 us)

commit v2 on v1

--- a/solution.py
+++ b/solution.py
@@ -46,7 +46,11 @@
 
 
 def shape(*dims):
-    return jax.ShapeDtypeStruct(dims, jnp.float32)
+    return pltpu.VMEM(dims, jnp.float32)
+
+
+def near(value):
+    return pltpu.with_memory_space_constraint(value, pltpu.VMEM)
 
 
 def call(kernel, outs, scalars, *operands, scratch=()):
@@ -58,7 +62,7 @@
         in_specs=[smem] * len(scalars) + [vmem] * len(operands),
         out_specs=jax.tree.map(lambda _: vmem, outs),
         scratch_shapes=list(scratch),
-    )(*scalars, *operands)
+    )(*scalars, *map(near, operands))
 
 
 def iota(dim):
@@ -119,10 +123,10 @@
     pair = lane // 8
     even = (pair & 1) == 0
     for s in range(4):
-        below = mine_ref[pl.ds(s, 64, stride=4), :]
-        above = mine_ref[pl.ds(256 + s, 64, stride=4), :]
-        kept = jnp.where(low, below, above)
-        got = other_ref[pl.ds(s, 64, stride=4), :]
+        kept, got = (
+            jnp.where(low, ref[pl.ds(s, 64, stride=4), :], ref[pl.ds(256 + s, 64, stride=4), :])
+            for ref in (mine_ref, other_ref)
+        )
         turn_ref[pl.ds(0, 64, stride=2), :] = jnp.where(low, kept, got)
         turn_ref[pl.ds(1, 64, stride=2), :] = jnp.where(low, got, kept)
         turned = turn_ref[...].T
@@ -234,8 +238,8 @@
 def finish_kernel(core_ref, *refs):
     zeros = refs[0:3]
     aboves = refs[3:6]
-    first_ref, second_ref, carry_ref, power_ref, misfit_ref, ones_ref = refs[6:12]
-    mine_ref, other_ref, turn_ref = refs[12:]
+    first_ref, second_ref, carry_ref, power_ref, misfit_ref = refs[6:11]
+    mine_ref, other_ref, turn_ref, back_ref = refs[11:]
     low = core_ref[0] == 0
     pair = iota(1) // 8
     subwindow = (2 * (pair + jnp.where(low, 0, 16))).astype(jnp.float32)
@@ -260,8 +264,13 @@
                     sums[n] = sums[n] + emphasis[j] * (change * change)
                     sums[ITERS + n] = sums[ITERS + n] + emphasis[j] * (so_far * so_far)
                 result[j, f, col] = so_far
-    parts = jnp.concatenate(sums + [misfit_ref[...], jnp.zeros((8, 128), jnp.float32)], axis=0)
-    totals = jnp.dot(parts, ones_ref[...], precision=lax.Precision.HIGHEST)
+    row = iota(0)
+    parts = jnp.zeros((8, 128), jnp.float32)
+    for at, part in enumerate(sums[:ITERS] + [misfit_ref[...]] + sums[ITERS:]):
+        parts = jnp.where(row == at, jnp.sum(part, axis=0, keepdims=True), parts)
+    ones = jnp.ones((128, 128), jnp.float32)
+    totals = jnp.dot(parts, ones, precision=lax.Precision.HIGHEST)
+    turn_ref[48:56, :] = totals
     for s in range(4):
         for half in range(2):
             at = 64 * half
@@ -269,13 +278,9 @@
                 for f in range(FIELDS):
                     to = at + 24 * j + 8 * f
                     turn_ref[to : to + 8, :] = result[j, f, s + 4 * half]
-            if s < 2:
-                which = 4 * half + 2 * s
-                turn_ref[at + 48 : at + 64, :] = totals[8 * which : 8 * which + 16, :]
-        back = turn_ref[...].T
-        turn_ref[...] = back
-        evens = turn_ref[pl.ds(0, 64, stride=2), :]
-        odds = turn_ref[pl.ds(1, 64, stride=2), :]
+        back_ref[...] = turn_ref[...].T
+        evens = back_ref[pl.ds(0, 64, stride=2), :]
+        odds = back_ref[pl.ds(1, 64, stride=2), :]
         mine_ref[pl.ds(s, 64, stride=4), :] = jnp.where(low, evens, odds)
         other_ref[pl.ds(s, 64, stride=4), :] = jnp.where(low, odds, evens)
 
@@ -283,18 +288,20 @@
 def join_kernel(core_ref, mine_ref, got_ref, out_ref):
     low = core_ref[0] == 0
     lane = lax.broadcasted_iota(jnp.int32, (256, 128), 1)
-    counted = (lane & 63) >= 48
+    counted = (lane & 120) == 48
     mine, got = mine_ref[...], got_ref[...]
     total = mine + got
     out_ref[0:256, :] = jnp.where(counted, total, jnp.where(low, mine, got))
     out_ref[256:512, :] = jnp.where(counted, total, jnp.where(low, got, mine))
 
 
-def unpack_kernel(in_ref, out_ref, sums_ref, rows_ref):
-    total = in_ref[0:8, :]
-    for v in range(1, 64):
-        total = total + in_ref[8 * v : 8 * v + 8, :]
-    sums_ref[...] = total
+def unpack_kernel(in_ref, out_ref, misfit_ref, changes_ref, rows_ref):
+    sums = [in_ref[8 * v : 8 * v + 8, :] for v in range(64)]
+    while len(sums) > 1:
+        sums = [a + b for a, b in zip(sums[::2], sums[1::2])]
+    total = pltpu.roll(sums[0] + pltpu.roll(sums[0], 4, 0), 80, 1)
+    misfit_ref[...] = total[0:1, 3:4]
+    changes_ref[...] = (total / (pltpu.roll(total, 124, 1) + epsilon))[0:1, 0:ITERS]
     second = (lax.broadcasted_iota(jnp.int32, (128, 128), 0) & 7) >= 4
     for b in range(8):
         for i in range(16):
@@ -336,8 +343,7 @@
         scratch=[pltpu.VMEM((512, 128), jnp.float32)],
     )
     got = lax.all_to_all(sent.reshape(CHIPS, 4, 128), ZYX, 0, 0).reshape(512, 128)
-    away = lax.dynamic_slice_in_dim(got, 256 * (1 - core), 256)
-    other = lax.ppermute(away, "c", SIBLING)
+    other = lax.ppermute(got, "c", SIBLING)
 
     field = shape(FIELDS, LONS, 8, 128)
     both = shape(2, FIELDS, LONS, 8, 128)
@@ -377,23 +383,23 @@
         carry,
         power,
         misfit_part,
-        jnp.ones((128, 128), jnp.float32),
-        scratch=[square],
+        scratch=[square, square],
     )
     other = lax.ppermute(away, "c", SIBLING)
     back = call(join_kernel, shape(512, 128), (core_arg,), mine, other)
     home = lax.all_to_all(back.reshape(CHIPS, 4, 128), ZYX, 0, 0).reshape(512, 128)
-    adjoint, sums = call(
+    adjoint, misfit, changes = call(
         unpack_kernel,
-        (shape(2, FIELDS, 8, 1024), shape(8, 128)),
+        (
+            jax.ShapeDtypeStruct((2, FIELDS, 8, 1024), jnp.float32),
+            jax.ShapeDtypeStruct((1, 1), jnp.float32),
+            jax.ShapeDtypeStruct((1, ITERS), jnp.float32),
+        ),
         (),
         home,
         scratch=[square],
     )
-    counted = jnp.sum(sums.reshape(2, 4, 2, 64)[:, :2, :, 48:].reshape(2, 2, 2, 2, 8), axis=(0, 4))
-    totals = counted.transpose(1, 0, 2).reshape(8)
-    changes = totals[:ITERS] / (totals[ITERS : 2 * ITERS] + epsilon)
-    return adjoint, totals[2 * ITERS], changes
+    return adjoint, misfit.reshape(()), changes.reshape(ITERS)
 
 
 def solution(mesh):

time: 128 us -> 97.5 us (0.76)
  blocking collectives: 21 us -> 49 us
  Pallas kernels: 27.6 us -> 8.58 us
  starting transfers between devices: 24.9 us -> 8.98 us
  waiting for transfers between devices: 41.2 us -> 27.1 us
  local copies, waits for them, and re-layouts: 8.75 us -> 1.29 us
  other arithmetic: 1.55 us -> 0.2 us
    all_to_all x0 -> x1, blocking collectives: none -> 29.5 us  [per_device(): lax.all_to_all(sent.reshape(CHIPS, 4, 128), ZYX, 0, 0).reshape(512, 128)]
    pallas_call x11, Pallas kernels: 27.6 us -> 8.58 us  [call(): pl.pallas_call(kernel, out_shape=outs, in_specs=[smem] * len(scalars) + [...]
    all_to_all x1 -> x0, starting transfers between devices: 16.3 us -> none  [per_device(): lax.all_to_all(sent.reshape(CHIPS, 4, 128), ZYX, 0, 0).reshape(512, 128)]
    all_to_all x1 -> x0, waiting for transfers between devices: 13.4 us -> none  [per_device(): lax.all_to_all(sent.reshape(CHIPS, 4, 128), ZYX, 0, 0).reshape(512, 128)]
    unnamed x32 -> x8, local copies, waits for them, and re-layouts: 6.56 us -> 1.29 us
    ppermute x0 -> x1, starting transfers between devices: none -> 2.69 us  [per_device(): other = lax.ppermute(got, 'c', SIBLING)]
    ppermute x2 -> x1, starting transfers between devices: 3.11 us -> 0.45 us  [per_device(): other = lax.ppermute(away, 'c', SIBLING)]
    all_to_all x1, blocking collectives: 21 us -> 19.5 us  [per_device(): lax.all_to_all(back.reshape(CHIPS, 4, 128), ZYX, 0, 0).reshape(512, 128)]
  transfers between devices with their start and end apart: 13 -> 12, of which waited for: 13 -> 12; matrix products, arithmetic and copies ran while one was open for 1% -> 0% of each run, Pallas kernels for 0% -> 0%
where the time goes in v2:
time: 97.5 us; the launch traced here: 97.3 us
  blocking collectives  49 us (50%)
  waiting for transfers between devices  27.1 us (28%)
  starting transfers between devices  8.98 us (9%)
  Pallas kernels  8.58 us (9%)
  matrix products  1.35 us (1%)
  local copies, waits for them, and re-layouts  1.29 us (1%)
    all_to_all x1, blocking collectives, per_device(): lax.all_to_all(sent.reshape(CHIPS, 4, 128), ZYX, 0, 0).reshape(512, 128)  29.5 us
    all_to_all x1, blocking collectives, per_device(): lax.all_to_all(back.reshape(CHIPS, 4, 128), ZYX, 0, 0).reshape(512, 128)  19.5 us
    ppermute x3, waiting for transfers between devices, per_device(): side_even = lax.ppermute(above, ZYX, swap_pairs(0))  17.5 us
    pallas_call x11, Pallas kernels, call(): pl.pallas_call(kernel, out_shape=outs, in_specs=[smem] * len(scalars) + [...  8.58 us
    ppermute x4, starting transfers between devices, per_device(): carry = lax.ppermute(carry, 'c', SIBLING)  4.92 us
    ppermute x4, waiting for transfers between devices, per_device(): carry = lax.ppermute(carry, 'c', SIBLING)  3.77 us
    ppermute x3, waiting for transfers between devices, per_device(): side_odd = lax.ppermute(above, ZYX, swap_pairs(1))  3.69 us
    ppermute x1, starting transfers between devices, per_device(): other = lax.ppermute(got, 'c', SIBLING)  2.69 us
  transfers between devices with their start and end apart: 12, of which 12 were waited for; matrix products, arithmetic and copies ran while one was open for 0% of the time, Pallas kernels for 0%

profile of v2, /device:TPU:1, one launch (start us, length us, event | category | flops | bytes accessed | tf_op | source)
XLA Modules:
  0.0 97.3 jit_solution(8722538774455218941)
XLA Ops:
  2.0 1.4 %convolution_bitcast_fusion.tiles_ref = f32[2,3,8,1024]{3,2,1,0:T(8,128)S(1)} fusion(f32[2,16,3,1024]{3,1,2,0:T(8,128)} %param.4, f32[2,16]{1,0:T(2,128)S(1)} %broadcast_multiply_fusion, s32[2,16]{1,0:T(2,128)S(1)} %copy-done.2), kind=kOutput, calls=%fused_computation | convolution fusion | flops 9437696 | bytes 590080 | tf_op jit(solution)/shard_map/sob,soct->scbt/dot_general | solution.py:335
  3.8 29.5 %all_to_all.10 = f32[128,4,128]{2,1,0:T(4,128)S(1)} all-to-all(f32[128,4,128]{2,1,0:T(4,128)S(1)} %bitcast.22), channel_id=1, replica_groups=mesh['z'=8,'y'=4,'x'=4,'c'=2] {'z','y','x'}, dimensions={0} | all-to-all | bytes 524288 | tf_op jit(solution)/shard_map/all_to_all | solution.py:345
  33.3 2.7 %collective-permute-start = (f32[512,128]{1,0:T(8,128)S(1)}, f32[512,128]{1,0:T(8,128)S(1)}, u32[]{:S(2)}, u32[]{:S(2)}) collective-permute-start(f32[512,128]{1,0:T(8,128)S(1)} %bitcast.19), channel_id=1, source_target_pairs={{0,1},{1,0},{2,3},{3,2},{4,5},{5,4},{6,7},{7,6},{8,9},{9,8},{10,11... | collective-permute-start | bytes 786440 | tf_op jit(solution)/shard_map/ppermute | solution.py:346
  36.0 1.2 %collective-permute-done.other_ref = f32[512,128]{1,0:T(8,128)S(1)} collective-permute-done((f32[512,128]{1,0:T(8,128)S(1)}, f32[512,128]{1,0:T(8,128)S(1)}, u32[]{:S(2)}, u32[]{:S(2)}) %collective-permute-start) | collective-permute-done | bytes 262176 | tf_op jit(solution)/shard_map/ppermute | solution.py:346
  37.2 1.0 %shard_map.68 = (f32[3,8,8,128]{3,2,1,0:T(8,128)S(1)}, f32[3,8,8,128]{3,2,1,0:T(8,128)S(1)}, f32[3,8,8,128]{3,2,1,0:T(8,128)S(1)}, f32[3,8,8,128]{3,2,1,0:T(8,128)S(1)}, f32[2,3,8,8,128]{4,3,2,1,0:T(8,128)S(1)}) custom-call(s32[1]{0:T(128)} %bitcast.core_ref, f32[512,128]{1,0:T(8,128)S(1)} %bitcast.20, f32[512,128]{1,0:T(8,128)S(1)} %collective-permute-done.other_ref), custom_call_target="tpu_custom_call" | custom-call | tf_op jit(solution)/shard_map/pallas_call | solution.py:59
  38.7 0.9 collective-permute-done.1.carry_ref
  40.1 5.8 %collective-permute-done.2.even_ref = f32[2,3,8,8,128]{4,3,2,1,0:T(8,128)S(1)} collective-permute-done((f32[2,3,8,8,128]{4,3,2,1,0:T(8,128)S(1)}, f32[2,3,8,8,128]{4,3,2,1,0:T(8,128)S(1)}, u32[]{:S(2)}, u32[]{:S(2)}) %collective-permute-start.2) | collective-permute-done | bytes 196640 | tf_op jit(solution)/shard_map/ppermute | solution.py:362
  45.9 1.2 %collective-permute-done.3.odd_side_ref = f32[2,3,8,8,128]{4,3,2,1,0:T(8,128)S(1)} collective-permute-done((f32[2,3,8,8,128]{4,3,2,1,0:T(8,128)S(1)}, f32[2,3,8,8,128]{4,3,2,1,0:T(8,128)S(1)}, u32[]{:S(2)}, u32[]{:S(2)}) %collective-permute-start.3) | collective-permute-done | bytes 196640 | tf_op jit(solution)/shard_map/ppermute | solution.py:363
  47.1 1.7 %shard_map.70 = (f32[3,8,8,128]{3,2,1,0:T(8,128)S(1)}, f32[3,8,8,128]{3,2,1,0:T(8,128)S(1)}, f32[3,8,8,128]{3,2,1,0:T(8,128)S(1)}) custom-call(s32[1]{0:T(128)} %bitcast.7.odd_ref, f32[2,3,8,8,128]{4,3,2,1,0:T(8,128)S(1)} %get-tuple-element.33.own_ref.refs_3_, f32[2,3,8,8,128]{4,3,2,1,0:T(8,128)S(1)} %collective-permute-done.2.even_ref, ...), custom_call_target="tpu_custom_call" | custom-call | tf_op jit(solution)/shard_map/pallas_call | solution.py:59
  48.9 1.6 %collective-permute-start.4 = (f32[3,8,8,128]{3,2,1,0:T(8,128)S(1)}, f32[3,8,8,128]{3,2,1,0:T(8,128)S(1)}, u32[]{:S(2)}, u32[]{:S(2)}) collective-permute-start(f32[3,8,8,128]{3,2,1,0:T(8,128)S(1)} %get-tuple-element.37), channel_id=1, source_target_pairs={{0,1},{1,0},{2,3},{3,2},{4,5},{5,4},{6,7},{7,6},{8,9},{9,8},{10,11... | collective-permute-start | bytes 294920 | tf_op jit(solution)/shard_map/ppermute | solution.py:356
  50.4 0.9 collective-permute-done.4.carry_ref
  51.7 6.0 %collective-permute-done.5.even_ref = f32[2,3,8,8,128]{4,3,2,1,0:T(8,128)S(1)} collective-permute-done((f32[2,3,8,8,128]{4,3,2,1,0:T(8,128)S(1)}, f32[2,3,8,8,128]{4,3,2,1,0:T(8,128)S(1)}, u32[]{:S(2)}, u32[]{:S(2)}) %collective-permute-start.5) | collective-permute-done | bytes 196640 | tf_op jit(solution)/shard_map/ppermute | solution.py:362
  57.7 1.1 %collective-permute-done.6.odd_side_ref = f32[2,3,8,8,128]{4,3,2,1,0:T(8,128)S(1)} collective-permute-done((f32[2,3,8,8,128]{4,3,2,1,0:T(8,128)S(1)}, f32[2,3,8,8,128]{4,3,2,1,0:T(8,128)S(1)}, u32[]{:S(2)}, u32[]{:S(2)}) %collective-permute-start.6) | collective-permute-done | bytes 196640 | tf_op jit(solution)/shard_map/ppermute | solution.py:363
  58.8 1.7 %shard_map.72 = (f32[3,8,8,128]{3,2,1,0:T(8,128)S(1)}, f32[3,8,8,128]{3,2,1,0:T(8,128)S(1)}, f32[3,8,8,128]{3,2,1,0:T(8,128)S(1)}) custom-call(s32[1]{0:T(128)} %bitcast.7.odd_ref, f32[2,3,8,8,128]{4,3,2,1,0:T(8,128)S(1)} %get-tuple-element.39.own_ref.refs_4_, f32[2,3,8,8,128]{4,3,2,1,0:T(8,128)S(1)} %collective-permute-done.5.even_ref, ...), custom_call_target="tpu_custom_call" | custom-call | tf_op jit(solution)/shard_map/pallas_call | solution.py:59
  60.6 1.5 %collective-permute-start.7 = (f32[3,8,8,128]{3,2,1,0:T(8,128)S(1)}, f32[3,8,8,128]{3,2,1,0:T(8,128)S(1)}, u32[]{:S(2)}, u32[]{:S(2)}) collective-permute-start(f32[3,8,8,128]{3,2,1,0:T(8,128)S(1)} %get-tuple-element.42), channel_id=1, source_target_pairs={{0,1},{1,0},{2,3},{3,2},{4,5},{5,4},{6,7},{7,6},{8,9},{9,8},{10,11... | collective-permute-start | bytes 294920 | tf_op jit(solution)/shard_map/ppermute | solution.py:356
  62.0 0.9 collective-permute-done.7.carry_ref
  63.6 5.7 %collective-permute-done.8.even_ref = f32[2,3,8,8,128]{4,3,2,1,0:T(8,128)S(1)} collective-permute-done((f32[2,3,8,8,128]{4,3,2,1,0:T(8,128)S(1)}, f32[2,3,8,8,128]{4,3,2,1,0:T(8,128)S(1)}, u32[]{:S(2)}, u32[]{:S(2)}) %collective-permute-start.8) | collective-permute-done | bytes 196640 | tf_op jit(solution)/shard_map/ppermute | solution.py:362
  69.3 1.3 %collective-permute-done.9.odd_side_ref = f32[2,3,8,8,128]{4,3,2,1,0:T(8,128)S(1)} collective-permute-done((f32[2,3,8,8,128]{4,3,2,1,0:T(8,128)S(1)}, f32[2,3,8,8,128]{4,3,2,1,0:T(8,128)S(1)}, u32[]{:S(2)}, u32[]{:S(2)}) %collective-permute-start.9) | collective-permute-done | bytes 196640 | tf_op jit(solution)/shard_map/ppermute | solution.py:363
  70.6 1.7 %shard_map.74 = (f32[3,8,8,128]{3,2,1,0:T(8,128)S(1)}, f32[3,8,8,128]{3,2,1,0:T(8,128)S(1)}, f32[3,8,8,128]{3,2,1,0:T(8,128)S(1)}) custom-call(s32[1]{0:T(128)} %bitcast.7.odd_ref, f32[2,3,8,8,128]{4,3,2,1,0:T(8,128)S(1)} %get-tuple-element.44.own_ref.refs_5_, f32[2,3,8,8,128]{4,3,2,1,0:T(8,128)S(1)} %collective-permute-done.8.even_ref, ...), custom_call_target="tpu_custom_call" | custom-call | tf_op jit(solution)/shard_map/pallas_call | solution.py:59
  72.4 1.4 %collective-permute-start.10 = (f32[3,8,8,128]{3,2,1,0:T(8,128)S(1)}, f32[3,8,8,128]{3,2,1,0:T(8,128)S(1)}, u32[]{:S(2)}, u32[]{:S(2)}) collective-permute-start(f32[3,8,8,128]{3,2,1,0:T(8,128)S(1)} %get-tuple-element.47), channel_id=1, source_target_pairs={{0,1},{1,0},{2,3},{3,2},{4,5},{5,4},{6,7},{7,6},{8,9},{9,8},{10,11... | collective-permute-start | bytes 294920 | tf_op jit(solution)/shard_map/ppermute | solution.py:374
  73.8 0.9 collective-permute-done.10.refs_8_
  75.7 1.0 %collective-permute-done.11.got_ref = f32[256,128]{1,0:T(8,128)S(1)} collective-permute-done((f32[256,128]{1,0:T(8,128)S(1)}, f32[256,128]{1,0:T(8,128)S(1)}, u32[]{:S(2)}, u32[]{:S(2)}) %collective-permute-start.11) | collective-permute-done | bytes 131104 | tf_op jit(solution)/shard_map/ppermute | solution.py:388
  76.7 19.5 %all_to_all.11 = f32[128,4,128]{2,1,0:T(4,128)S(1)} all-to-all(f32[128,4,128]{2,1,0:T(4,128)S(1)} %bitcast.21), channel_id=1, replica_groups=mesh['z'=8,'y'=4,'x'=4,'c'=2] {'z','y','x'}, dimensions={0} | all-to-all | bytes 524288 | tf_op jit(solution)/shard_map/all_to_all | solution.py:390
  96.2 1.1 %shard_map.77 = (f32[2,3,8,1024]{3,2,1,0:T(8,128)}, f32[1,1]{1,0:T(1,128)}, f32[1,3]{1,0:T(1,128)}) custom-call(f32[512,128]{1,0:T(8,128)S(1)} %bitcast.23), custom_call_target="tpu_custom_call" | custom-call | tf_op jit(solution)/shard_map/pallas_call | solution.py:59
  (26 shorter events, 4.5 us)
Async XLA Ops:
  0.7 0.7 copy-start.3
  1.3 0.7 copy-start.2
  2.0 1.4 %copy-start = (f32[3,8,1024]{2,1,0:T(8,128)S(1)}, f32[3,8,1024]{2,1,0:T(8,128)}, u32[]{:S(2)}) copy-start(f32[3,8,1024]{2,1,0:T(8,128)} %decay_ref.1) | copy-start | bytes 294916
  33.3 3.8 %collective-permute-start = (f32[512,128]{1,0:T(8,128)S(1)}, f32[512,128]{1,0:T(8,128)S(1)}, u32[]{:S(2)}, u32[]{:S(2)}) collective-permute-start(f32[512,128]{1,0:T(8,128)S(1)} %bitcast.19), channel_id=1, source_target_pairs={{0,1},{1,0},{2,3},{3,2},{4,5},{5,4},{6,7},{7,6},{8,9},{9,8},{10,11... | collective-permute-start | bytes 786440 | tf_op jit(solution)/shard_map/ppermute | solution.py:346
  38.2 1.4 %collective-permute-start.1 = (f32[3,8,8,128]{3,2,1,0:T(8,128)S(1)}, f32[3,8,8,128]{3,2,1,0:T(8,128)S(1)}, u32[]{:S(2)}, u32[]{:S(2)}) collective-permute-start(f32[3,8,8,128]{3,2,1,0:T(8,128)S(1)} %get-tuple-element.30), channel_id=1, source_target_pairs={{0,1},{1,0},{2,3},{3,2},{4,5},{5,4},{6,7},{7,6},{8,9},{9,8},{10,11... | collective-permute-start | bytes 294920 | tf_op jit(solution)/shard_map/ppermute | solution.py:356
  39.7 6.2 %collective-permute-start.2 = (f32[2,3,8,8,128]{4,3,2,1,0:T(8,128)S(1)}, f32[2,3,8,8,128]{4,3,2,1,0:T(8,128)S(1)}, u32[]{:S(2)}, u32[]{:S(2)}) collective-permute-start(f32[2,3,8,8,128]{4,3,2,1,0:T(8,128)S(1)} %get-tuple-element.33.own_ref.refs_3_), channel_id=1, source_target_pairs={{0,2},{2,0},{4,6},{6,4},{14,12},{12,14},{10,8},{8,10},{16,18},{18,... | collective-permute-start | bytes 589832 | tf_op jit(solution)/shard_map/ppermute | solution.py:362
  40.1 7.0 %collective-permute-start.3 = (f32[2,3,8,8,128]{4,3,2,1,0:T(8,128)S(1)}, f32[2,3,8,8,128]{4,3,2,1,0:T(8,128)S(1)}, u32[]{:S(2)}, u32[]{:S(2)}) collective-permute-start(f32[2,3,8,8,128]{4,3,2,1,0:T(8,128)S(1)} %get-tuple-element.33.own_ref.refs_3_), channel_id=1, source_target_pairs={{2,4},{4,2},{6,14},{14,6},{12,10},{10,12},{8,16},{16,8},{18,20},{2... | collective-permute-start | bytes 589832 | tf_op jit(solution)/shard_map/ppermute | solution.py:363
  48.9 2.5 %collective-permute-start.4 = (f32[3,8,8,128]{3,2,1,0:T(8,128)S(1)}, f32[3,8,8,128]{3,2,1,0:T(8,128)S(1)}, u32[]{:S(2)}, u32[]{:S(2)}) collective-permute-start(f32[3,8,8,128]{3,2,1,0:T(8,128)S(1)} %get-tuple-element.37), channel_id=1, source_target_pairs={{0,1},{1,0},{2,3},{3,2},{4,5},{5,4},{6,7},{7,6},{8,9},{9,8},{10,11... | collective-permute-start | bytes 294920 | tf_op jit(solution)/shard_map/ppermute | solution.py:356
  51.5 6.2 %collective-permute-start.5 = (f32[2,3,8,8,128]{4,3,2,1,0:T(8,128)S(1)}, f32[2,3,8,8,128]{4,3,2,1,0:T(8,128)S(1)}, u32[]{:S(2)}, u32[]{:S(2)}) collective-permute-start(f32[2,3,8,8,128]{4,3,2,1,0:T(8,128)S(1)} %get-tuple-element.39.own_ref.refs_4_), channel_id=1, source_target_pairs={{0,2},{2,0},{4,6},{6,4},{14,12},{12,14},{10,8},{8,10},{16,18},{18,... | collective-permute-start | bytes 589832 | tf_op jit(solution)/shard_map/ppermute | solution.py:362
  51.6 7.2 %collective-permute-start.6 = (f32[2,3,8,8,128]{4,3,2,1,0:T(8,128)S(1)}, f32[2,3,8,8,128]{4,3,2,1,0:T(8,128)S(1)}, u32[]{:S(2)}, u32[]{:S(2)}) collective-permute-start(f32[2,3,8,8,128]{4,3,2,1,0:T(8,128)S(1)} %get-tuple-element.39.own_ref.refs_4_), channel_id=1, source_target_pairs={{2,4},{4,2},{6,14},{14,6},{12,10},{10,12},{8,16},{16,8},{18,20},{2... | collective-permute-start | bytes 589832 | tf_op jit(solution)/shard_map/ppermute | solution.py:363
  60.6 2.9 %copy-start.1 = (f32[2,16,3,1024]{3,1,2,0:T(8,128)S(1)}, f32[2,16,3,1024]{3,1,2,0:T(8,128)}, u32[]{:S(2)}) copy-start(f32[2,16,3,1024]{3,1,2,0:T(8,128)} %param.4) | copy-start | bytes 1179652
  60.6 2.4 %collective-permute-start.7 = (f32[3,8,8,128]{3,2,1,0:T(8,128)S(1)}, f32[3,8,8,128]{3,2,1,0:T(8,128)S(1)}, u32[]{:S(2)}, u32[]{:S(2)}) collective-permute-start(f32[3,8,8,128]{3,2,1,0:T(8,128)S(1)} %get-tuple-element.42), channel_id=1, source_target_pairs={{0,1},{1,0},{2,3},{3,2},{4,5},{5,4},{6,7},{7,6},{8,9},{9,8},{10,11... | collective-permute-start | bytes 294920 | tf_op jit(solution)/shard_map/ppermute | solution.py:356
  63.1 6.2 %collective-permute-start.8 = (f32[2,3,8,8,128]{4,3,2,1,0:T(8,128)S(1)}, f32[2,3,8,8,128]{4,3,2,1,0:T(8,128)S(1)}, u32[]{:S(2)}, u32[]{:S(2)}) collective-permute-start(f32[2,3,8,8,128]{4,3,2,1,0:T(8,128)S(1)} %get-tuple-element.44.own_ref.refs_5_), channel_id=1, source_target_pairs={{0,2},{2,0},{4,6},{6,4},{14,12},{12,14},{10,8},{8,10},{16,18},{18,... | collective-permute-start | bytes 589832 | tf_op jit(solution)/shard_map/ppermute | solution.py:362
  63.3 7.3 %collective-permute-start.9 = (f32[2,3,8,8,128]{4,3,2,1,0:T(8,128)S(1)}, f32[2,3,8,8,128]{4,3,2,1,0:T(8,128)S(1)}, u32[]{:S(2)}, u32[]{:S(2)}) collective-permute-start(f32[2,3,8,8,128]{4,3,2,1,0:T(8,128)S(1)} %get-tuple-element.44.own_ref.refs_5_), channel_id=1, source_target_pairs={{2,4},{4,2},{6,14},{14,6},{12,10},{10,12},{8,16},{16,8},{18,20},{2... | collective-permute-start | bytes 589832 | tf_op jit(solution)/shard_map/ppermute | solution.py:363
  72.4 2.4 %collective-permute-start.10 = (f32[3,8,8,128]{3,2,1,0:T(8,128)S(1)}, f32[3,8,8,128]{3,2,1,0:T(8,128)S(1)}, u32[]{:S(2)}, u32[]{:S(2)}) collective-permute-start(f32[3,8,8,128]{3,2,1,0:T(8,128)S(1)} %get-tuple-element.47), channel_id=1, source_target_pairs={{0,1},{1,0},{2,3},{3,2},{4,5},{5,4},{6,7},{7,6},{8,9},{9,8},{10,11... | collective-permute-start | bytes 294920 | tf_op jit(solution)/shard_map/ppermute | solution.py:374
  75.2 1.4 %collective-permute-start.11 = (f32[256,128]{1,0:T(8,128)S(1)}, f32[256,128]{1,0:T(8,128)S(1)}, u32[]{:S(2)}, u32[]{:S(2)}) collective-permute-start(f32[256,128]{1,0:T(8,128)S(1)} %get-tuple-element.49), channel_id=1, source_target_pairs={{0,1},{1,0},{2,3},{3,2},{4,5},{5,4},{6,7},{7,6},{8,9},{9,8},{10,11... | collective-permute-start | bytes 393224 | tf_op jit(solution)/shard_map/ppermute | solution.py:388

commit v3 on v2

--- a/solution.py
+++ b/solution.py
@@ -17,6 +17,7 @@
 TM = ("z", "y")
 GRID = ("x", "c")
 ZYX = ("z", "y", "x")
+ALL = ("z", "y", "x", "c")
 
 wave_coef = 0.6
 diffusion = 0.05
@@ -36,8 +37,9 @@
 
 def swap_pairs(first):
     pairs = []
-    for tile in range(first, CHIPS, 2):
-        a, b = chip_of(tile), chip_of((tile + 1) % CHIPS)
+    for tile in range(CHIPS):
+        core = (tile + first) % 2
+        a, b = 2 * chip_of(tile) + core, 2 * chip_of((tile + 1) % CHIPS) + core
         pairs += [(a, b), (b, a)]
     return pairs
 
@@ -53,36 +55,81 @@
     return pltpu.with_memory_space_constraint(value, pltpu.VMEM)
 
 
-def call(kernel, outs, scalars, *operands, scratch=()):
+def call(kernel, outs, scalars, *operands, far=(), far_out=(), scratch=()):
     vmem = pl.BlockSpec(memory_space=pltpu.VMEM)
+    hbm = pl.BlockSpec(memory_space=pl.ANY)
     smem = pl.BlockSpec(memory_space=pltpu.SMEM)
-    return pl.pallas_call(
+    outs = outs if isinstance(outs, tuple) else (outs,)
+    results = pl.pallas_call(
         kernel,
         out_shape=outs,
-        in_specs=[smem] * len(scalars) + [vmem] * len(operands),
-        out_specs=jax.tree.map(lambda _: vmem, outs),
+        in_specs=[smem] * len(scalars) + [hbm] * len(far) + [vmem] * len(operands),
+        out_specs=[hbm if i in far_out else vmem for i in range(len(outs))],
         scratch_shapes=list(scratch),
-    )(*scalars, *map(near, operands))
+    )(*scalars, *far, *map(near, operands))
+    return results if len(outs) > 1 else results[0]
 
 
 def iota(dim):
     return lax.broadcasted_iota(jnp.int32, (8, 128), dim)
 
 
-def pack_kernel(odd_ref, tiles_ref, decay_ref, out_ref, rows_ref):
-    odd = odd_ref[0] == 1
+def pack_kernel(
+    place_ref,
+    departure_ref,
+    weight_ref,
+    block_ref,
+    decay_ref,
+    out_ref,
+    values_ref,
+    weights_ref,
+    blocks_ref,
+    decays_ref,
+    rows_ref,
+    sems,
+):
+    copies = [
+        pltpu.make_async_copy(weight_ref, weights_ref, sems.at[0]),
+        pltpu.make_async_copy(block_ref, blocks_ref, sems.at[1]),
+        pltpu.make_async_copy(decay_ref, decays_ref, sems.at[2]),
+    ]
+    parts = {
+        (j, f): pltpu.make_async_copy(
+            departure_ref.at[j, f], values_ref.at[j, f], sems.at[3 + FIELDS * j + f]
+        )
+        for j in range(2)
+        for f in range(FIELDS)
+    }
+    for copy in copies[:2] + list(parts.values()) + copies[2:]:
+        copy.start()
+    copies[0].wait()
+    copies[1].wait()
+    block = lax.broadcasted_iota(jnp.int32, (8, 16), 0)
     for j in range(2):
+        emphasis = 1.0 + 2.0 * (place_ref[0] * 2 + j).astype(jnp.float32) / 63.0
+        choose = jnp.where(
+            blocks_ref[j : j + 1, :] == block, emphasis * weights_ref[j : j + 1, :], 0.0
+        )
         for f in range(FIELDS):
+            parts[j, f].wait()
+            tiles = jnp.dot(
+                choose,
+                values_ref[j, f],
+                precision=lax.Precision.HIGHEST,
+                preferred_element_type=jnp.float32,
+            )
             for r in range(8):
-                rows_ref[pl.ds(24 * j + 8 * f + r, 8, stride=64), :] = tiles_ref[
-                    j, f, :, 128 * r : 128 * r + 128
+                rows_ref[pl.ds(24 * j + 8 * f + r, 8, stride=64), :] = tiles[
+                    :, 128 * r : 128 * r + 128
                 ]
+    copies[2].wait()
+    odd = (place_ref[0] & 1) == 1
     for b in range(8):
         span = slice(128 * b, 128 * b + 128)
         rows_ref[64 * b + 48 : 64 * b + 56, :] = jnp.where(
-            odd, decay_ref[2, :, span], decay_ref[0, :, span]
-        )
-        rows_ref[64 * b + 56 : 64 * b + 64, :] = decay_ref[1, :, span]
+            odd, decays_ref[2, :, span], decays_ref[0, :, span]
+        )
+        rows_ref[64 * b + 56 : 64 * b + 64, :] = decays_ref[1, :, span]
     for b in range(8):
         block = rows_ref[64 * b : 64 * b + 64, :]
         both = jnp.concatenate([block, pltpu.roll(block, 124, 1)], axis=0)
@@ -195,40 +242,35 @@
             state_ref[f, 8:16] = own_ref[j, f]
             state_ref[f, 16:24] = jnp.where(odd, two, one)
         p, q, r = state_ref[0], state_ref[1], state_ref[2]
-        keep = 1.0 - 4.0 * diffusion
-        wave = 0.5 * wave_coef
+        keep = 1.0 / diffusion - 4.0
+        wave = 0.5 * wave_coef / diffusion
+        wave_new = 0.5 * wave_coef
+        turn = coriolis / diffusion
         for step in range(STEPS):
             n = p.shape[0]
-            inside = slice(1, n - 1)
-            pc, rc = p[inside], r[inside]
+            pc, rc = p[1 : n - 1], r[1 : n - 1]
+            side = wave * rc
             p1 = (
-                keep * pc
-                + diffusion * (p[: n - 2] + p[2:])
+                (keep * pc + (p[: n - 2] + p[2:]))
                 + wave * (q[2:] - q[: n - 2])
-                + next_row(diffusion * pc + wave * rc)
-                + last_row(diffusion * pc - wave * rc)
-            )
-            m = n - 2
-            q2, r2, p2 = q[inside], rc, p1
-            qc, rcc, pcc = q2[1 : m - 1], r2[1 : m - 1], p2[1 : m - 1]
-            scaled = diffusion * qc
+                + (next_row(pc + side) + last_row(pc - side))
+            )
+            qc, rc, pc = q[2 : n - 2], r[2 : n - 2], p1[1 : n - 3]
+            push = wave_new * p1
+            side = push[1 : n - 3]
             q1 = (
-                keep * qc
-                + diffusion * (q2[: m - 2] + q2[2:])
-                + wave * (p2[2:] - p2[: m - 2])
-                + coriolis * rcc
-                + next_row(scaled)
-                + last_row(scaled)
+                (keep * qc + (q[1 : n - 3] + q[3 : n - 1]))
+                + ((push[2:] - push[: n - 4]) + turn * rc)
+                + (next_row(qc) + last_row(qc))
             )
             r1 = (
-                keep * rcc
-                + diffusion * (r2[: m - 2] + r2[2:])
-                - coriolis * qc
-                + next_row(diffusion * rcc + wave * pcc)
-                + last_row(diffusion * rcc - wave * pcc)
-            )
-            p, q, r = pcc, q1, r1
-        corrections.append([v - decay_ref[f] * own_ref[j, f] for f, v in enumerate((p, q, r))])
+                (keep * rc + (r[1 : n - 3] + r[3 : n - 1]))
+                - turn * qc
+                + (next_row(rc + side) + last_row(rc - side))
+            )
+            p, q, r = pc, q1, r1
+        unit = diffusion**STEPS
+        corrections.append([unit * v - decay_ref[f] * own_ref[j, f] for f, v in enumerate((p, q, r))])
     for f in range(FIELDS):
         chain_here(
             corrections[0][f], corrections[1][f], decay_ref[f], pair, first_ref, second_ref, carry_ref, f
@@ -295,7 +337,7 @@
     out_ref[256:512, :] = jnp.where(counted, total, jnp.where(low, got, mine))
 
 
-def unpack_kernel(in_ref, out_ref, misfit_ref, changes_ref, rows_ref):
+def unpack_kernel(in_ref, out_ref, misfit_ref, changes_ref, rows_ref, stage_ref, sems):
     sums = [in_ref[8 * v : 8 * v + 8, :] for v in range(64)]
     while len(sums) > 1:
         sums = [a + b for a, b in zip(sums[::2], sums[1::2])]
@@ -303,6 +345,7 @@
     misfit_ref[...] = total[0:1, 3:4]
     changes_ref[...] = (total / (pltpu.roll(total, 124, 1) + epsilon))[0:1, 0:ITERS]
     second = (lax.broadcasted_iota(jnp.int32, (128, 128), 0) & 7) >= 4
+    copies = []
     for b in range(8):
         for i in range(16):
             at = 4 * chip_of(16 * b + i)
@@ -314,33 +357,42 @@
         for j in range(2):
             for f in range(FIELDS):
                 at = 24 * j + 8 * f
-                out_ref[j, f, :, 128 * b : 128 * b + 128] = turned[at : at + 8, :]
+                stage_ref[b, j, f] = turned[at : at + 8, :]
+        copies.append(
+            pltpu.make_async_copy(
+                stage_ref.at[b], out_ref.at[:, :, :, 128 * b : 128 * b + 128], sems.at[b]
+            )
+        )
+        copies[-1].start()
+    for copy in copies:
+        copy.wait()
 
 
 def per_device(departure, obs_weight, obs_block, coarse_decay):
     z, y, x, core = (lax.axis_index(name) for name in ("z", "y", "x", "c"))
     core_arg = core.astype(jnp.int32).reshape(1)
-    tile_odd = ((x + y + z) % 2).astype(jnp.int32).reshape(1)
-    pair_odd = (y % 2).astype(jnp.int32).reshape(1)
+    tile_odd = ((x + y + z + core) % 2).astype(jnp.int32).reshape(1)
+    place = (z * NY + y).astype(jnp.int32).reshape(1)
 
     position = ((z * NY + y) * 2 + jnp.arange(2)).astype(jnp.float32)
-    emphasis = 1.0 + 2.0 * position / 63.0
-    strength = emphasis[:, None] * obs_weight
+    strength = (1.0 + 2.0 * position / 63.0)[:, None] * obs_weight
     misfit_part = 0.5 * jnp.sum(
         strength[:, :, None, None] * departure * departure, axis=(0, 1, 2)
     ).reshape(8, 128)
-    choose = jnp.where(
-        obs_block[:, :, None] == jnp.arange(8, dtype=jnp.int32), strength[:, :, None], 0.0
-    )
-    tiles = jnp.einsum("sob,soct->scbt", choose, departure, precision=lax.Precision.HIGHEST)
 
     sent = call(
         pack_kernel,
         shape(512, 128),
-        (pair_odd,),
-        tiles,
-        coarse_decay,
-        scratch=[pltpu.VMEM((512, 128), jnp.float32)],
+        (place,),
+        far=(departure.transpose(0, 2, 1, 3), obs_weight, obs_block, coarse_decay),
+        scratch=[
+            pltpu.VMEM((2, FIELDS, 16, 1024), jnp.float32),
+            pltpu.VMEM((2, 16), jnp.float32),
+            pltpu.VMEM((2, 16), jnp.int32),
+            pltpu.VMEM((FIELDS, 8, 1024), jnp.float32),
+            pltpu.VMEM((512, 128), jnp.float32),
+            pltpu.SemaphoreType.DMA((9,)),
+        ],
     )
     got = lax.all_to_all(sent.reshape(CHIPS, 4, 128), ZYX, 0, 0).reshape(512, 128)
     other = lax.ppermute(got, "c", SIBLING)
@@ -359,8 +411,8 @@
         )
         zeros.append(zero)
         aboves.append(above)
-        side_even = lax.ppermute(above, ZYX, swap_pairs(0))
-        side_odd = lax.ppermute(above, ZYX, swap_pairs(1))
+        side_even = lax.ppermute(above, ALL, swap_pairs(0))
+        side_odd = lax.ppermute(above, ALL, swap_pairs(1))
         first, second, carry = call(
             fine_kernel,
             (field, field, field),
@@ -397,7 +449,12 @@
         ),
         (),
         home,
-        scratch=[square],
+        far_out=(0,),
+        scratch=[
+            square,
+            pltpu.VMEM((8, 2, FIELDS, 8, 128), jnp.float32),
+            pltpu.SemaphoreType.DMA((8,)),
+        ],
     )
     return adjoint, misfit.reshape(()), changes.reshape(ITERS)
 

time: 97.5 us -> 96.7 us (level)
  Pallas kernels: 8.58 us -> 11 us
  waiting for transfers between devices: 27.1 us -> 25.6 us
  matrix products: 1.35 us -> 0 us
  local copies, waits for them, and re-layouts: 1.29 us -> 0.3 us
    pallas_call x11, Pallas kernels: 8.58 us -> 11 us  [call(): pl.pallas_call(kernel, out_shape=outs, in_specs=[smem] * len(scalars) + [...]
    ppermute x6, waiting for transfers between devices: 21.2 us -> 19.7 us  [the longest x3 19.7 us: per_device(): side_even = lax.ppermute(above, ALL, swap_pairs(0))]
    dot_general x1 -> x0, matrix products: 1.35 us -> none  [per_device(): jnp.einsum('sob,soct->scbt', choose, departure, precision=lax.Precision.H...]
    unnamed x8 -> x4, local copies, waits for them, and re-layouts: 1.29 us -> 0.3 us
  transfers between devices with their start and end apart: 12 -> 12, of which waited for: 12 -> 9; matrix products, arithmetic and copies ran while one was open for 0% -> 0% of each run, Pallas kernels for 0% -> 0%
where the time goes in v3:
time: 96.7 us; the launch traced here: 96.5 us
  blocking collectives  49 us (51%)
  waiting for transfers between devices  25.6 us (26%)
  Pallas kernels  11 us (11%)
  starting transfers between devices  9.35 us (10%)
    all_to_all x1, blocking collectives, per_device(): lax.all_to_all(sent.reshape(CHIPS, 4, 128), ZYX, 0, 0).reshape(512, 128)  29.5 us
    ppermute x3, waiting for transfers between devices, per_device(): side_even = lax.ppermute(above, ALL, swap_pairs(0))  19.7 us
    all_to_all x1, blocking collectives, per_device(): lax.all_to_all(back.reshape(CHIPS, 4, 128), ZYX, 0, 0).reshape(512, 128)  19.5 us
    pallas_call x11, Pallas kernels, call(): pl.pallas_call(kernel, out_shape=outs, in_specs=[smem] * len(scalars) + [...  11 us
    ppermute x4, starting transfers between devices, per_device(): carry = lax.ppermute(carry, 'c', SIBLING)  5.21 us
    ppermute x4, waiting for transfers between devices, per_device(): carry = lax.ppermute(carry, 'c', SIBLING)  3.77 us
    ppermute x1, starting transfers between devices, per_device(): other = lax.ppermute(got, 'c', SIBLING)  2.69 us
  transfers between devices with their start and end apart: 12, of which 9 were waited for; matrix products, arithmetic and copies ran while one was open for 0% of the time, Pallas kernels for 0%

profile of v3, /device:TPU:1, one launch (start us, length us, event | category | flops | bytes accessed | tf_op | source)
XLA Modules:
  0.0 96.5 jit_solution(15044627031134111970)
XLA Ops:
  0.6 2.3 %shard_map.67 = f32[512,128]{1,0:T(8,128)S(1)} custom-call(s32[1]{0:T(128)} %bitcast.1.place_ref, f32[2,3,16,1024]{3,2,1,0:T(8,128)} %bitcast.17, f32[2,16]{1,0:T(2,128)} %weight_ref.1, s32[2,16]{1,0:T(2,128)} %block_ref.1, f32[3,8,1024]{2,1,0:T(8,128)} %decay_ref.1), custom_call_target="tpu_custom_call" | custom-call | tf_op jit(solution)/shard_map/pallas_call | solution.py:63
  3.0 29.5 %all_to_all.10 = f32[128,4,128]{2,1,0:T(4,128)S(1)} all-to-all(f32[128,4,128]{2,1,0:T(4,128)S(1)} %bitcast.16), channel_id=1, replica_groups=mesh['z'=8,'y'=4,'x'=4,'c'=2] {'z','y','x'}, dimensions={0} | all-to-all | bytes 524288 | tf_op jit(solution)/shard_map/all_to_all | solution.py:397
  32.5 2.7 %collective-permute-start = (f32[512,128]{1,0:T(8,128)S(1)}, f32[512,128]{1,0:T(8,128)S(1)}, u32[]{:S(2)}, u32[]{:S(2)}) collective-permute-start(f32[512,128]{1,0:T(8,128)S(1)} %bitcast.12), channel_id=1, source_target_pairs={{0,1},{1,0},{2,3},{3,2},{4,5},{5,4},{6,7},{7,6},{8,9},{9,8},{10,11... | collective-permute-start | bytes 786440 | tf_op jit(solution)/shard_map/ppermute | solution.py:398
  35.2 1.2 %collective-permute-done.other_ref = f32[512,128]{1,0:T(8,128)S(1)} collective-permute-done((f32[512,128]{1,0:T(8,128)S(1)}, f32[512,128]{1,0:T(8,128)S(1)}, u32[]{:S(2)}, u32[]{:S(2)}) %collective-permute-start) | collective-permute-done | bytes 262176 | tf_op jit(solution)/shard_map/ppermute | solution.py:398
  36.4 1.0 %shard_map.68 = (f32[3,8,8,128]{3,2,1,0:T(8,128)S(1)}, f32[3,8,8,128]{3,2,1,0:T(8,128)S(1)}, f32[3,8,8,128]{3,2,1,0:T(8,128)S(1)}, f32[3,8,8,128]{3,2,1,0:T(8,128)S(1)}, f32[2,3,8,8,128]{4,3,2,1,0:T(8,128)S(1)}) custom-call(s32[1]{0:T(128)} %bitcast.core_ref, f32[512,128]{1,0:T(8,128)S(1)} %bitcast.13, f32[512,128]{1,0:T(8,128)S(1)} %collective-permute-done.other_ref), custom_call_target="tpu_custom_call" | custom-call | tf_op jit(solution)/shard_map/pallas_call | solution.py:63
  37.4 0.4 collective-permute-start.1
  37.9 0.9 collective-permute-done.1.carry_ref
  39.4 6.4 %collective-permute-done.2.even_ref = f32[2,3,8,8,128]{4,3,2,1,0:T(8,128)S(1)} collective-permute-done((f32[2,3,8,8,128]{4,3,2,1,0:T(8,128)S(1)}, f32[2,3,8,8,128]{4,3,2,1,0:T(8,128)S(1)}, u32[]{:S(2)}, u32[]{:S(2)}) %collective-permute-start.2) | collective-permute-done | bytes 196640 | tf_op jit(solution)/shard_map/ppermute | solution.py:414
  45.8 1.7 %shard_map.70 = (f32[3,8,8,128]{3,2,1,0:T(8,128)S(1)}, f32[3,8,8,128]{3,2,1,0:T(8,128)S(1)}, f32[3,8,8,128]{3,2,1,0:T(8,128)S(1)}) custom-call(s32[1]{0:T(128)} %bitcast.5.odd_ref, f32[2,3,8,8,128]{4,3,2,1,0:T(8,128)S(1)} %get-tuple-element.33.own_ref.refs_3_, f32[2,3,8,8,128]{4,3,2,1,0:T(8,128)S(1)} %collective-permute-done.2.even_ref, ...), custom_call_target="tpu_custom_call" | custom-call | tf_op jit(solution)/shard_map/pallas_call | solution.py:63
  47.5 1.8 %collective-permute-start.4 = (f32[3,8,8,128]{3,2,1,0:T(8,128)S(1)}, f32[3,8,8,128]{3,2,1,0:T(8,128)S(1)}, u32[]{:S(2)}, u32[]{:S(2)}) collective-permute-start(f32[3,8,8,128]{3,2,1,0:T(8,128)S(1)} %get-tuple-element.37), channel_id=1, source_target_pairs={{0,1},{1,0},{2,3},{3,2},{4,5},{5,4},{6,7},{7,6},{8,9},{9,8},{10,11... | collective-permute-start | bytes 294920 | tf_op jit(solution)/shard_map/ppermute | solution.py:408
  49.3 0.9 collective-permute-done.4.carry_ref
  50.6 7.1 %collective-permute-done.5.even_ref = f32[2,3,8,8,128]{4,3,2,1,0:T(8,128)S(1)} collective-permute-done((f32[2,3,8,8,128]{4,3,2,1,0:T(8,128)S(1)}, f32[2,3,8,8,128]{4,3,2,1,0:T(8,128)S(1)}, u32[]{:S(2)}, u32[]{:S(2)}) %collective-permute-start.5) | collective-permute-done | bytes 196640 | tf_op jit(solution)/shard_map/ppermute | solution.py:414
  57.7 1.7 %shard_map.72 = (f32[3,8,8,128]{3,2,1,0:T(8,128)S(1)}, f32[3,8,8,128]{3,2,1,0:T(8,128)S(1)}, f32[3,8,8,128]{3,2,1,0:T(8,128)S(1)}) custom-call(s32[1]{0:T(128)} %bitcast.5.odd_ref, f32[2,3,8,8,128]{4,3,2,1,0:T(8,128)S(1)} %get-tuple-element.39.own_ref.refs_4_, f32[2,3,8,8,128]{4,3,2,1,0:T(8,128)S(1)} %collective-permute-done.5.even_ref, ...), custom_call_target="tpu_custom_call" | custom-call | tf_op jit(solution)/shard_map/pallas_call | solution.py:63
  59.4 1.4 %collective-permute-start.7 = (f32[3,8,8,128]{3,2,1,0:T(8,128)S(1)}, f32[3,8,8,128]{3,2,1,0:T(8,128)S(1)}, u32[]{:S(2)}, u32[]{:S(2)}) collective-permute-start(f32[3,8,8,128]{3,2,1,0:T(8,128)S(1)} %get-tuple-element.42), channel_id=1, source_target_pairs={{0,1},{1,0},{2,3},{3,2},{4,5},{5,4},{6,7},{7,6},{8,9},{9,8},{10,11... | collective-permute-start | bytes 294920 | tf_op jit(solution)/shard_map/ppermute | solution.py:408
  60.8 0.9 collective-permute-done.7.carry_ref
  62.8 6.2 %collective-permute-done.8.even_ref = f32[2,3,8,8,128]{4,3,2,1,0:T(8,128)S(1)} collective-permute-done((f32[2,3,8,8,128]{4,3,2,1,0:T(8,128)S(1)}, f32[2,3,8,8,128]{4,3,2,1,0:T(8,128)S(1)}, u32[]{:S(2)}, u32[]{:S(2)}) %collective-permute-start.8) | collective-permute-done | bytes 196640 | tf_op jit(solution)/shard_map/ppermute | solution.py:414
  69.0 1.7 %shard_map.74 = (f32[3,8,8,128]{3,2,1,0:T(8,128)S(1)}, f32[3,8,8,128]{3,2,1,0:T(8,128)S(1)}, f32[3,8,8,128]{3,2,1,0:T(8,128)S(1)}) custom-call(s32[1]{0:T(128)} %bitcast.5.odd_ref, f32[2,3,8,8,128]{4,3,2,1,0:T(8,128)S(1)} %get-tuple-element.44.own_ref.refs_5_, f32[2,3,8,8,128]{4,3,2,1,0:T(8,128)S(1)} %collective-permute-done.8.even_ref, ...), custom_call_target="tpu_custom_call" | custom-call | tf_op jit(solution)/shard_map/pallas_call | solution.py:63
  70.8 1.6 %collective-permute-start.10 = (f32[3,8,8,128]{3,2,1,0:T(8,128)S(1)}, f32[3,8,8,128]{3,2,1,0:T(8,128)S(1)}, u32[]{:S(2)}, u32[]{:S(2)}) collective-permute-start(f32[3,8,8,128]{3,2,1,0:T(8,128)S(1)} %get-tuple-element.47), channel_id=1, source_target_pairs={{0,1},{1,0},{2,3},{3,2},{4,5},{5,4},{6,7},{7,6},{8,9},{9,8},{10,11... | collective-permute-start | bytes 294920 | tf_op jit(solution)/shard_map/ppermute | solution.py:426
  72.3 0.9 collective-permute-done.10.refs_8_
  73.3 0.4 shard_map.75
  73.7 0.4 collective-permute-start.11
  74.2 1.0 %collective-permute-done.11.got_ref = f32[256,128]{1,0:T(8,128)S(1)} collective-permute-done((f32[256,128]{1,0:T(8,128)S(1)}, f32[256,128]{1,0:T(8,128)S(1)}, u32[]{:S(2)}, u32[]{:S(2)}) %collective-permute-start.11) | collective-permute-done | bytes 131104 | tf_op jit(solution)/shard_map/ppermute | solution.py:440
  75.2 19.5 %all_to_all.11 = f32[128,4,128]{2,1,0:T(4,128)S(1)} all-to-all(f32[128,4,128]{2,1,0:T(4,128)S(1)} %bitcast.14), channel_id=1, replica_groups=mesh['z'=8,'y'=4,'x'=4,'c'=2] {'z','y','x'}, dimensions={0} | all-to-all | bytes 524288 | tf_op jit(solution)/shard_map/all_to_all | solution.py:442
  94.7 1.6 %shard_map.77 = (f32[2,3,8,1024]{3,2,1,0:T(8,128)}, f32[1,1]{1,0:T(1,128)}, f32[1,3]{1,0:T(1,128)}) custom-call(f32[512,128]{1,0:T(8,128)S(1)} %bitcast.15), custom_call_target="tpu_custom_call" | custom-call | tf_op jit(solution)/shard_map/pallas_call | solution.py:63
  (21 shorter events, 1.9 us)
Async XLA Ops:
  32.5 3.8 %collective-permute-start = (f32[512,128]{1,0:T(8,128)S(1)}, f32[512,128]{1,0:T(8,128)S(1)}, u32[]{:S(2)}, u32[]{:S(2)}) collective-permute-start(f32[512,128]{1,0:T(8,128)S(1)} %bitcast.12), channel_id=1, source_target_pairs={{0,1},{1,0},{2,3},{3,2},{4,5},{5,4},{6,7},{7,6},{8,9},{9,8},{10,11... | collective-permute-start | bytes 786440 | tf_op jit(solution)/shard_map/ppermute | solution.py:398
  37.4 1.4 %collective-permute-start.1 = (f32[3,8,8,128]{3,2,1,0:T(8,128)S(1)}, f32[3,8,8,128]{3,2,1,0:T(8,128)S(1)}, u32[]{:S(2)}, u32[]{:S(2)}) collective-permute-start(f32[3,8,8,128]{3,2,1,0:T(8,128)S(1)} %get-tuple-element.30), channel_id=1, source_target_pairs={{0,1},{1,0},{2,3},{3,2},{4,5},{5,4},{6,7},{7,6},{8,9},{9,8},{10,11... | collective-permute-start | bytes 294920 | tf_op jit(solution)/shard_map/ppermute | solution.py:408
  38.9 6.8 %collective-permute-start.2 = (f32[2,3,8,8,128]{4,3,2,1,0:T(8,128)S(1)}, f32[2,3,8,8,128]{4,3,2,1,0:T(8,128)S(1)}, u32[]{:S(2)}, u32[]{:S(2)}) collective-permute-start(f32[2,3,8,8,128]{4,3,2,1,0:T(8,128)S(1)} %get-tuple-element.33.own_ref.refs_3_), channel_id=1, source_target_pairs={{0,2},{2,0},{3,5},{5,3},{4,6},{6,4},{7,15},{15,7},{14,12},{12,14},... | collective-permute-start | bytes 589832 | tf_op jit(solution)/shard_map/ppermute | solution.py:414
  39.0 6.7 %collective-permute-start.3 = (f32[2,3,8,8,128]{4,3,2,1,0:T(8,128)S(1)}, f32[2,3,8,8,128]{4,3,2,1,0:T(8,128)S(1)}, u32[]{:S(2)}, u32[]{:S(2)}) collective-permute-start(f32[2,3,8,8,128]{4,3,2,1,0:T(8,128)S(1)} %get-tuple-element.33.own_ref.refs_3_), channel_id=1, source_target_pairs={{1,3},{3,1},{2,4},{4,2},{5,7},{7,5},{6,14},{14,6},{15,13},{13,15},... | collective-permute-start | bytes 589832 | tf_op jit(solution)/shard_map/ppermute | solution.py:415
  47.5 2.8 %collective-permute-start.4 = (f32[3,8,8,128]{3,2,1,0:T(8,128)S(1)}, f32[3,8,8,128]{3,2,1,0:T(8,128)S(1)}, u32[]{:S(2)}, u32[]{:S(2)}) collective-permute-start(f32[3,8,8,128]{3,2,1,0:T(8,128)S(1)} %get-tuple-element.37), channel_id=1, source_target_pairs={{0,1},{1,0},{2,3},{3,2},{4,5},{5,4},{6,7},{7,6},{8,9},{9,8},{10,11... | collective-permute-start | bytes 294920 | tf_op jit(solution)/shard_map/ppermute | solution.py:408
  50.4 7.3 %collective-permute-start.5 = (f32[2,3,8,8,128]{4,3,2,1,0:T(8,128)S(1)}, f32[2,3,8,8,128]{4,3,2,1,0:T(8,128)S(1)}, u32[]{:S(2)}, u32[]{:S(2)}) collective-permute-start(f32[2,3,8,8,128]{4,3,2,1,0:T(8,128)S(1)} %get-tuple-element.39.own_ref.refs_4_), channel_id=1, source_target_pairs={{0,2},{2,0},{3,5},{5,3},{4,6},{6,4},{7,15},{15,7},{14,12},{12,14},... | collective-permute-start | bytes 589832 | tf_op jit(solution)/shard_map/ppermute | solution.py:414
  50.5 7.2 %collective-permute-start.6 = (f32[2,3,8,8,128]{4,3,2,1,0:T(8,128)S(1)}, f32[2,3,8,8,128]{4,3,2,1,0:T(8,128)S(1)}, u32[]{:S(2)}, u32[]{:S(2)}) collective-permute-start(f32[2,3,8,8,128]{4,3,2,1,0:T(8,128)S(1)} %get-tuple-element.39.own_ref.refs_4_), channel_id=1, source_target_pairs={{1,3},{3,1},{2,4},{4,2},{5,7},{7,5},{6,14},{14,6},{15,13},{13,15},... | collective-permute-start | bytes 589832 | tf_op jit(solution)/shard_map/ppermute | solution.py:415
  59.4 3.2 %copy-start = (f32[2,16,3,1024]{3,1,2,0:T(8,128)S(1)}, f32[2,16,3,1024]{3,1,2,0:T(8,128)}, u32[]{:S(2)}) copy-start(f32[2,16,3,1024]{3,1,2,0:T(8,128)} %param.4) | copy-start | bytes 1179652
  59.4 2.3 %collective-permute-start.7 = (f32[3,8,8,128]{3,2,1,0:T(8,128)S(1)}, f32[3,8,8,128]{3,2,1,0:T(8,128)S(1)}, u32[]{:S(2)}, u32[]{:S(2)}) collective-permute-start(f32[3,8,8,128]{3,2,1,0:T(8,128)S(1)} %get-tuple-element.42), channel_id=1, source_target_pairs={{0,1},{1,0},{2,3},{3,2},{4,5},{5,4},{6,7},{7,6},{8,9},{9,8},{10,11... | collective-permute-start | bytes 294920 | tf_op jit(solution)/shard_map/ppermute | solution.py:408
  61.9 0.7 copy-start.1
  61.9 7.1 %collective-permute-start.8 = (f32[2,3,8,8,128]{4,3,2,1,0:T(8,128)S(1)}, f32[2,3,8,8,128]{4,3,2,1,0:T(8,128)S(1)}, u32[]{:S(2)}, u32[]{:S(2)}) collective-permute-start(f32[2,3,8,8,128]{4,3,2,1,0:T(8,128)S(1)} %get-tuple-element.44.own_ref.refs_5_), channel_id=1, source_target_pairs={{0,2},{2,0},{3,5},{5,3},{4,6},{6,4},{7,15},{15,7},{14,12},{12,14},... | collective-permute-start | bytes 589832 | tf_op jit(solution)/shard_map/ppermute | solution.py:414
  62.0 7.0 %collective-permute-start.9 = (f32[2,3,8,8,128]{4,3,2,1,0:T(8,128)S(1)}, f32[2,3,8,8,128]{4,3,2,1,0:T(8,128)S(1)}, u32[]{:S(2)}, u32[]{:S(2)}) collective-permute-start(f32[2,3,8,8,128]{4,3,2,1,0:T(8,128)S(1)} %get-tuple-element.44.own_ref.refs_5_), channel_id=1, source_target_pairs={{1,3},{3,1},{2,4},{4,2},{5,7},{7,5},{6,14},{14,6},{15,13},{13,15},... | collective-permute-start | bytes 589832 | tf_op jit(solution)/shard_map/ppermute | solution.py:415
  70.8 2.5 %collective-permute-start.10 = (f32[3,8,8,128]{3,2,1,0:T(8,128)S(1)}, f32[3,8,8,128]{3,2,1,0:T(8,128)S(1)}, u32[]{:S(2)}, u32[]{:S(2)}) collective-permute-start(f32[3,8,8,128]{3,2,1,0:T(8,128)S(1)} %get-tuple-element.47), channel_id=1, source_target_pairs={{0,1},{1,0},{2,3},{3,2},{4,5},{5,4},{6,7},{7,6},{8,9},{9,8},{10,11... | collective-permute-start | bytes 294920 | tf_op jit(solution)/shard_map/ppermute | solution.py:426
  73.7 1.4 %collective-permute-start.11 = (f32[256,128]{1,0:T(8,128)S(1)}, f32[256,128]{1,0:T(8,128)S(1)}, u32[]{:S(2)}, u32[]{:S(2)}) collective-permute-start(f32[256,128]{1,0:T(8,128)S(1)} %get-tuple-element.49), channel_id=1, source_target_pairs={{0,1},{1,0},{2,3},{3,2},{4,5},{5,4},{6,7},{7,6},{8,9},{9,8},{10,11... | collective-permute-start | bytes 393224 | tf_op jit(solution)/shard_map/ppermute | solution.py:440

commit v4 on v3

--- a/solution.py
+++ b/solution.py
@@ -55,7 +55,7 @@
     return pltpu.with_memory_space_constraint(value, pltpu.VMEM)
 
 
-def call(kernel, outs, scalars, *operands, far=(), far_out=(), scratch=()):
+def call(kernel, outs, scalars, *operands, far=(), scratch=()):
     vmem = pl.BlockSpec(memory_space=pltpu.VMEM)
     hbm = pl.BlockSpec(memory_space=pl.ANY)
     smem = pl.BlockSpec(memory_space=pltpu.SMEM)
@@ -64,7 +64,7 @@
         kernel,
         out_shape=outs,
         in_specs=[smem] * len(scalars) + [hbm] * len(far) + [vmem] * len(operands),
-        out_specs=[hbm if i in far_out else vmem for i in range(len(outs))],
+        out_specs=[vmem] * len(outs),
         scratch_shapes=list(scratch),
     )(*scalars, *far, *map(near, operands))
     return results if len(outs) > 1 else results[0]
@@ -144,26 +144,45 @@
 
 
 def scan_pairs(u, square, pair):
-    factor = square
-    for groups in (1, 2, 4, 8):
-        u = u + jnp.where(pair < 16 - groups, factor, 0.0) * later(u, groups)
-        factor = factor * factor
+    for groups in (1, 4):
+        factor = square
+        total = u
+        for times in (1, 2, 3):
+            back = times * groups
+            total = total + jnp.where(pair < 16 - back, factor, 0.0) * later(u, back)
+            factor = factor * square
+        u, square = total, factor
     return u
 
 
-def chain_here(c0, c1, decay, pair, first_ref, second_ref, carry_ref, at):
-    square = decay * decay
-    value = scan_pairs(c0 + decay * c1, square, pair)
-    first_ref[at] = value
-    second_ref[at] = c1 + decay * jnp.where(pair < 15, later(value, 1), 0.0)
-    spread = jnp.where(pair < 1, value, 0.0)
-    for groups in (1, 2, 4, 8):
-        spread = spread + pltpu.roll(spread, 8 * groups, spread.ndim - 1)
-    carry_ref[at] = spread
+def chain_here(terms, first_ref, second_ref, carry_ref):
+    pair = iota(1) // 8
+    for f in range(FIELDS):
+        for col in range(LONS):
+            c0, c1, decay = terms(f, col)
+            value = scan_pairs(c0 + decay * c1, decay * decay, pair)
+            first_ref[f, col] = value
+            second_ref[f, col] = c1 + decay * jnp.where(pair < 15, later(value, 1), 0.0)
+    source = lax.broadcasted_iota(jnp.int32, (128, 128), 0)
+    target = lax.broadcasted_iota(jnp.int32, (128, 128), 1)
+    spread = (source == target % 8).astype(jnp.float32)
+    values = first_ref[...].reshape(FIELDS * LONS * 8, 128)
+    carried = jnp.dot(
+        values, spread, precision=lax.Precision.HIGHEST, preferred_element_type=jnp.float32
+    )
+    carry_ref[...] = carried.reshape(FIELDS, LONS, 8, 128)
+
+
+def powers(square, exponent):
+    power = jnp.where((exponent & 1) != 0, square, 1.0)
+    for bit in (2, 4, 8, 16):
+        square = square * square
+        power = power * jnp.where((exponent & bit) != 0, square, 1.0)
+    return power
 
 
 def open_kernel(
-    core_ref, mine_ref, other_ref, first_ref, second_ref, carry_ref, decay_ref, power_ref, turn_ref
+    core_ref, mine_ref, other_ref, first_ref, second_ref, carry_ref, decay_ref, power_ref, turn_ref, terms_ref
 ):
     low = core_ref[0] == 0
     lane = iota(1)
@@ -188,15 +207,18 @@
             )
             for f in range(FIELDS):
                 decay = decays[f]
-                c0 = turned[at + 8 * f : at + 8 * f + 8, :]
-                c1 = turned[at + 24 + 8 * f : at + 32 + 8 * f, :]
                 decay_ref[f, col] = decay
-                chain_here(c0, c1, decay, pair, first_ref, second_ref, carry_ref, (f, col))
-                power = decay * decay
-                for groups in (1, 2, 4, 8):
-                    power = power * jnp.where(pair < 16 - groups, later(power, groups), 1.0)
-                power_ref[0, f, col] = power
-                power_ref[1, f, col] = decay * jnp.where(pair < 15, later(power, 1), 1.0)
+                terms_ref[0, f, col] = turned[at + 8 * f : at + 8 * f + 8, :]
+                terms_ref[1, f, col] = turned[at + 24 + 8 * f : at + 32 + 8 * f, :]
+                square = decay * decay
+                power_ref[0, f, col] = powers(square, 16 - pair)
+                power_ref[1, f, col] = decay * powers(square, 15 - pair)
+    chain_here(
+        lambda f, col: (terms_ref[0, f, col], terms_ref[1, f, col], decay_ref[f, col]),
+        first_ref,
+        second_ref,
+        carry_ref,
+    )
 
 
 def close_kernel(core_ref, first_ref, second_ref, carry_ref, power_ref, zero_ref, above_ref):
@@ -212,69 +234,96 @@
 
 
 def fine_kernel(
-    odd_ref, own_ref, even_ref, odd_side_ref, decay_ref, first_ref, second_ref, carry_ref, state_ref
+    odd_ref, own_ref, one_ref, two_ref, decay_ref, first_ref, second_ref, carry_ref, state_ref
 ):
     odd = odd_ref[0] == 1
-    row = iota(0)[None]
-    lane = iota(1)[None]
+    lane = iota(1)
     band = lane % 8
-    pair = lane // 8
-    at_top = row == 0
-    at_end = row == 7
-    not_first = band > 0
-    not_last = band < 7
-
-    def next_row(v):
-        inner = pltpu.roll(v, 7, 1)
-        edge = jnp.where(not_last, pltpu.roll(inner, 127, 2), 0.0)
-        return jnp.where(at_end, edge, inner)
-
-    def last_row(v):
-        inner = pltpu.roll(v, 1, 1)
-        edge = jnp.where(not_first, pltpu.roll(inner, 1, 2), 0.0)
-        return jnp.where(at_top, edge, inner)
-
-    corrections = []
+    width = 3 * LONS
+
+    def slot(j, f, col):
+        return 24 * ((j * FIELDS + f) * width + col)
+
+    def put(j, f, col, value):
+        at = slot(j, f, col) + 8
+        state_ref[at : at + 8, :] = value
+
+    def here(j, f, col):
+        at = slot(j, f, col) + 8
+        return state_ref[at : at + 8, :]
+
+    def rows(j, f, col):
+        at = slot(j, f, col) + 8
+        return state_ref[at + 1 : at + 9, :], state_ref[at - 1 : at + 7, :]
+
+    def edges(j, f, low, high):
+        for col in range(low, high, 8):
+            at = slot(j, f, min(col, width - 8))
+            first = pltpu.roll(state_ref[pl.ds(at + 8, 8, stride=24), :], 127, 1)
+            last = pltpu.roll(state_ref[pl.ds(at + 15, 8, stride=24), :], 1, 1)
+            state_ref[pl.ds(at + 16, 8, stride=24), :] = jnp.where(band < 7, first, 0.0)
+            state_ref[pl.ds(at + 7, 8, stride=24), :] = jnp.where(band > 0, last, 0.0)
+
     for j in range(2):
         for f in range(FIELDS):
-            one, two = even_ref[j, f], odd_side_ref[j, f]
-            state_ref[f, 0:8] = jnp.where(odd, one, two)
-            state_ref[f, 8:16] = own_ref[j, f]
-            state_ref[f, 16:24] = jnp.where(odd, two, one)
-        p, q, r = state_ref[0], state_ref[1], state_ref[2]
-        keep = 1.0 / diffusion - 4.0
-        wave = 0.5 * wave_coef / diffusion
-        wave_new = 0.5 * wave_coef
-        turn = coriolis / diffusion
-        for step in range(STEPS):
-            n = p.shape[0]
-            pc, rc = p[1 : n - 1], r[1 : n - 1]
-            side = wave * rc
-            p1 = (
-                (keep * pc + (p[: n - 2] + p[2:]))
-                + wave * (q[2:] - q[: n - 2])
-                + (next_row(pc + side) + last_row(pc - side))
+            for at in range(LONS):
+                one, two = one_ref[j, f, at], two_ref[j, f, at]
+                put(j, f, at, jnp.where(odd, one, two))
+                put(j, f, LONS + at, own_ref[j, f, at])
+                put(j, f, 2 * LONS + at, jnp.where(odd, two, one))
+            edges(j, f, 0, width)
+
+    keep = 1.0 / diffusion - 4.0
+    wave = 0.5 * wave_coef / diffusion
+    wave_new = 0.5 * wave_coef
+    turn = coriolis / diffusion
+    unit = diffusion**STEPS
+    result = {}
+    for step in range(STEPS):
+        low, high = 2 * step + 1, width - 2 * step - 1
+        for j in range(2):
+            p = {col: here(j, 0, col) for col in (low - 1, low)}
+            q = {col: here(j, 1, col) for col in (low - 1, low)}
+            for col in range(low, high):
+                p[col + 1], q[col + 1] = here(j, 0, col + 1), here(j, 1, col + 1)
+                p_next, p_last = rows(j, 0, col)
+                r_next, r_last = rows(j, 2, col)
+                p1 = ((keep * p[col] + (p[col - 1] + p[col + 1])) + (p_next + p_last)) + wave * (
+                    (q[col + 1] - q[col - 1]) + (r_next - r_last)
+                )
+                put(j, 0, col, p1)
+            edges(j, 0, low, high)
+        low, high = low + 1, high - 1
+        for j in range(2):
+            p, q, r = (
+                {col: here(j, f, col) for col in (low - 1, low)} for f in range(FIELDS)
             )
-            qc, rc, pc = q[2 : n - 2], r[2 : n - 2], p1[1 : n - 3]
-            push = wave_new * p1
-            side = push[1 : n - 3]
-            q1 = (
-                (keep * qc + (q[1 : n - 3] + q[3 : n - 1]))
-                + ((push[2:] - push[: n - 4]) + turn * rc)
-                + (next_row(qc) + last_row(qc))
-            )
-            r1 = (
-                (keep * rc + (r[1 : n - 3] + r[3 : n - 1]))
-                - turn * qc
-                + (next_row(rc + side) + last_row(rc - side))
-            )
-            p, q, r = pc, q1, r1
-        unit = diffusion**STEPS
-        corrections.append([unit * v - decay_ref[f] * own_ref[j, f] for f, v in enumerate((p, q, r))])
-    for f in range(FIELDS):
-        chain_here(
-            corrections[0][f], corrections[1][f], decay_ref[f], pair, first_ref, second_ref, carry_ref, f
-        )
+            for col in range(low, high):
+                p[col + 1], q[col + 1], r[col + 1] = (here(j, f, col + 1) for f in range(FIELDS))
+                p_next, p_last = rows(j, 0, col)
+                q_next, q_last = rows(j, 1, col)
+                r_next, r_last = rows(j, 2, col)
+                q1 = (
+                    (keep * q[col] + (q[col - 1] + q[col + 1])) + (q_next + q_last)
+                ) + (wave_new * (p[col + 1] - p[col - 1]) + turn * r[col])
+                r1 = (
+                    (keep * r[col] + (r[col - 1] + r[col + 1])) + (r_next + r_last)
+                ) + (wave_new * (p_next - p_last) - turn * q[col])
+                if step < STEPS - 1:
+                    put(j, 1, col, q1)
+                    put(j, 2, col, r1)
+                else:
+                    for f, value in enumerate((p[col], q1, r1)):
+                        result[j, f, col - LONS] = value
+            if step < STEPS - 1:
+                edges(j, 1, low, high)
+                edges(j, 2, low, high)
+
+    def terms(f, col):
+        decay = decay_ref[f, col]
+        return *(unit * result[j, f, col] - decay * own_ref[j, f, col] for j in range(2)), decay
+
+    chain_here(terms, first_ref, second_ref, carry_ref)
 
 
 def finish_kernel(core_ref, *refs):
@@ -337,7 +386,7 @@
     out_ref[256:512, :] = jnp.where(counted, total, jnp.where(low, got, mine))
 
 
-def unpack_kernel(in_ref, out_ref, misfit_ref, changes_ref, rows_ref, stage_ref, sems):
+def unpack_kernel(in_ref, out_ref, misfit_ref, changes_ref, rows_ref):
     sums = [in_ref[8 * v : 8 * v + 8, :] for v in range(64)]
     while len(sums) > 1:
         sums = [a + b for a, b in zip(sums[::2], sums[1::2])]
@@ -345,7 +394,6 @@
     misfit_ref[...] = total[0:1, 3:4]
     changes_ref[...] = (total / (pltpu.roll(total, 124, 1) + epsilon))[0:1, 0:ITERS]
     second = (lax.broadcasted_iota(jnp.int32, (128, 128), 0) & 7) >= 4
-    copies = []
     for b in range(8):
         for i in range(16):
             at = 4 * chip_of(16 * b + i)
@@ -357,15 +405,7 @@
         for j in range(2):
             for f in range(FIELDS):
                 at = 24 * j + 8 * f
-                stage_ref[b, j, f] = turned[at : at + 8, :]
-        copies.append(
-            pltpu.make_async_copy(
-                stage_ref.at[b], out_ref.at[:, :, :, 128 * b : 128 * b + 128], sems.at[b]
-            )
-        )
-        copies[-1].start()
-    for copy in copies:
-        copy.wait()
+                out_ref[j, f, :, 128 * b : 128 * b + 128] = turned[at : at + 8, :]
 
 
 def per_device(departure, obs_weight, obs_block, coarse_decay):
@@ -401,7 +441,7 @@
     both = shape(2, FIELDS, LONS, 8, 128)
     square = pltpu.VMEM((128, 128), jnp.float32)
     first, second, carry, decay, power = call(
-        open_kernel, (field, field, field, field, both), (core_arg,), got, other, scratch=[square]
+        open_kernel, (field, field, field, field, both), (core_arg,), got, other, scratch=[square, pltpu.VMEM((2, FIELDS, LONS, 8, 128), jnp.float32)]
     )
     zeros, aboves = [], []
     for _ in range(ITERS):
@@ -421,7 +461,7 @@
             side_even,
             side_odd,
             decay,
-            scratch=[pltpu.VMEM((FIELDS, 24, 8, 128), jnp.float32)],
+            scratch=[pltpu.VMEM((2 * FIELDS * 3 * LONS * 24, 128), jnp.float32)],
         )
     carry = lax.ppermute(carry, "c", SIBLING)
     mine, away = call(
@@ -449,12 +489,7 @@
         ),
         (),
         home,
-        far_out=(0,),
-        scratch=[
-            square,
-            pltpu.VMEM((8, 2, FIELDS, 8, 128), jnp.float32),
-            pltpu.SemaphoreType.DMA((8,)),
-        ],
+        scratch=[square],
     )
     return adjoint, misfit.reshape(()), changes.reshape(ITERS)
 

time: 96.7 us -> 94.6 us (0.978)
  Pallas kernels: 11 us -> 9 us
    pallas_call x11, Pallas kernels: 11 us -> 9 us  [call(): pl.pallas_call(kernel, out_shape=outs, in_specs=[smem] * len(scalars) + [...]
where the time goes in v4:
time: 94.6 us; the launch traced here: 94.4 us
  blocking collectives  49 us (52%)
  waiting for transfers between devices  25.6 us (27%)
  starting transfers between devices  9.44 us (10%)
  Pallas kernels  9 us (10%)
    all_to_all x1, blocking collectives, per_device(): lax.all_to_all(sent.reshape(CHIPS, 4, 128), ZYX, 0, 0).reshape(512, 128)  29.5 us
    ppermute x3, waiting for transfers between devices, per_device(): side_even = lax.ppermute(above, ALL, swap_pairs(0))  19.7 us
    all_to_all x1, blocking collectives, per_device(): lax.all_to_all(back.reshape(CHIPS, 4, 128), ZYX, 0, 0).reshape(512, 128)  19.5 us
    pallas_call x11, Pallas kernels, call(): pl.pallas_call(kernel, out_shape=outs, in_specs=[smem] * len(scalars) + [...  9 us
    ppermute x4, starting transfers between devices, per_device(): carry = lax.ppermute(carry, 'c', SIBLING)  5.3 us
    ppermute x4, waiting for transfers between devices, per_device(): carry = lax.ppermute(carry, 'c', SIBLING)  3.77 us
    ppermute x1, starting transfers between devices, per_device(): other = lax.ppermute(got, 'c', SIBLING)  2.69 us
  transfers between devices with their start and end apart: 12, of which 9 were waited for; matrix products, arithmetic and copies ran while one was open for 0% of the time, Pallas kernels for 0%

profile of v4, /device:TPU:1, one launch (start us, length us, event | category | flops | bytes accessed | tf_op | source)
XLA Modules:
  0.0 94.4 jit_solution(6518380529621885033)
XLA Ops:
  0.6 2.3 %shard_map.67 = f32[512,128]{1,0:T(8,128)S(1)} custom-call(s32[1]{0:T(128)} %bitcast.1.place_ref, f32[2,3,16,1024]{3,2,1,0:T(8,128)} %bitcast.17, f32[2,16]{1,0:T(2,128)} %weight_ref.1, s32[2,16]{1,0:T(2,128)} %block_ref.1, f32[3,8,1024]{2,1,0:T(8,128)} %decay_ref.1), custom_call_target="tpu_custom_call" | custom-call | tf_op jit(solution)/shard_map/pallas_call | solution.py:63
  3.0 29.5 %all_to_all.10 = f32[128,4,128]{2,1,0:T(4,128)S(1)} all-to-all(f32[128,4,128]{2,1,0:T(4,128)S(1)} %bitcast.16), channel_id=1, replica_groups=mesh['z'=8,'y'=4,'x'=4,'c'=2] {'z','y','x'}, dimensions={0} | all-to-all | bytes 524288 | tf_op jit(solution)/shard_map/all_to_all | solution.py:437
  32.5 2.7 %collective-permute-start = (f32[512,128]{1,0:T(8,128)S(1)}, f32[512,128]{1,0:T(8,128)S(1)}, u32[]{:S(2)}, u32[]{:S(2)}) collective-permute-start(f32[512,128]{1,0:T(8,128)S(1)} %bitcast.12), channel_id=1, source_target_pairs={{0,1},{1,0},{2,3},{3,2},{4,5},{5,4},{6,7},{7,6},{8,9},{9,8},{10,11... | collective-permute-start | bytes 786440 | tf_op jit(solution)/shard_map/ppermute | solution.py:438
  35.2 1.2 %collective-permute-done.other_ref = f32[512,128]{1,0:T(8,128)S(1)} collective-permute-done((f32[512,128]{1,0:T(8,128)S(1)}, f32[512,128]{1,0:T(8,128)S(1)}, u32[]{:S(2)}, u32[]{:S(2)}) %collective-permute-start) | collective-permute-done | bytes 262176 | tf_op jit(solution)/shard_map/ppermute | solution.py:438
  36.4 0.6 shard_map.68
  37.0 0.5 collective-permute-start.1
  37.5 0.9 %collective-permute-done.1.carry_ref = f32[3,8,8,128]{3,2,1,0:T(8,128)S(1)} collective-permute-done((f32[3,8,8,128]{3,2,1,0:T(8,128)S(1)}, f32[3,8,8,128]{3,2,1,0:T(8,128)S(1)}, u32[]{:S(2)}, u32[]{:S(2)}) %collective-permute-start.1) | collective-permute-done | bytes 98336 | tf_op jit(solution)/shard_map/ppermute | solution.py:448
  39.0 6.4 %collective-permute-done.2.one_ref = f32[2,3,8,8,128]{4,3,2,1,0:T(8,128)S(1)} collective-permute-done((f32[2,3,8,8,128]{4,3,2,1,0:T(8,128)S(1)}, f32[2,3,8,8,128]{4,3,2,1,0:T(8,128)S(1)}, u32[]{:S(2)}, u32[]{:S(2)}) %collective-permute-start.2) | collective-permute-done | bytes 196640 | tf_op jit(solution)/shard_map/ppermute | solution.py:454
  45.4 1.4 %shard_map.70 = (f32[3,8,8,128]{3,2,1,0:T(8,128)S(1)}, f32[3,8,8,128]{3,2,1,0:T(8,128)S(1)}, f32[3,8,8,128]{3,2,1,0:T(8,128)S(1)}) custom-call(s32[1]{0:T(128)} %bitcast.5.odd_ref, f32[2,3,8,8,128]{4,3,2,1,0:T(8,128)S(1)} %get-tuple-element.33.own_ref.refs_3_, f32[2,3,8,8,128]{4,3,2,1,0:T(8,128)S(1)} %collective-permute-done.2.one_ref, ...), custom_call_target="tpu_custom_call" | custom-call | tf_op jit(solution)/shard_map/pallas_call | solution.py:63
  46.8 1.9 %collective-permute-start.4 = (f32[3,8,8,128]{3,2,1,0:T(8,128)S(1)}, f32[3,8,8,128]{3,2,1,0:T(8,128)S(1)}, u32[]{:S(2)}, u32[]{:S(2)}) collective-permute-start(f32[3,8,8,128]{3,2,1,0:T(8,128)S(1)} %get-tuple-element.37), channel_id=1, source_target_pairs={{0,1},{1,0},{2,3},{3,2},{4,5},{5,4},{6,7},{7,6},{8,9},{9,8},{10,11... | collective-permute-start | bytes 294920 | tf_op jit(solution)/shard_map/ppermute | solution.py:448
  48.6 0.9 %collective-permute-done.4.carry_ref = f32[3,8,8,128]{3,2,1,0:T(8,128)S(1)} collective-permute-done((f32[3,8,8,128]{3,2,1,0:T(8,128)S(1)}, f32[3,8,8,128]{3,2,1,0:T(8,128)S(1)}, u32[]{:S(2)}, u32[]{:S(2)}) %collective-permute-start.4) | collective-permute-done | bytes 98336 | tf_op jit(solution)/shard_map/ppermute | solution.py:448
  49.9 7.1 %collective-permute-done.5.one_ref = f32[2,3,8,8,128]{4,3,2,1,0:T(8,128)S(1)} collective-permute-done((f32[2,3,8,8,128]{4,3,2,1,0:T(8,128)S(1)}, f32[2,3,8,8,128]{4,3,2,1,0:T(8,128)S(1)}, u32[]{:S(2)}, u32[]{:S(2)}) %collective-permute-start.5) | collective-permute-done | bytes 196640 | tf_op jit(solution)/shard_map/ppermute | solution.py:454
  57.0 1.4 %shard_map.72 = (f32[3,8,8,128]{3,2,1,0:T(8,128)S(1)}, f32[3,8,8,128]{3,2,1,0:T(8,128)S(1)}, f32[3,8,8,128]{3,2,1,0:T(8,128)S(1)}) custom-call(s32[1]{0:T(128)} %bitcast.5.odd_ref, f32[2,3,8,8,128]{4,3,2,1,0:T(8,128)S(1)} %get-tuple-element.39.own_ref.refs_4_, f32[2,3,8,8,128]{4,3,2,1,0:T(8,128)S(1)} %collective-permute-done.5.one_ref, ...), custom_call_target="tpu_custom_call" | custom-call | tf_op jit(solution)/shard_map/pallas_call | solution.py:63
  58.4 1.4 %collective-permute-start.7 = (f32[3,8,8,128]{3,2,1,0:T(8,128)S(1)}, f32[3,8,8,128]{3,2,1,0:T(8,128)S(1)}, u32[]{:S(2)}, u32[]{:S(2)}) collective-permute-start(f32[3,8,8,128]{3,2,1,0:T(8,128)S(1)} %get-tuple-element.42), channel_id=1, source_target_pairs={{0,1},{1,0},{2,3},{3,2},{4,5},{5,4},{6,7},{7,6},{8,9},{9,8},{10,11... | collective-permute-start | bytes 294920 | tf_op jit(solution)/shard_map/ppermute | solution.py:448
  59.8 0.9 collective-permute-done.7.carry_ref
  61.7 6.2 %collective-permute-done.8.one_ref = f32[2,3,8,8,128]{4,3,2,1,0:T(8,128)S(1)} collective-permute-done((f32[2,3,8,8,128]{4,3,2,1,0:T(8,128)S(1)}, f32[2,3,8,8,128]{4,3,2,1,0:T(8,128)S(1)}, u32[]{:S(2)}, u32[]{:S(2)}) %collective-permute-start.8) | collective-permute-done | bytes 196640 | tf_op jit(solution)/shard_map/ppermute | solution.py:454
  68.0 1.4 %shard_map.74 = (f32[3,8,8,128]{3,2,1,0:T(8,128)S(1)}, f32[3,8,8,128]{3,2,1,0:T(8,128)S(1)}, f32[3,8,8,128]{3,2,1,0:T(8,128)S(1)}) custom-call(s32[1]{0:T(128)} %bitcast.5.odd_ref, f32[2,3,8,8,128]{4,3,2,1,0:T(8,128)S(1)} %get-tuple-element.44.own_ref.refs_5_, f32[2,3,8,8,128]{4,3,2,1,0:T(8,128)S(1)} %collective-permute-done.8.one_ref, ...), custom_call_target="tpu_custom_call" | custom-call | tf_op jit(solution)/shard_map/pallas_call | solution.py:63
  69.3 1.6 %collective-permute-start.10 = (f32[3,8,8,128]{3,2,1,0:T(8,128)S(1)}, f32[3,8,8,128]{3,2,1,0:T(8,128)S(1)}, u32[]{:S(2)}, u32[]{:S(2)}) collective-permute-start(f32[3,8,8,128]{3,2,1,0:T(8,128)S(1)} %get-tuple-element.47), channel_id=1, source_target_pairs={{0,1},{1,0},{2,3},{3,2},{4,5},{5,4},{6,7},{7,6},{8,9},{9,8},{10,11... | collective-permute-start | bytes 294920 | tf_op jit(solution)/shard_map/ppermute | solution.py:466
  70.9 0.9 collective-permute-done.10.refs_8_
  71.9 0.4 shard_map.75
  72.3 0.4 collective-permute-start.11
  72.8 1.0 %collective-permute-done.11.got_ref = f32[256,128]{1,0:T(8,128)S(1)} collective-permute-done((f32[256,128]{1,0:T(8,128)S(1)}, f32[256,128]{1,0:T(8,128)S(1)}, u32[]{:S(2)}, u32[]{:S(2)}) %collective-permute-start.11) | collective-permute-done | bytes 131104 | tf_op jit(solution)/shard_map/ppermute | solution.py:480
  73.8 19.5 %all_to_all.11 = f32[128,4,128]{2,1,0:T(4,128)S(1)} all-to-all(f32[128,4,128]{2,1,0:T(4,128)S(1)} %bitcast.14), channel_id=1, replica_groups=mesh['z'=8,'y'=4,'x'=4,'c'=2] {'z','y','x'}, dimensions={0} | all-to-all | bytes 524288 | tf_op jit(solution)/shard_map/all_to_all | solution.py:482
  93.3 1.1 %shard_map.77 = (f32[2,3,8,1024]{3,2,1,0:T(8,128)}, f32[1,1]{1,0:T(1,128)}, f32[1,3]{1,0:T(1,128)}) custom-call(f32[512,128]{1,0:T(8,128)S(1)} %bitcast.15), custom_call_target="tpu_custom_call" | custom-call | tf_op jit(solution)/shard_map/pallas_call | solution.py:63
  (21 shorter events, 1.9 us)
Async XLA Ops:
  32.5 3.8 %collective-permute-start = (f32[512,128]{1,0:T(8,128)S(1)}, f32[512,128]{1,0:T(8,128)S(1)}, u32[]{:S(2)}, u32[]{:S(2)}) collective-permute-start(f32[512,128]{1,0:T(8,128)S(1)} %bitcast.12), channel_id=1, source_target_pairs={{0,1},{1,0},{2,3},{3,2},{4,5},{5,4},{6,7},{7,6},{8,9},{9,8},{10,11... | collective-permute-start | bytes 786440 | tf_op jit(solution)/shard_map/ppermute | solution.py:438
  37.0 1.4 %collective-permute-start.1 = (f32[3,8,8,128]{3,2,1,0:T(8,128)S(1)}, f32[3,8,8,128]{3,2,1,0:T(8,128)S(1)}, u32[]{:S(2)}, u32[]{:S(2)}) collective-permute-start(f32[3,8,8,128]{3,2,1,0:T(8,128)S(1)} %get-tuple-element.30), channel_id=1, source_target_pairs={{0,1},{1,0},{2,3},{3,2},{4,5},{5,4},{6,7},{7,6},{8,9},{9,8},{10,11... | collective-permute-start | bytes 294920 | tf_op jit(solution)/shard_map/ppermute | solution.py:448
  38.5 6.8 %collective-permute-start.2 = (f32[2,3,8,8,128]{4,3,2,1,0:T(8,128)S(1)}, f32[2,3,8,8,128]{4,3,2,1,0:T(8,128)S(1)}, u32[]{:S(2)}, u32[]{:S(2)}) collective-permute-start(f32[2,3,8,8,128]{4,3,2,1,0:T(8,128)S(1)} %get-tuple-element.33.own_ref.refs_3_), channel_id=1, source_target_pairs={{0,2},{2,0},{3,5},{5,3},{4,6},{6,4},{7,15},{15,7},{14,12},{12,14},... | collective-permute-start | bytes 589832 | tf_op jit(solution)/shard_map/ppermute | solution.py:454
  38.6 6.7 %collective-permute-start.3 = (f32[2,3,8,8,128]{4,3,2,1,0:T(8,128)S(1)}, f32[2,3,8,8,128]{4,3,2,1,0:T(8,128)S(1)}, u32[]{:S(2)}, u32[]{:S(2)}) collective-permute-start(f32[2,3,8,8,128]{4,3,2,1,0:T(8,128)S(1)} %get-tuple-element.33.own_ref.refs_3_), channel_id=1, source_target_pairs={{1,3},{3,1},{2,4},{4,2},{5,7},{7,5},{6,14},{14,6},{15,13},{13,15},... | collective-permute-start | bytes 589832 | tf_op jit(solution)/shard_map/ppermute | solution.py:455
  46.8 2.8 %collective-permute-start.4 = (f32[3,8,8,128]{3,2,1,0:T(8,128)S(1)}, f32[3,8,8,128]{3,2,1,0:T(8,128)S(1)}, u32[]{:S(2)}, u32[]{:S(2)}) collective-permute-start(f32[3,8,8,128]{3,2,1,0:T(8,128)S(1)} %get-tuple-element.37), channel_id=1, source_target_pairs={{0,1},{1,0},{2,3},{3,2},{4,5},{5,4},{6,7},{7,6},{8,9},{9,8},{10,11... | collective-permute-start | bytes 294920 | tf_op jit(solution)/shard_map/ppermute | solution.py:448
  49.7 7.3 %collective-permute-start.5 = (f32[2,3,8,8,128]{4,3,2,1,0:T(8,128)S(1)}, f32[2,3,8,8,128]{4,3,2,1,0:T(8,128)S(1)}, u32[]{:S(2)}, u32[]{:S(2)}) collective-permute-start(f32[2,3,8,8,128]{4,3,2,1,0:T(8,128)S(1)} %get-tuple-element.39.own_ref.refs_4_), channel_id=1, source_target_pairs={{0,2},{2,0},{3,5},{5,3},{4,6},{6,4},{7,15},{15,7},{14,12},{12,14},... | collective-permute-start | bytes 589832 | tf_op jit(solution)/shard_map/ppermute | solution.py:454
  49.8 7.2 %collective-permute-start.6 = (f32[2,3,8,8,128]{4,3,2,1,0:T(8,128)S(1)}, f32[2,3,8,8,128]{4,3,2,1,0:T(8,128)S(1)}, u32[]{:S(2)}, u32[]{:S(2)}) collective-permute-start(f32[2,3,8,8,128]{4,3,2,1,0:T(8,128)S(1)} %get-tuple-element.39.own_ref.refs_4_), channel_id=1, source_target_pairs={{1,3},{3,1},{2,4},{4,2},{5,7},{7,5},{6,14},{14,6},{15,13},{13,15},... | collective-permute-start | bytes 589832 | tf_op jit(solution)/shard_map/ppermute | solution.py:455
  58.4 3.2 %copy-start = (f32[2,16,3,1024]{3,1,2,0:T(8,128)S(1)}, f32[2,16,3,1024]{3,1,2,0:T(8,128)}, u32[]{:S(2)}) copy-start(f32[2,16,3,1024]{3,1,2,0:T(8,128)} %param.4) | copy-start | bytes 1179652
  58.4 2.3 %collective-permute-start.7 = (f32[3,8,8,128]{3,2,1,0:T(8,128)S(1)}, f32[3,8,8,128]{3,2,1,0:T(8,128)S(1)}, u32[]{:S(2)}, u32[]{:S(2)}) collective-permute-start(f32[3,8,8,128]{3,2,1,0:T(8,128)S(1)} %get-tuple-element.42), channel_id=1, source_target_pairs={{0,1},{1,0},{2,3},{3,2},{4,5},{5,4},{6,7},{7,6},{8,9},{9,8},{10,11... | collective-permute-start | bytes 294920 | tf_op jit(solution)/shard_map/ppermute | solution.py:448
  60.8 0.7 copy-start.1
  60.8 7.1 %collective-permute-start.8 = (f32[2,3,8,8,128]{4,3,2,1,0:T(8,128)S(1)}, f32[2,3,8,8,128]{4,3,2,1,0:T(8,128)S(1)}, u32[]{:S(2)}, u32[]{:S(2)}) collective-permute-start(f32[2,3,8,8,128]{4,3,2,1,0:T(8,128)S(1)} %get-tuple-element.44.own_ref.refs_5_), channel_id=1, source_target_pairs={{0,2},{2,0},{3,5},{5,3},{4,6},{6,4},{7,15},{15,7},{14,12},{12,14},... | collective-permute-start | bytes 589832 | tf_op jit(solution)/shard_map/ppermute | solution.py:454
  60.9 7.0 %collective-permute-start.9 = (f32[2,3,8,8,128]{4,3,2,1,0:T(8,128)S(1)}, f32[2,3,8,8,128]{4,3,2,1,0:T(8,128)S(1)}, u32[]{:S(2)}, u32[]{:S(2)}) collective-permute-start(f32[2,3,8,8,128]{4,3,2,1,0:T(8,128)S(1)} %get-tuple-element.44.own_ref.refs_5_), channel_id=1, source_target_pairs={{1,3},{3,1},{2,4},{4,2},{5,7},{7,5},{6,14},{14,6},{15,13},{13,15},... | collective-permute-start | bytes 589832 | tf_op jit(solution)/shard_map/ppermute | solution.py:455
  69.3 2.5 %collective-permute-start.10 = (f32[3,8,8,128]{3,2,1,0:T(8,128)S(1)}, f32[3,8,8,128]{3,2,1,0:T(8,128)S(1)}, u32[]{:S(2)}, u32[]{:S(2)}) collective-permute-start(f32[3,8,8,128]{3,2,1,0:T(8,128)S(1)} %get-tuple-element.47), channel_id=1, source_target_pairs={{0,1},{1,0},{2,3},{3,2},{4,5},{5,4},{6,7},{7,6},{8,9},{9,8},{10,11... | collective-permute-start | bytes 294920 | tf_op jit(solution)/shard_map/ppermute | solution.py:466
  72.3 1.4 %collective-permute-start.11 = (f32[256,128]{1,0:T(8,128)S(1)}, f32[256,128]{1,0:T(8,128)S(1)}, u32[]{:S(2)}, u32[]{:S(2)}) collective-permute-start(f32[256,128]{1,0:T(8,128)S(1)} %get-tuple-element.49), channel_id=1, source_target_pairs={{0,1},{1,0},{2,3},{3,2},{4,5},{5,4},{6,7},{7,6},{8,9},{9,8},{10,11... | collective-permute-start | bytes 393224 | tf_op jit(solution)/shard_map/ppermute | solution.py:480

commit v5 on v4

--- a/solution.py
+++ b/solution.py
@@ -155,70 +155,118 @@
     return u
 
 
-def chain_here(terms, first_ref, second_ref, carry_ref):
+def bands_summed(values):
+    source = lax.broadcasted_iota(jnp.int32, (128, 128), 0)
+    target = lax.broadcasted_iota(jnp.int32, (128, 128), 1)
+    same = (source % 8 == target % 8).astype(jnp.float32)
+    return jnp.dot(
+        values, same, precision=lax.Precision.HIGHEST, preferred_element_type=jnp.float32
+    )
+
+
+def chain_first(terms_of, decay_ref, pairs_ref, carry_ref, weigh_ref):
     pair = iota(1) // 8
     for f in range(FIELDS):
         for col in range(LONS):
-            c0, c1, decay = terms(f, col)
-            value = scan_pairs(c0 + decay * c1, decay * decay, pair)
-            first_ref[f, col] = value
-            second_ref[f, col] = c1 + decay * jnp.where(pair < 15, later(value, 1), 0.0)
-    source = lax.broadcasted_iota(jnp.int32, (128, 128), 0)
-    target = lax.broadcasted_iota(jnp.int32, (128, 128), 1)
-    spread = (source == target % 8).astype(jnp.float32)
-    values = first_ref[...].reshape(FIELDS * LONS * 8, 128)
-    carried = jnp.dot(
-        values, spread, precision=lax.Precision.HIGHEST, preferred_element_type=jnp.float32
-    )
-    carry_ref[...] = carried.reshape(FIELDS, LONS, 8, 128)
-
-
-def powers(square, exponent):
+            decay = decay_ref[f, col]
+            c0, c1 = terms_of(f, col)
+            both = c0 + decay * c1
+            if pairs_ref is not None:
+                pairs_ref[0, f, col] = both
+                pairs_ref[1, f, col] = c1
+            at = 8 * (LONS * f + col)
+            weigh_ref[at : at + 8, :] = powers(decay * decay, pair, (1, 2, 4, 8)) * both
+    carry_ref[...] = bands_summed(weigh_ref[...]).reshape(FIELDS, LONS, 8, 128)
+
+
+def chain_local(both, c1, decay, pair):
+    value = scan_pairs(both, decay * decay, pair)
+    return value, c1 + decay * jnp.where(pair < 15, later(value, 1), 0.0)
+
+
+def scan_kernel(pairs_ref, decay_ref, first_ref, second_ref):
+    pair = iota(1) // 8
+    for f in range(FIELDS):
+        for col in range(LONS):
+            first_ref[f, col], second_ref[f, col] = chain_local(
+                pairs_ref[0, f, col], pairs_ref[1, f, col], decay_ref[f, col], pair
+            )
+
+
+def powers(square, exponent, bits=(1, 2, 4, 8, 16)):
     power = jnp.where((exponent & 1) != 0, square, 1.0)
-    for bit in (2, 4, 8, 16):
+    for bit in bits[1:]:
         square = square * square
         power = power * jnp.where((exponent & bit) != 0, square, 1.0)
     return power
 
 
 def open_kernel(
-    core_ref, mine_ref, other_ref, first_ref, second_ref, carry_ref, decay_ref, power_ref, turn_ref, terms_ref
+    core_ref,
+    mine_ref,
+    other_ref,
+    zero_ref,
+    above_ref,
+    decay_ref,
+    power_ref,
+    turn_ref,
+    terms_ref,
+    weigh_ref,
+    carry_ref,
 ):
     low = core_ref[0] == 0
     lane = iota(1)
     pair = lane // 8
     even = (pair & 1) == 0
+
+    def turned(half_ref, s):
+        turn_ref[pl.ds(0, 64, stride=2), :] = jnp.where(low, half_ref[0], half_ref[1])
+        turn_ref[pl.ds(1, 64, stride=2), :] = jnp.where(low, half_ref[1], half_ref[0])
+        return turn_ref[...].T
+
     for s in range(4):
-        kept, got = (
-            jnp.where(low, ref[pl.ds(s, 64, stride=4), :], ref[pl.ds(256 + s, 64, stride=4), :])
-            for ref in (mine_ref, other_ref)
+        early, late = (
+            [ref[pl.ds(at + s, 64, stride=4), :] for ref in (mine_ref, other_ref)]
+            for at in (0, 256)
         )
-        turn_ref[pl.ds(0, 64, stride=2), :] = jnp.where(low, kept, got)
-        turn_ref[pl.ds(1, 64, stride=2), :] = jnp.where(low, got, kept)
-        turned = turn_ref[...].T
+        here = turned([jnp.where(low, a, b) for a, b in zip(early, late)], s)
+        behind = turned(late, s)
         for half in range(2):
             at = 64 * half
             col = s + 4 * half
-            mixed = turned[at + 48 : at + 56, :]
+            mixed = here[at + 48 : at + 56, :]
             decays = (
                 jnp.where(even, mixed, pltpu.roll(mixed, 8, 1)),
-                turned[at + 56 : at + 64, :],
+                here[at + 56 : at + 64, :],
                 jnp.where(even, pltpu.roll(mixed, 120, 1), mixed),
             )
             for f in range(FIELDS):
                 decay = decays[f]
                 decay_ref[f, col] = decay
-                terms_ref[0, f, col] = turned[at + 8 * f : at + 8 * f + 8, :]
-                terms_ref[1, f, col] = turned[at + 24 + 8 * f : at + 32 + 8 * f, :]
+                for j in range(2):
+                    to = at + 24 * j + 8 * f
+                    terms_ref[0, j, f, col] = here[to : to + 8, :]
+                    terms_ref[1, j, f, col] = behind[to : to + 8, :]
                 square = decay * decay
                 power_ref[0, f, col] = powers(square, 16 - pair)
-                power_ref[1, f, col] = decay * powers(square, 15 - pair)
-    chain_here(
-        lambda f, col: (terms_ref[0, f, col], terms_ref[1, f, col], decay_ref[f, col]),
-        first_ref,
-        second_ref,
+                power_ref[1, f, col] = decay * powers(square, 15 - pair, (1, 2, 4, 8))
+    chain_first(
+        lambda f, col: (terms_ref[1, 0, f, col], terms_ref[1, 1, f, col]),
+        decay_ref,
+        None,
         carry_ref,
-    )
+        weigh_ref,
+    )
+    for f in range(FIELDS):
+        for col in range(LONS):
+            decay = decay_ref[f, col]
+            c0, c1 = terms_ref[0, 0, f, col], terms_ref[0, 1, f, col]
+            carry = jnp.where(low, carry_ref[f, col], 0.0)
+            c1 = c1 + jnp.where(pair == 15, decay * carry, 0.0)
+            value, second = chain_local(c0 + decay * c1, c1, decay, pair)
+            zero_ref[f, col] = value
+            above_ref[0, f, col] = second
+            above_ref[1, f, col] = jnp.where(pair < 15, later(value, 1), carry)
 
 
 def close_kernel(core_ref, first_ref, second_ref, carry_ref, power_ref, zero_ref, above_ref):
@@ -234,7 +282,7 @@
 
 
 def fine_kernel(
-    odd_ref, own_ref, one_ref, two_ref, decay_ref, first_ref, second_ref, carry_ref, state_ref
+    odd_ref, own_ref, one_ref, two_ref, decay_ref, pairs_ref, carry_ref, state_ref, weigh_ref
 ):
     odd = odd_ref[0] == 1
     lane = iota(1)
@@ -320,10 +368,9 @@
                 edges(j, 2, low, high)
 
     def terms(f, col):
-        decay = decay_ref[f, col]
-        return *(unit * result[j, f, col] - decay * own_ref[j, f, col] for j in range(2)), decay
-
-    chain_here(terms, first_ref, second_ref, carry_ref)
+        return [unit * result[j, f, col] - decay_ref[f, col] * own_ref[j, f, col] for j in range(2)]
+
+    chain_first(terms, decay_ref, pairs_ref, carry_ref, weigh_ref)
 
 
 def finish_kernel(core_ref, *refs):
@@ -440,30 +487,42 @@
     field = shape(FIELDS, LONS, 8, 128)
     both = shape(2, FIELDS, LONS, 8, 128)
     square = pltpu.VMEM((128, 128), jnp.float32)
-    first, second, carry, decay, power = call(
-        open_kernel, (field, field, field, field, both), (core_arg,), got, other, scratch=[square, pltpu.VMEM((2, FIELDS, LONS, 8, 128), jnp.float32)]
+    weigh = pltpu.VMEM((FIELDS * LONS * 8, 128), jnp.float32)
+    zero, above, decay, power = call(
+        open_kernel,
+        (field, both, field, both),
+        (core_arg,),
+        got,
+        other,
+        scratch=[
+            square,
+            pltpu.VMEM((2, 2, FIELDS, LONS, 8, 128), jnp.float32),
+            weigh,
+            pltpu.VMEM((FIELDS, LONS, 8, 128), jnp.float32),
+        ],
     )
     zeros, aboves = [], []
-    for _ in range(ITERS):
-        carry = lax.ppermute(carry, "c", SIBLING)
-        zero, above = call(
-            close_kernel, (field, both), (core_arg,), first, second, carry, power
-        )
+    for iteration in range(ITERS):
+        if iteration > 0:
+            zero, above = call(
+                close_kernel, (field, both), (core_arg,), first, second, carry, power
+            )
         zeros.append(zero)
         aboves.append(above)
-        side_even = lax.ppermute(above, ALL, swap_pairs(0))
-        side_odd = lax.ppermute(above, ALL, swap_pairs(1))
-        first, second, carry = call(
+        side_one = lax.ppermute(above, ALL, swap_pairs(0))
+        side_two = lax.ppermute(above, ALL, swap_pairs(1))
+        pairs, carry = call(
             fine_kernel,
-            (field, field, field),
+            (both, field),
             (tile_odd,),
             above,
-            side_even,
-            side_odd,
+            side_one,
+            side_two,
             decay,
-            scratch=[pltpu.VMEM((2 * FIELDS * 3 * LONS * 24, 128), jnp.float32)],
+            scratch=[pltpu.VMEM((2 * FIELDS * 3 * LONS * 24, 128), jnp.float32), weigh],
         )
-    carry = lax.ppermute(carry, "c", SIBLING)
+        carry = lax.ppermute(carry, "c", SIBLING)
+        first, second = call(scan_kernel, (field, field), (), pairs, decay)
     mine, away = call(
         finish_kernel,
         (shape(256, 128), shape(256, 128)),

time: 94.6 us -> 92.9 us (0.982)
  waiting for transfers between devices: 25.6 us -> 23.7 us
    ppermute x4 -> x3, waiting for transfers between devices: 3.77 us -> 1.69 us  [per_device(): carry = lax.ppermute(carry, 'c', SIBLING)]
    pallas_call x11 -> x13, Pallas kernels: 9 us -> 9.61 us  [call(): pl.pallas_call(kernel, out_shape=outs, in_specs=[smem] * len(scalars) + [...]
    ppermute x4 -> x3, starting transfers between devices: 5.3 us -> 4.86 us  [per_device(): carry = lax.ppermute(carry, 'c', SIBLING)]
  transfers between devices with their start and end apart: 12 -> 11, of which waited for: 9 -> 8; matrix products, arithmetic and copies ran while one was open for 0% -> 0% of each run, Pallas kernels for 0% -> 1%
where the time goes in v5:
time: 92.9 us; the launch traced here: 92.7 us
  blocking collectives  49 us (53%)
  waiting for transfers between devices  23.7 us (26%)
  Pallas kernels  9.61 us (10%)
  starting transfers between devices  8.82 us (9%)
    all_to_all x1, blocking collectives, per_device(): lax.all_to_all(sent.reshape(CHIPS, 4, 128), ZYX, 0, 0).reshape(512, 128)  29.5 us
    ppermute x3, waiting for transfers between devices, per_device(): side_one = lax.ppermute(above, ALL, swap_pairs(0))  19.9 us
    all_to_all x1, blocking collectives, per_device(): lax.all_to_all(back.reshape(CHIPS, 4, 128), ZYX, 0, 0).reshape(512, 128)  19.5 us
    pallas_call x13, Pallas kernels, call(): pl.pallas_call(kernel, out_shape=outs, in_specs=[smem] * len(scalars) + [...  9.61 us
    ppermute x3, starting transfers between devices, per_device(): carry = lax.ppermute(carry, 'c', SIBLING)  4.86 us
    ppermute x1, starting transfers between devices, per_device(): other = lax.ppermute(got, 'c', SIBLING)  2.69 us
  transfers between devices with their start and end apart: 11, of which 8 were waited for; matrix products, arithmetic and copies ran while one was open for 0% of the time, Pallas kernels for 1%

profile of v5, /device:TPU:1, one launch (start us, length us, event | category | flops | bytes accessed | tf_op | source)
XLA Modules:
  0.0 92.7 jit_solution(10054867684515924429)
XLA Ops:
  0.6 2.3 %shard_map.67 = f32[512,128]{1,0:T(8,128)S(1)} custom-call(s32[1]{0:T(128)} %bitcast.1.place_ref, f32[2,3,16,1024]{3,2,1,0:T(8,128)} %bitcast.17, f32[2,16]{1,0:T(2,128)} %weight_ref.1, s32[2,16]{1,0:T(2,128)} %block_ref.1, f32[3,8,1024]{2,1,0:T(8,128)} %decay_ref.1), custom_call_target="tpu_custom_call" | custom-call | tf_op jit(solution)/shard_map/pallas_call | solution.py:63
  3.0 29.5 %all_to_all.10 = f32[128,4,128]{2,1,0:T(4,128)S(1)} all-to-all(f32[128,4,128]{2,1,0:T(4,128)S(1)} %bitcast.16), channel_id=1, replica_groups=mesh['z'=8,'y'=4,'x'=4,'c'=2] {'z','y','x'}, dimensions={0} | all-to-all | bytes 524288 | tf_op jit(solution)/shard_map/all_to_all | solution.py:484
  32.5 2.7 %collective-permute-start = (f32[512,128]{1,0:T(8,128)S(1)}, f32[512,128]{1,0:T(8,128)S(1)}, u32[]{:S(2)}, u32[]{:S(2)}) collective-permute-start(f32[512,128]{1,0:T(8,128)S(1)} %bitcast.12), channel_id=1, source_target_pairs={{0,1},{1,0},{2,3},{3,2},{4,5},{5,4},{6,7},{7,6},{8,9},{9,8},{10,11... | collective-permute-start | bytes 786440 | tf_op jit(solution)/shard_map/ppermute | solution.py:485
  35.2 1.2 %collective-permute-done.other_ref = f32[512,128]{1,0:T(8,128)S(1)} collective-permute-done((f32[512,128]{1,0:T(8,128)S(1)}, f32[512,128]{1,0:T(8,128)S(1)}, u32[]{:S(2)}, u32[]{:S(2)}) %collective-permute-start) | collective-permute-done | bytes 262176 | tf_op jit(solution)/shard_map/ppermute | solution.py:485
  36.4 0.8 shard_map.68
  37.7 6.4 %collective-permute-done.1.one_ref = f32[2,3,8,8,128]{4,3,2,1,0:T(8,128)S(1)} collective-permute-done((f32[2,3,8,8,128]{4,3,2,1,0:T(8,128)S(1)}, f32[2,3,8,8,128]{4,3,2,1,0:T(8,128)S(1)}, u32[]{:S(2)}, u32[]{:S(2)}) %collective-permute-start.1) | collective-permute-done | bytes 196640 | tf_op jit(solution)/shard_map/ppermute | solution.py:512
  44.1 1.2 %shard_map.69 = (f32[2,3,8,8,128]{4,3,2,1,0:T(8,128)S(1)}, f32[3,8,8,128]{3,2,1,0:T(8,128)S(1)}) custom-call(s32[1]{0:T(128)} %bitcast.5.odd_ref, f32[2,3,8,8,128]{4,3,2,1,0:T(8,128)S(1)} %get-tuple-element.29.own_ref.refs_3_, f32[2,3,8,8,128]{4,3,2,1,0:T(8,128)S(1)} %collective-permute-done.1.one_ref, ...), custom_call_target="tpu_custom_call" | custom-call | tf_op jit(solution)/shard_map/pallas_call | solution.py:63
  45.2 1.9 %collective-permute-start.3 = (f32[3,8,8,128]{3,2,1,0:T(8,128)S(1)}, f32[3,8,8,128]{3,2,1,0:T(8,128)S(1)}, u32[]{:S(2)}, u32[]{:S(2)}) collective-permute-start(f32[3,8,8,128]{3,2,1,0:T(8,128)S(1)} %get-tuple-element.34), channel_id=1, source_target_pairs={{0,1},{1,0},{2,3},{3,2},{4,5},{5,4},{6,7},{7,6},{8,9},{9,8},{10,11... | collective-permute-start | bytes 294920 | tf_op jit(solution)/shard_map/ppermute | solution.py:524
  47.1 0.4 shard_map.70
  47.5 0.6 collective-permute-done.3.carry_ref
  48.4 7.1 %collective-permute-done.4.one_ref = f32[2,3,8,8,128]{4,3,2,1,0:T(8,128)S(1)} collective-permute-done((f32[2,3,8,8,128]{4,3,2,1,0:T(8,128)S(1)}, f32[2,3,8,8,128]{4,3,2,1,0:T(8,128)S(1)}, u32[]{:S(2)}, u32[]{:S(2)}) %collective-permute-start.4) | collective-permute-done | bytes 196640 | tf_op jit(solution)/shard_map/ppermute | solution.py:512
  55.5 1.2 %shard_map.72 = (f32[2,3,8,8,128]{4,3,2,1,0:T(8,128)S(1)}, f32[3,8,8,128]{3,2,1,0:T(8,128)S(1)}) custom-call(s32[1]{0:T(128)} %bitcast.5.odd_ref, f32[2,3,8,8,128]{4,3,2,1,0:T(8,128)S(1)} %get-tuple-element.37.own_ref.refs_4_, f32[2,3,8,8,128]{4,3,2,1,0:T(8,128)S(1)} %collective-permute-done.4.one_ref, ...), custom_call_target="tpu_custom_call" | custom-call | tf_op jit(solution)/shard_map/pallas_call | solution.py:63
  56.6 1.4 %collective-permute-start.6 = (f32[3,8,8,128]{3,2,1,0:T(8,128)S(1)}, f32[3,8,8,128]{3,2,1,0:T(8,128)S(1)}, u32[]{:S(2)}, u32[]{:S(2)}) collective-permute-start(f32[3,8,8,128]{3,2,1,0:T(8,128)S(1)} %get-tuple-element.41), channel_id=1, source_target_pairs={{0,1},{1,0},{2,3},{3,2},{4,5},{5,4},{6,7},{7,6},{8,9},{9,8},{10,11... | collective-permute-start | bytes 294920 | tf_op jit(solution)/shard_map/ppermute | solution.py:524
  58.4 0.6 collective-permute-done.6.carry_ref
  59.3 0.5 copy-done.1
  60.0 6.4 %collective-permute-done.7.one_ref = f32[2,3,8,8,128]{4,3,2,1,0:T(8,128)S(1)} collective-permute-done((f32[2,3,8,8,128]{4,3,2,1,0:T(8,128)S(1)}, f32[2,3,8,8,128]{4,3,2,1,0:T(8,128)S(1)}, u32[]{:S(2)}, u32[]{:S(2)}) %collective-permute-start.7) | collective-permute-done | bytes 196640 | tf_op jit(solution)/shard_map/ppermute | solution.py:512
  66.4 1.2 %shard_map.75 = (f32[2,3,8,8,128]{4,3,2,1,0:T(8,128)S(1)}, f32[3,8,8,128]{3,2,1,0:T(8,128)S(1)}) custom-call(s32[1]{0:T(128)} %bitcast.5.odd_ref, f32[2,3,8,8,128]{4,3,2,1,0:T(8,128)S(1)} %get-tuple-element.43.own_ref.refs_5_, f32[2,3,8,8,128]{4,3,2,1,0:T(8,128)S(1)} %collective-permute-done.7.one_ref, ...), custom_call_target="tpu_custom_call" | custom-call | tf_op jit(solution)/shard_map/pallas_call | solution.py:63
  67.6 1.6 %collective-permute-start.9 = (f32[3,8,8,128]{3,2,1,0:T(8,128)S(1)}, f32[3,8,8,128]{3,2,1,0:T(8,128)S(1)}, u32[]{:S(2)}, u32[]{:S(2)}) collective-permute-start(f32[3,8,8,128]{3,2,1,0:T(8,128)S(1)} %get-tuple-element.47), channel_id=1, source_target_pairs={{0,1},{1,0},{2,3},{3,2},{4,5},{5,4},{6,7},{7,6},{8,9},{9,8},{10,11... | collective-permute-start | bytes 294920 | tf_op jit(solution)/shard_map/ppermute | solution.py:524
  69.6 0.6 collective-permute-done.9.refs_8_
  70.1 0.4 shard_map.77
  70.6 0.5 collective-permute-start.10
  71.0 1.0 %collective-permute-done.10.got_ref = f32[256,128]{1,0:T(8,128)S(1)} collective-permute-done((f32[256,128]{1,0:T(8,128)S(1)}, f32[256,128]{1,0:T(8,128)S(1)}, u32[]{:S(2)}, u32[]{:S(2)}) %collective-permute-start.10) | collective-permute-done | bytes 131104 | tf_op jit(solution)/shard_map/ppermute | solution.py:539
  72.0 19.5 %all_to_all.11 = f32[128,4,128]{2,1,0:T(4,128)S(1)} all-to-all(f32[128,4,128]{2,1,0:T(4,128)S(1)} %bitcast.14), channel_id=1, replica_groups=mesh['z'=8,'y'=4,'x'=4,'c'=2] {'z','y','x'}, dimensions={0} | all-to-all | bytes 524288 | tf_op jit(solution)/shard_map/all_to_all | solution.py:541
  91.5 1.1 %shard_map.79 = (f32[2,3,8,1024]{3,2,1,0:T(8,128)}, f32[1,1]{1,0:T(1,128)}, f32[1,3]{1,0:T(1,128)}) custom-call(f32[512,128]{1,0:T(8,128)S(1)} %bitcast.15), custom_call_target="tpu_custom_call" | custom-call | tf_op jit(solution)/shard_map/pallas_call | solution.py:63
  (21 shorter events, 2.0 us)
Async XLA Ops:
  32.5 3.8 %collective-permute-start = (f32[512,128]{1,0:T(8,128)S(1)}, f32[512,128]{1,0:T(8,128)S(1)}, u32[]{:S(2)}, u32[]{:S(2)}) collective-permute-start(f32[512,128]{1,0:T(8,128)S(1)} %bitcast.12), channel_id=1, source_target_pairs={{0,1},{1,0},{2,3},{3,2},{4,5},{5,4},{6,7},{7,6},{8,9},{9,8},{10,11... | collective-permute-start | bytes 786440 | tf_op jit(solution)/shard_map/ppermute | solution.py:485
  37.2 6.8 %collective-permute-start.1 = (f32[2,3,8,8,128]{4,3,2,1,0:T(8,128)S(1)}, f32[2,3,8,8,128]{4,3,2,1,0:T(8,128)S(1)}, u32[]{:S(2)}, u32[]{:S(2)}) collective-permute-start(f32[2,3,8,8,128]{4,3,2,1,0:T(8,128)S(1)} %get-tuple-element.29.own_ref.refs_3_), channel_id=1, source_target_pairs={{0,2},{2,0},{3,5},{5,3},{4,6},{6,4},{7,15},{15,7},{14,12},{12,14},... | collective-permute-start | bytes 589832 | tf_op jit(solution)/shard_map/ppermute | solution.py:512
  37.3 6.7 %collective-permute-start.2 = (f32[2,3,8,8,128]{4,3,2,1,0:T(8,128)S(1)}, f32[2,3,8,8,128]{4,3,2,1,0:T(8,128)S(1)}, u32[]{:S(2)}, u32[]{:S(2)}) collective-permute-start(f32[2,3,8,8,128]{4,3,2,1,0:T(8,128)S(1)} %get-tuple-element.29.own_ref.refs_3_), channel_id=1, source_target_pairs={{1,3},{3,1},{2,4},{4,2},{5,7},{7,5},{6,14},{14,6},{15,13},{13,15},... | collective-permute-start | bytes 589832 | tf_op jit(solution)/shard_map/ppermute | solution.py:513
  45.2 2.8 %collective-permute-start.3 = (f32[3,8,8,128]{3,2,1,0:T(8,128)S(1)}, f32[3,8,8,128]{3,2,1,0:T(8,128)S(1)}, u32[]{:S(2)}, u32[]{:S(2)}) collective-permute-start(f32[3,8,8,128]{3,2,1,0:T(8,128)S(1)} %get-tuple-element.34), channel_id=1, source_target_pairs={{0,1},{1,0},{2,3},{3,2},{4,5},{5,4},{6,7},{7,6},{8,9},{9,8},{10,11... | collective-permute-start | bytes 294920 | tf_op jit(solution)/shard_map/ppermute | solution.py:524
  48.2 7.3 %collective-permute-start.4 = (f32[2,3,8,8,128]{4,3,2,1,0:T(8,128)S(1)}, f32[2,3,8,8,128]{4,3,2,1,0:T(8,128)S(1)}, u32[]{:S(2)}, u32[]{:S(2)}) collective-permute-start(f32[2,3,8,8,128]{4,3,2,1,0:T(8,128)S(1)} %get-tuple-element.37.own_ref.refs_4_), channel_id=1, source_target_pairs={{0,2},{2,0},{3,5},{5,3},{4,6},{6,4},{7,15},{15,7},{14,12},{12,14},... | collective-permute-start | bytes 589832 | tf_op jit(solution)/shard_map/ppermute | solution.py:512
  48.3 7.2 %collective-permute-start.5 = (f32[2,3,8,8,128]{4,3,2,1,0:T(8,128)S(1)}, f32[2,3,8,8,128]{4,3,2,1,0:T(8,128)S(1)}, u32[]{:S(2)}, u32[]{:S(2)}) collective-permute-start(f32[2,3,8,8,128]{4,3,2,1,0:T(8,128)S(1)} %get-tuple-element.37.own_ref.refs_4_), channel_id=1, source_target_pairs={{1,3},{3,1},{2,4},{4,2},{5,7},{7,5},{6,14},{14,6},{15,13},{13,15},... | collective-permute-start | bytes 589832 | tf_op jit(solution)/shard_map/ppermute | solution.py:513
  56.6 2.3 %collective-permute-start.6 = (f32[3,8,8,128]{3,2,1,0:T(8,128)S(1)}, f32[3,8,8,128]{3,2,1,0:T(8,128)S(1)}, u32[]{:S(2)}, u32[]{:S(2)}) collective-permute-start(f32[3,8,8,128]{3,2,1,0:T(8,128)S(1)} %get-tuple-element.41), channel_id=1, source_target_pairs={{0,1},{1,0},{2,3},{3,2},{4,5},{5,4},{6,7},{7,6},{8,9},{9,8},{10,11... | collective-permute-start | bytes 294920 | tf_op jit(solution)/shard_map/ppermute | solution.py:524
  58.1 1.8 %copy-start = (f32[2,16,3,1024]{3,1,2,0:T(8,128)S(1)}, f32[2,16,3,1024]{3,1,2,0:T(8,128)}, u32[]{:S(2)}) copy-start(f32[2,16,3,1024]{3,1,2,0:T(8,128)} %param.4) | copy-start | bytes 1179652
  59.1 0.7 copy-start.1
  59.1 7.3 %collective-permute-start.7 = (f32[2,3,8,8,128]{4,3,2,1,0:T(8,128)S(1)}, f32[2,3,8,8,128]{4,3,2,1,0:T(8,128)S(1)}, u32[]{:S(2)}, u32[]{:S(2)}) collective-permute-start(f32[2,3,8,8,128]{4,3,2,1,0:T(8,128)S(1)} %get-tuple-element.43.own_ref.refs_5_), channel_id=1, source_target_pairs={{0,2},{2,0},{3,5},{5,3},{4,6},{6,4},{7,15},{15,7},{14,12},{12,14},... | collective-permute-start | bytes 589832 | tf_op jit(solution)/shard_map/ppermute | solution.py:512
  59.2 7.2 %collective-permute-start.8 = (f32[2,3,8,8,128]{4,3,2,1,0:T(8,128)S(1)}, f32[2,3,8,8,128]{4,3,2,1,0:T(8,128)S(1)}, u32[]{:S(2)}, u32[]{:S(2)}) collective-permute-start(f32[2,3,8,8,128]{4,3,2,1,0:T(8,128)S(1)} %get-tuple-element.43.own_ref.refs_5_), channel_id=1, source_target_pairs={{1,3},{3,1},{2,4},{4,2},{5,7},{7,5},{6,14},{14,6},{15,13},{13,15},... | collective-permute-start | bytes 589832 | tf_op jit(solution)/shard_map/ppermute | solution.py:513
  67.6 2.5 %collective-permute-start.9 = (f32[3,8,8,128]{3,2,1,0:T(8,128)S(1)}, f32[3,8,8,128]{3,2,1,0:T(8,128)S(1)}, u32[]{:S(2)}, u32[]{:S(2)}) collective-permute-start(f32[3,8,8,128]{3,2,1,0:T(8,128)S(1)} %get-tuple-element.47), channel_id=1, source_target_pairs={{0,1},{1,0},{2,3},{3,2},{4,5},{5,4},{6,7},{7,6},{8,9},{9,8},{10,11... | collective-permute-start | bytes 294920 | tf_op jit(solution)/shard_map/ppermute | solution.py:524
  70.6 1.4 %collective-permute-start.10 = (f32[256,128]{1,0:T(8,128)S(1)}, f32[256,128]{1,0:T(8,128)S(1)}, u32[]{:S(2)}, u32[]{:S(2)}) collective-permute-start(f32[256,128]{1,0:T(8,128)S(1)} %get-tuple-element.49), channel_id=1, source_target_pairs={{0,1},{1,0},{2,3},{3,2},{4,5},{5,4},{6,7},{7,6},{8,9},{9,8},{10,11... | collective-permute-start | bytes 393224 | tf_op jit(solution)/shard_map/ppermute | solution.py:539

commit v6 on v5

--- a/solution.py
+++ b/solution.py
@@ -72,6 +72,11 @@
 
 def iota(dim):
     return lax.broadcasted_iota(jnp.int32, (8, 128), dim)
+
+
+def split(values):
+    high = values.astype(jnp.bfloat16)
+    return high, (values - high.astype(jnp.float32)).astype(jnp.bfloat16)
 
 
 def pack_kernel(
@@ -91,38 +96,30 @@
     copies = [
         pltpu.make_async_copy(weight_ref, weights_ref, sems.at[0]),
         pltpu.make_async_copy(block_ref, blocks_ref, sems.at[1]),
-        pltpu.make_async_copy(decay_ref, decays_ref, sems.at[2]),
+        pltpu.make_async_copy(departure_ref, values_ref, sems.at[2]),
+        pltpu.make_async_copy(decay_ref, decays_ref, sems.at[3]),
     ]
-    parts = {
-        (j, f): pltpu.make_async_copy(
-            departure_ref.at[j, f], values_ref.at[j, f], sems.at[3 + FIELDS * j + f]
-        )
-        for j in range(2)
-        for f in range(FIELDS)
-    }
-    for copy in copies[:2] + list(parts.values()) + copies[2:]:
+    for copy in copies:
         copy.start()
-    copies[0].wait()
-    copies[1].wait()
+    for copy in copies:
+        copy.wait()
     block = lax.broadcasted_iota(jnp.int32, (8, 16), 0)
     for j in range(2):
         emphasis = 1.0 + 2.0 * (place_ref[0] * 2 + j).astype(jnp.float32) / 63.0
         choose = jnp.where(
             blocks_ref[j : j + 1, :] == block, emphasis * weights_ref[j : j + 1, :], 0.0
         )
+        choose_high, choose_low = split(choose)
+        choose_both = jnp.concatenate([choose_high, choose_low], axis=0)
         for f in range(FIELDS):
-            parts[j, f].wait()
-            tiles = jnp.dot(
-                choose,
-                values_ref[j, f],
-                precision=lax.Precision.HIGHEST,
-                preferred_element_type=jnp.float32,
-            )
+            values_high, values_low = split(values_ref[j, f])
+            main = jnp.dot(choose_both, values_high, preferred_element_type=jnp.float32)
+            rest = jnp.dot(choose_high, values_low, preferred_element_type=jnp.float32)
+            tiles = main[0:8] + (main[8:16] + rest)
             for r in range(8):
                 rows_ref[pl.ds(24 * j + 8 * f + r, 8, stride=64), :] = tiles[
                     :, 128 * r : 128 * r + 128
                 ]
-    copies[2].wait()
     odd = (place_ref[0] & 1) == 1
     for b in range(8):
         span = slice(128 * b, 128 * b + 128)
@@ -478,7 +475,7 @@
             pltpu.VMEM((2, 16), jnp.int32),
             pltpu.VMEM((FIELDS, 8, 1024), jnp.float32),
             pltpu.VMEM((512, 128), jnp.float32),
-            pltpu.SemaphoreType.DMA((9,)),
+            pltpu.SemaphoreType.DMA((4,)),
         ],
     )
     got = lax.all_to_all(sent.reshape(CHIPS, 4, 128), ZYX, 0, 0).reshape(512, 128)

time: 92.9 us -> 92.1 us (level)
  no operation moved by 1% of the time
where the time goes in v6:
time: 92.1 us; the launch traced here: 92 us
  blocking collectives  49 us (53%)
  waiting for transfers between devices  23.7 us (26%)
  Pallas kernels  8.91 us (10%)
  starting transfers between devices  8.82 us (10%)
    all_to_all x1, blocking collectives, per_device(): lax.all_to_all(sent.reshape(CHIPS, 4, 128), ZYX, 0, 0).reshape(512, 128)  29.5 us
    ppermute x3, waiting for transfers between devices, per_device(): side_one = lax.ppermute(above, ALL, swap_pairs(0))  19.9 us
    all_to_all x1, blocking collectives, per_device(): lax.all_to_all(back.reshape(CHIPS, 4, 128), ZYX, 0, 0).reshape(512, 128)  19.5 us
    pallas_call x13, Pallas kernels, call(): pl.pallas_call(kernel, out_shape=outs, in_specs=[smem] * len(scalars) + [...  8.91 us
    ppermute x3, starting transfers between devices, per_device(): carry = lax.ppermute(carry, 'c', SIBLING)  4.86 us
    ppermute x1, starting transfers between devices, per_device(): other = lax.ppermute(got, 'c', SIBLING)  2.69 us
  transfers between devices with their start and end apart: 11, of which 8 were waited for; matrix products, arithmetic and copies ran while one was open for 0% of the time, Pallas kernels for 1%

profile of v6, /device:TPU:1, one launch (start us, length us, event | category | flops | bytes accessed | tf_op | source)
XLA Modules:
  0.0 92.0 jit_solution(10878637113487966775)
XLA Ops:
  0.6 1.6 %shard_map.67 = f32[512,128]{1,0:T(8,128)S(1)} custom-call(s32[1]{0:T(128)} %bitcast.1.place_ref, f32[2,3,16,1024]{3,2,1,0:T(8,128)} %bitcast.17, f32[2,16]{1,0:T(2,128)} %weight_ref.1, s32[2,16]{1,0:T(2,128)} %block_ref.1, f32[3,8,1024]{2,1,0:T(8,128)} %decay_ref.1), custom_call_target="tpu_custom_call" | custom-call | tf_op jit(solution)/shard_map/pallas_call | solution.py:63
  2.3 29.5 %all_to_all.10 = f32[128,4,128]{2,1,0:T(4,128)S(1)} all-to-all(f32[128,4,128]{2,1,0:T(4,128)S(1)} %bitcast.16), channel_id=1, replica_groups=mesh['z'=8,'y'=4,'x'=4,'c'=2] {'z','y','x'}, dimensions={0} | all-to-all | bytes 524288 | tf_op jit(solution)/shard_map/all_to_all | solution.py:481
  31.8 2.7 %collective-permute-start = (f32[512,128]{1,0:T(8,128)S(1)}, f32[512,128]{1,0:T(8,128)S(1)}, u32[]{:S(2)}, u32[]{:S(2)}) collective-permute-start(f32[512,128]{1,0:T(8,128)S(1)} %bitcast.12), channel_id=1, source_target_pairs={{0,1},{1,0},{2,3},{3,2},{4,5},{5,4},{6,7},{7,6},{8,9},{9,8},{10,11... | collective-permute-start | bytes 786440 | tf_op jit(solution)/shard_map/ppermute | solution.py:482
  34.5 1.2 %collective-permute-done.other_ref = f32[512,128]{1,0:T(8,128)S(1)} collective-permute-done((f32[512,128]{1,0:T(8,128)S(1)}, f32[512,128]{1,0:T(8,128)S(1)}, u32[]{:S(2)}, u32[]{:S(2)}) %collective-permute-start) | collective-permute-done | bytes 262176 | tf_op jit(solution)/shard_map/ppermute | solution.py:482
  35.7 0.8 shard_map.68
  37.0 6.4 %collective-permute-done.1.one_ref = f32[2,3,8,8,128]{4,3,2,1,0:T(8,128)S(1)} collective-permute-done((f32[2,3,8,8,128]{4,3,2,1,0:T(8,128)S(1)}, f32[2,3,8,8,128]{4,3,2,1,0:T(8,128)S(1)}, u32[]{:S(2)}, u32[]{:S(2)}) %collective-permute-start.1) | collective-permute-done | bytes 196640 | tf_op jit(solution)/shard_map/ppermute | solution.py:509
  43.4 1.2 %shard_map.69 = (f32[2,3,8,8,128]{4,3,2,1,0:T(8,128)S(1)}, f32[3,8,8,128]{3,2,1,0:T(8,128)S(1)}) custom-call(s32[1]{0:T(128)} %bitcast.5.odd_ref, f32[2,3,8,8,128]{4,3,2,1,0:T(8,128)S(1)} %get-tuple-element.29.own_ref.refs_3_, f32[2,3,8,8,128]{4,3,2,1,0:T(8,128)S(1)} %collective-permute-done.1.one_ref, ...), custom_call_target="tpu_custom_call" | custom-call | tf_op jit(solution)/shard_map/pallas_call | solution.py:63
  44.5 1.9 %collective-permute-start.3 = (f32[3,8,8,128]{3,2,1,0:T(8,128)S(1)}, f32[3,8,8,128]{3,2,1,0:T(8,128)S(1)}, u32[]{:S(2)}, u32[]{:S(2)}) collective-permute-start(f32[3,8,8,128]{3,2,1,0:T(8,128)S(1)} %get-tuple-element.34), channel_id=1, source_target_pairs={{0,1},{1,0},{2,3},{3,2},{4,5},{5,4},{6,7},{7,6},{8,9},{9,8},{10,11... | collective-permute-start | bytes 294920 | tf_op jit(solution)/shard_map/ppermute | solution.py:521
  46.4 0.4 shard_map.70
  46.8 0.6 collective-permute-done.3.carry_ref
  47.7 7.1 %collective-permute-done.4.one_ref = f32[2,3,8,8,128]{4,3,2,1,0:T(8,128)S(1)} collective-permute-done((f32[2,3,8,8,128]{4,3,2,1,0:T(8,128)S(1)}, f32[2,3,8,8,128]{4,3,2,1,0:T(8,128)S(1)}, u32[]{:S(2)}, u32[]{:S(2)}) %collective-permute-start.4) | collective-permute-done | bytes 196640 | tf_op jit(solution)/shard_map/ppermute | solution.py:509
  54.8 1.2 %shard_map.72 = (f32[2,3,8,8,128]{4,3,2,1,0:T(8,128)S(1)}, f32[3,8,8,128]{3,2,1,0:T(8,128)S(1)}) custom-call(s32[1]{0:T(128)} %bitcast.5.odd_ref, f32[2,3,8,8,128]{4,3,2,1,0:T(8,128)S(1)} %get-tuple-element.37.own_ref.refs_4_, f32[2,3,8,8,128]{4,3,2,1,0:T(8,128)S(1)} %collective-permute-done.4.one_ref, ...), custom_call_target="tpu_custom_call" | custom-call | tf_op jit(solution)/shard_map/pallas_call | solution.py:63
  55.9 1.4 %collective-permute-start.6 = (f32[3,8,8,128]{3,2,1,0:T(8,128)S(1)}, f32[3,8,8,128]{3,2,1,0:T(8,128)S(1)}, u32[]{:S(2)}, u32[]{:S(2)}) collective-permute-start(f32[3,8,8,128]{3,2,1,0:T(8,128)S(1)} %get-tuple-element.41), channel_id=1, source_target_pairs={{0,1},{1,0},{2,3},{3,2},{4,5},{5,4},{6,7},{7,6},{8,9},{9,8},{10,11... | collective-permute-start | bytes 294920 | tf_op jit(solution)/shard_map/ppermute | solution.py:521
  57.7 0.6 collective-permute-done.6.carry_ref
  58.6 0.5 copy-done.1
  59.3 6.4 %collective-permute-done.7.one_ref = f32[2,3,8,8,128]{4,3,2,1,0:T(8,128)S(1)} collective-permute-done((f32[2,3,8,8,128]{4,3,2,1,0:T(8,128)S(1)}, f32[2,3,8,8,128]{4,3,2,1,0:T(8,128)S(1)}, u32[]{:S(2)}, u32[]{:S(2)}) %collective-permute-start.7) | collective-permute-done | bytes 196640 | tf_op jit(solution)/shard_map/ppermute | solution.py:509
  65.7 1.2 %shard_map.75 = (f32[2,3,8,8,128]{4,3,2,1,0:T(8,128)S(1)}, f32[3,8,8,128]{3,2,1,0:T(8,128)S(1)}) custom-call(s32[1]{0:T(128)} %bitcast.5.odd_ref, f32[2,3,8,8,128]{4,3,2,1,0:T(8,128)S(1)} %get-tuple-element.43.own_ref.refs_5_, f32[2,3,8,8,128]{4,3,2,1,0:T(8,128)S(1)} %collective-permute-done.7.one_ref, ...), custom_call_target="tpu_custom_call" | custom-call | tf_op jit(solution)/shard_map/pallas_call | solution.py:63
  66.9 1.6 %collective-permute-start.9 = (f32[3,8,8,128]{3,2,1,0:T(8,128)S(1)}, f32[3,8,8,128]{3,2,1,0:T(8,128)S(1)}, u32[]{:S(2)}, u32[]{:S(2)}) collective-permute-start(f32[3,8,8,128]{3,2,1,0:T(8,128)S(1)} %get-tuple-element.47), channel_id=1, source_target_pairs={{0,1},{1,0},{2,3},{3,2},{4,5},{5,4},{6,7},{7,6},{8,9},{9,8},{10,11... | collective-permute-start | bytes 294920 | tf_op jit(solution)/shard_map/ppermute | solution.py:521
  68.9 0.6 collective-permute-done.9.refs_8_
  69.4 0.4 shard_map.77
  69.9 0.5 collective-permute-start.10
  70.3 1.0 %collective-permute-done.10.got_ref = f32[256,128]{1,0:T(8,128)S(1)} collective-permute-done((f32[256,128]{1,0:T(8,128)S(1)}, f32[256,128]{1,0:T(8,128)S(1)}, u32[]{:S(2)}, u32[]{:S(2)}) %collective-permute-start.10) | collective-permute-done | bytes 131104 | tf_op jit(solution)/shard_map/ppermute | solution.py:536
  71.3 19.5 %all_to_all.11 = f32[128,4,128]{2,1,0:T(4,128)S(1)} all-to-all(f32[128,4,128]{2,1,0:T(4,128)S(1)} %bitcast.14), channel_id=1, replica_groups=mesh['z'=8,'y'=4,'x'=4,'c'=2] {'z','y','x'}, dimensions={0} | all-to-all | bytes 524288 | tf_op jit(solution)/shard_map/all_to_all | solution.py:538
  90.8 1.1 %shard_map.79 = (f32[2,3,8,1024]{3,2,1,0:T(8,128)}, f32[1,1]{1,0:T(1,128)}, f32[1,3]{1,0:T(1,128)}) custom-call(f32[512,128]{1,0:T(8,128)S(1)} %bitcast.15), custom_call_target="tpu_custom_call" | custom-call | tf_op jit(solution)/shard_map/pallas_call | solution.py:63
  (21 shorter events, 2.0 us)
Async XLA Ops:
  31.8 3.8 %collective-permute-start = (f32[512,128]{1,0:T(8,128)S(1)}, f32[512,128]{1,0:T(8,128)S(1)}, u32[]{:S(2)}, u32[]{:S(2)}) collective-permute-start(f32[512,128]{1,0:T(8,128)S(1)} %bitcast.12), channel_id=1, source_target_pairs={{0,1},{1,0},{2,3},{3,2},{4,5},{5,4},{6,7},{7,6},{8,9},{9,8},{10,11... | collective-permute-start | bytes 786440 | tf_op jit(solution)/shard_map/ppermute | solution.py:482
  36.5 6.8 %collective-permute-start.1 = (f32[2,3,8,8,128]{4,3,2,1,0:T(8,128)S(1)}, f32[2,3,8,8,128]{4,3,2,1,0:T(8,128)S(1)}, u32[]{:S(2)}, u32[]{:S(2)}) collective-permute-start(f32[2,3,8,8,128]{4,3,2,1,0:T(8,128)S(1)} %get-tuple-element.29.own_ref.refs_3_), channel_id=1, source_target_pairs={{0,2},{2,0},{3,5},{5,3},{4,6},{6,4},{7,15},{15,7},{14,12},{12,14},... | collective-permute-start | bytes 589832 | tf_op jit(solution)/shard_map/ppermute | solution.py:509
  36.6 6.7 %collective-permute-start.2 = (f32[2,3,8,8,128]{4,3,2,1,0:T(8,128)S(1)}, f32[2,3,8,8,128]{4,3,2,1,0:T(8,128)S(1)}, u32[]{:S(2)}, u32[]{:S(2)}) collective-permute-start(f32[2,3,8,8,128]{4,3,2,1,0:T(8,128)S(1)} %get-tuple-element.29.own_ref.refs_3_), channel_id=1, source_target_pairs={{1,3},{3,1},{2,4},{4,2},{5,7},{7,5},{6,14},{14,6},{15,13},{13,15},... | collective-permute-start | bytes 589832 | tf_op jit(solution)/shard_map/ppermute | solution.py:510
  44.5 2.8 %collective-permute-start.3 = (f32[3,8,8,128]{3,2,1,0:T(8,128)S(1)}, f32[3,8,8,128]{3,2,1,0:T(8,128)S(1)}, u32[]{:S(2)}, u32[]{:S(2)}) collective-permute-start(f32[3,8,8,128]{3,2,1,0:T(8,128)S(1)} %get-tuple-element.34), channel_id=1, source_target_pairs={{0,1},{1,0},{2,3},{3,2},{4,5},{5,4},{6,7},{7,6},{8,9},{9,8},{10,11... | collective-permute-start | bytes 294920 | tf_op jit(solution)/shard_map/ppermute | solution.py:521
  47.5 7.3 %collective-permute-start.4 = (f32[2,3,8,8,128]{4,3,2,1,0:T(8,128)S(1)}, f32[2,3,8,8,128]{4,3,2,1,0:T(8,128)S(1)}, u32[]{:S(2)}, u32[]{:S(2)}) collective-permute-start(f32[2,3,8,8,128]{4,3,2,1,0:T(8,128)S(1)} %get-tuple-element.37.own_ref.refs_4_), channel_id=1, source_target_pairs={{0,2},{2,0},{3,5},{5,3},{4,6},{6,4},{7,15},{15,7},{14,12},{12,14},... | collective-permute-start | bytes 589832 | tf_op jit(solution)/shard_map/ppermute | solution.py:509
  47.6 7.2 %collective-permute-start.5 = (f32[2,3,8,8,128]{4,3,2,1,0:T(8,128)S(1)}, f32[2,3,8,8,128]{4,3,2,1,0:T(8,128)S(1)}, u32[]{:S(2)}, u32[]{:S(2)}) collective-permute-start(f32[2,3,8,8,128]{4,3,2,1,0:T(8,128)S(1)} %get-tuple-element.37.own_ref.refs_4_), channel_id=1, source_target_pairs={{1,3},{3,1},{2,4},{4,2},{5,7},{7,5},{6,14},{14,6},{15,13},{13,15},... | collective-permute-start | bytes 589832 | tf_op jit(solution)/shard_map/ppermute | solution.py:510
  55.9 2.4 %collective-permute-start.6 = (f32[3,8,8,128]{3,2,1,0:T(8,128)S(1)}, f32[3,8,8,128]{3,2,1,0:T(8,128)S(1)}, u32[]{:S(2)}, u32[]{:S(2)}) collective-permute-start(f32[3,8,8,128]{3,2,1,0:T(8,128)S(1)} %get-tuple-element.41), channel_id=1, source_target_pairs={{0,1},{1,0},{2,3},{3,2},{4,5},{5,4},{6,7},{7,6},{8,9},{9,8},{10,11... | collective-permute-start | bytes 294920 | tf_op jit(solution)/shard_map/ppermute | solution.py:521
  57.4 1.8 %copy-start = (f32[2,16,3,1024]{3,1,2,0:T(8,128)S(1)}, f32[2,16,3,1024]{3,1,2,0:T(8,128)}, u32[]{:S(2)}) copy-start(f32[2,16,3,1024]{3,1,2,0:T(8,128)} %param.4) | copy-start | bytes 1179652
  58.4 0.7 copy-start.1
  58.4 7.3 %collective-permute-start.7 = (f32[2,3,8,8,128]{4,3,2,1,0:T(8,128)S(1)}, f32[2,3,8,8,128]{4,3,2,1,0:T(8,128)S(1)}, u32[]{:S(2)}, u32[]{:S(2)}) collective-permute-start(f32[2,3,8,8,128]{4,3,2,1,0:T(8,128)S(1)} %get-tuple-element.43.own_ref.refs_5_), channel_id=1, source_target_pairs={{0,2},{2,0},{3,5},{5,3},{4,6},{6,4},{7,15},{15,7},{14,12},{12,14},... | collective-permute-start | bytes 589832 | tf_op jit(solution)/shard_map/ppermute | solution.py:509
  58.5 7.2 %collective-permute-start.8 = (f32[2,3,8,8,128]{4,3,2,1,0:T(8,128)S(1)}, f32[2,3,8,8,128]{4,3,2,1,0:T(8,128)S(1)}, u32[]{:S(2)}, u32[]{:S(2)}) collective-permute-start(f32[2,3,8,8,128]{4,3,2,1,0:T(8,128)S(1)} %get-tuple-element.43.own_ref.refs_5_), channel_id=1, source_target_pairs={{1,3},{3,1},{2,4},{4,2},{5,7},{7,5},{6,14},{14,6},{15,13},{13,15},... | collective-permute-start | bytes 589832 | tf_op jit(solution)/shard_map/ppermute | solution.py:510
  66.9 2.5 %collective-permute-start.9 = (f32[3,8,8,128]{3,2,1,0:T(8,128)S(1)}, f32[3,8,8,128]{3,2,1,0:T(8,128)S(1)}, u32[]{:S(2)}, u32[]{:S(2)}) collective-permute-start(f32[3,8,8,128]{3,2,1,0:T(8,128)S(1)} %get-tuple-element.47), channel_id=1, source_target_pairs={{0,1},{1,0},{2,3},{3,2},{4,5},{5,4},{6,7},{7,6},{8,9},{9,8},{10,11... | collective-permute-start | bytes 294920 | tf_op jit(solution)/shard_map/ppermute | solution.py:521
  69.9 1.4 %collective-permute-start.10 = (f32[256,128]{1,0:T(8,128)S(1)}, f32[256,128]{1,0:T(8,128)S(1)}, u32[]{:S(2)}, u32[]{:S(2)}) collective-permute-start(f32[256,128]{1,0:T(8,128)S(1)} %get-tuple-element.49), channel_id=1, source_target_pairs={{0,1},{1,0},{2,3},{3,2},{4,5},{5,4},{6,7},{7,6},{8,9},{9,8},{10,11... | collective-permute-start | bytes 393224 | tf_op jit(solution)/shard_map/ppermute | solution.py:536

commit v7 on v6

--- a/solution.py
+++ b/solution.py
@@ -14,6 +14,7 @@
 CHIPS = NZ * NY * NX
 LONS = 8
 FIELDS = 3
+CELLS = 2 * FIELDS * LONS
 TM = ("z", "y")
 GRID = ("x", "c")
 ZYX = ("z", "y", "x")
@@ -161,19 +162,24 @@
     )
 
 
-def chain_first(terms_of, decay_ref, pairs_ref, carry_ref, weigh_ref):
+def chain_first(terms_of, decay_ref, pairs_ref, carry_ref, weigh_ref, both_of=None):
     pair = iota(1) // 8
     for f in range(FIELDS):
         for col in range(LONS):
             decay = decay_ref[f, col]
-            c0, c1 = terms_of(f, col)
-            both = c0 + decay * c1
+            if both_of is None:
+                c0, c1 = terms_of(f, col)
+                both = c0 + decay * c1
+            else:
+                both = both_of(f, col)
             if pairs_ref is not None:
                 pairs_ref[0, f, col] = both
                 pairs_ref[1, f, col] = c1
-            at = 8 * (LONS * f + col)
-            weigh_ref[at : at + 8, :] = powers(decay * decay, pair, (1, 2, 4, 8)) * both
-    carry_ref[...] = bands_summed(weigh_ref[...]).reshape(FIELDS, LONS, 8, 128)
+            if carry_ref is not None:
+                at = 8 * (LONS * f + col)
+                weigh_ref[at : at + 8, :] = powers(decay * decay, pair, (1, 2, 4, 8)) * both
+    if carry_ref is not None:
+        carry_ref[...] = bands_summed(weigh_ref[...]).reshape(FIELDS, LONS, 8, 128)
 
 
 def chain_local(both, c1, decay, pair):
@@ -279,8 +285,9 @@
 
 
 def fine_kernel(
-    odd_ref, own_ref, one_ref, two_ref, decay_ref, pairs_ref, carry_ref, state_ref, weigh_ref
+    odd_ref, own_ref, one_ref, two_ref, decay_ref, pairs_ref, *rest
 ):
+    carry_ref, state_ref, weigh_ref = rest if len(rest) == 3 else (None, *rest, None)
     odd = odd_ref[0] == 1
     lane = iota(1)
     band = lane % 8
@@ -370,64 +377,98 @@
     chain_first(terms, decay_ref, pairs_ref, carry_ref, weigh_ref)
 
 
-def finish_kernel(core_ref, *refs):
-    zeros = refs[0:3]
-    aboves = refs[3:6]
-    first_ref, second_ref, carry_ref, power_ref, misfit_ref = refs[6:11]
-    mine_ref, other_ref, turn_ref, back_ref = refs[11:]
+def emphases(core):
+    first = (2 * (iota(1) // 8 + 16 * core)).astype(jnp.float32)
+    return [1.0 + 2.0 * (first + j) / 63.0 for j in range(2)]
+
+
+def so_far_kernel(core_ref, *refs):
+    zeros, aboves = refs[0:ITERS], refs[ITERS : 2 * ITERS]
+    misfit_ref, out_ref = refs[2 * ITERS :]
+    emphasis = emphases(core_ref[0])
+    sums = [jnp.zeros((8, 128), jnp.float32) for _ in range(2 * ITERS - 2)]
+    for f in range(FIELDS):
+        for col in range(LONS):
+            for j in range(2):
+                parts = [
+                    zeros[n][f, col] if j == 0 else aboves[n][0, f, col] for n in range(ITERS)
+                ]
+                total = parts[0]
+                for n in range(1, ITERS):
+                    total = total + parts[n]
+                    changed, size = emphasis[j] * (parts[n] * parts[n]), emphasis[j] * (total * total)
+                    sums[n - 1] = sums[n - 1] + changed
+                    sums[ITERS + n - 2] = sums[ITERS + n - 2] + size
+                out_ref[(j * FIELDS + f) * LONS + col] = total
+    for at, value in enumerate(sums + [misfit_ref[...]]):
+        out_ref[CELLS + at] = value
+
+
+def finish_kernel(
+    core_ref,
+    pairs_ref,
+    other_pairs_ref,
+    total_ref,
+    other_total_ref,
+    decay_ref,
+    out_ref,
+    weigh_ref,
+    carry_ref,
+    turn_ref,
+    back_ref,
+):
     low = core_ref[0] == 0
     pair = iota(1) // 8
-    subwindow = (2 * (pair + jnp.where(low, 0, 16))).astype(jnp.float32)
-    emphasis = [1.0 + 2.0 * (subwindow + j) / 63.0 for j in range(2)]
-    sums = [jnp.zeros((8, 128), jnp.float32) for _ in range(2 * ITERS)]
+    pairs = (pairs_ref, other_pairs_ref)
+    totals = (total_ref, other_total_ref)
+
+    def of_half(half, refs, *at):
+        mine, other = refs[0][at], refs[1][at]
+        return jnp.where(low, mine, other) if half == 0 else jnp.where(low, other, mine)
+
+    chain_first(
+        lambda f, col: None,
+        decay_ref,
+        None,
+        carry_ref,
+        weigh_ref,
+        both_of=lambda f, col: of_half(1, pairs, 0, f, col),
+    )
+    change = size = jnp.zeros((8, 128), jnp.float32)
     result = {}
-    for f in range(FIELDS):
-        for col in range(LONS):
-            carry = jnp.where(low, carry_ref[f, col], 0.0)
-            last = (
-                first_ref[f, col] + power_ref[0, f, col] * carry,
-                second_ref[f, col] + power_ref[1, f, col] * carry,
-            )
-            for j in range(2):
-                so_far = zeros[0][f, col] if j == 0 else aboves[0][0, f, col]
-                for n in range(ITERS):
-                    if n == ITERS - 1:
-                        change = last[j]
-                    else:
-                        change = zeros[n + 1][f, col] if j == 0 else aboves[n + 1][0, f, col]
-                    so_far = so_far + change
-                    sums[n] = sums[n] + emphasis[j] * (change * change)
-                    sums[ITERS + n] = sums[ITERS + n] + emphasis[j] * (so_far * so_far)
-                result[j, f, col] = so_far
+    for half in range(2):
+        emphasis = emphases(half)
+        for f in range(FIELDS):
+            for col in range(LONS):
+                decay = decay_ref[f, col]
+                both, c1 = (of_half(half, pairs, i, f, col) for i in range(2))
+                if half == 0:
+                    enters = jnp.where(pair == 15, decay * carry_ref[f, col], 0.0)
+                    both, c1 = both + decay * enters, c1 + enters
+                for j, value in enumerate(chain_local(both, c1, decay, pair)):
+                    total = of_half(half, totals, (j * FIELDS + f) * LONS + col) + value
+                    change = change + emphasis[j] * (value * value)
+                    size = size + emphasis[j] * (total * total)
+                    result[half, j, f, col] = total
     row = iota(0)
+    sums = [total_ref[CELLS + at] + other_total_ref[CELLS + at] for at in range(2 * ITERS - 1)]
+    counted = sums[0 : ITERS - 1] + [change, sums[-1]] + sums[ITERS - 1 : 2 * ITERS - 2] + [size]
     parts = jnp.zeros((8, 128), jnp.float32)
-    for at, part in enumerate(sums[:ITERS] + [misfit_ref[...]] + sums[ITERS:]):
+    for at, part in enumerate(counted):
         parts = jnp.where(row == at, jnp.sum(part, axis=0, keepdims=True), parts)
     ones = jnp.ones((128, 128), jnp.float32)
-    totals = jnp.dot(parts, ones, precision=lax.Precision.HIGHEST)
-    turn_ref[48:56, :] = totals
-    for s in range(4):
-        for half in range(2):
-            at = 64 * half
-            for j in range(2):
-                for f in range(FIELDS):
-                    to = at + 24 * j + 8 * f
-                    turn_ref[to : to + 8, :] = result[j, f, s + 4 * half]
-        back_ref[...] = turn_ref[...].T
-        evens = back_ref[pl.ds(0, 64, stride=2), :]
-        odds = back_ref[pl.ds(1, 64, stride=2), :]
-        mine_ref[pl.ds(s, 64, stride=4), :] = jnp.where(low, evens, odds)
-        other_ref[pl.ds(s, 64, stride=4), :] = jnp.where(low, odds, evens)
-
-
-def join_kernel(core_ref, mine_ref, got_ref, out_ref):
-    low = core_ref[0] == 0
-    lane = lax.broadcasted_iota(jnp.int32, (256, 128), 1)
-    counted = (lane & 120) == 48
-    mine, got = mine_ref[...], got_ref[...]
-    total = mine + got
-    out_ref[0:256, :] = jnp.where(counted, total, jnp.where(low, mine, got))
-    out_ref[256:512, :] = jnp.where(counted, total, jnp.where(low, got, mine))
+    turn_ref[48:56, :] = jnp.dot(parts, ones, precision=lax.Precision.HIGHEST)
+    for half in range(2):
+        for s in range(4):
+            for side in range(2):
+                for j in range(2):
+                    for f in range(FIELDS):
+                        to = 64 * side + 24 * j + 8 * f
+                        turn_ref[to : to + 8, :] = result[half, j, f, s + 4 * side]
+            back_ref[...] = turn_ref[...].T
+            evens = back_ref[pl.ds(0, 64, stride=2), :]
+            odds = back_ref[pl.ds(1, 64, stride=2), :]
+            out_ref[pl.ds(256 * half + s, 64, stride=4), :] = jnp.where(low, evens, odds)
 
 
 def unpack_kernel(in_ref, out_ref, misfit_ref, changes_ref, rows_ref):
@@ -508,33 +549,42 @@
         aboves.append(above)
         side_one = lax.ppermute(above, ALL, swap_pairs(0))
         side_two = lax.ppermute(above, ALL, swap_pairs(1))
-        pairs, carry = call(
+        last = iteration == ITERS - 1
+        found = call(
             fine_kernel,
-            (both, field),
+            both if last else (both, field),
             (tile_odd,),
             above,
             side_one,
             side_two,
             decay,
-            scratch=[pltpu.VMEM((2 * FIELDS * 3 * LONS * 24, 128), jnp.float32), weigh],
+            scratch=[pltpu.VMEM((2 * FIELDS * 3 * LONS * 24, 128), jnp.float32)]
+            + ([] if last else [weigh]),
         )
-        carry = lax.ppermute(carry, "c", SIBLING)
-        first, second = call(scan_kernel, (field, field), (), pairs, decay)
-    mine, away = call(
-        finish_kernel,
-        (shape(256, 128), shape(256, 128)),
+        pairs, carry = (found, None) if last else found
+        if not last:
+            carry = lax.ppermute(carry, "c", SIBLING)
+            first, second = call(scan_kernel, (field, field), (), pairs, decay)
+    total = call(
+        so_far_kernel,
+        shape(CELLS + 2 * ITERS - 1, 8, 128),
         (core_arg,),
         *zeros,
         *aboves,
-        first,
-        second,
-        carry,
-        power,
         misfit_part,
-        scratch=[square, square],
-    )
-    other = lax.ppermute(away, "c", SIBLING)
-    back = call(join_kernel, shape(512, 128), (core_arg,), mine, other)
+    )
+    other_total, other_pairs = (lax.ppermute(value, "c", SIBLING) for value in (total, pairs))
+    back = call(
+        finish_kernel,
+        shape(512, 128),
+        (core_arg,),
+        pairs,
+        other_pairs,
+        total,
+        other_total,
+        decay,
+        scratch=[weigh, pltpu.VMEM((FIELDS, LONS, 8, 128), jnp.float32), square, square],
+    )
     home = lax.all_to_all(back.reshape(CHIPS, 4, 128), ZYX, 0, 0).reshape(512, 128)
     adjoint, misfit, changes = call(
         unpack_kernel,

time: 92.1 us -> 91.1 us (0.989)
  waiting for transfers between devices: 23.7 us -> 22.4 us
    ppermute x1 -> x2, starting transfers between devices: 0.45 us -> 2.28 us  [per_device(): lax.ppermute(value, 'c', SIBLING)]
    ppermute x3 -> x2, starting transfers between devices: 4.86 us -> 3.26 us  [per_device(): carry = lax.ppermute(carry, 'c', SIBLING)]
    pallas_call x13 -> x12, Pallas kernels: 8.91 us -> 9.12 us  [call(): pl.pallas_call(kernel, out_shape=outs, in_specs=[smem] * len(scalars) + [...]
  transfers between devices with their start and end apart: 11 -> 11, of which waited for: 8 -> 7; matrix products, arithmetic and copies ran while one was open for 0% -> 0% of each run, Pallas kernels for 1% -> 2%
where the time goes in v7:
time: 91.1 us; the launch traced here: 90.9 us
  blocking collectives  49 us (54%)
  waiting for transfers between devices  22.4 us (25%)
  Pallas kernels  9.12 us (10%)
  starting transfers between devices  9.05 us (10%)
    all_to_all x1, blocking collectives, per_device(): lax.all_to_all(sent.reshape(CHIPS, 4, 128), ZYX, 0, 0).reshape(512, 128)  29.5 us
    all_to_all x1, blocking collectives, per_device(): lax.all_to_all(back.reshape(CHIPS, 4, 128), ZYX, 0, 0).reshape(512, 128)  19.5 us
    ppermute x3, waiting for transfers between devices, per_device(): side_one = lax.ppermute(above, ALL, swap_pairs(0))  19.1 us
    pallas_call x12, Pallas kernels, call(): pl.pallas_call(kernel, out_shape=outs, in_specs=[smem] * len(scalars) + [...  9.12 us
    ppermute x2, starting transfers between devices, per_device(): carry = lax.ppermute(carry, 'c', SIBLING)  3.26 us
    ppermute x1, starting transfers between devices, per_device(): other = lax.ppermute(got, 'c', SIBLING)  2.69 us
    ppermute x2, starting transfers between devices, per_device(): lax.ppermute(value, 'c', SIBLING)  2.28 us
  transfers between devices with their start and end apart: 11, of which 7 were waited for; matrix products, arithmetic and copies ran while one was open for 0% of the time, Pallas kernels for 2%

profile of v7, /device:TPU:1, one launch (start us, length us, event | category | flops | bytes accessed | tf_op | source)
XLA Modules:
  0.0 90.9 jit_solution(11269413052074922946)
XLA Ops:
  0.6 1.6 %shard_map.67 = f32[512,128]{1,0:T(8,128)S(1)} custom-call(s32[1]{0:T(128)} %bitcast.2.place_ref, f32[2,3,16,1024]{3,2,1,0:T(8,128)} %bitcast.17, f32[2,16]{1,0:T(2,128)} %weight_ref.1, s32[2,16]{1,0:T(2,128)} %block_ref.1, f32[3,8,1024]{2,1,0:T(8,128)} %decay_ref.1), custom_call_target="tpu_custom_call" | custom-call | tf_op jit(solution)/shard_map/pallas_call | solution.py:64
  2.3 29.5 %all_to_all.10 = f32[128,4,128]{2,1,0:T(4,128)S(1)} all-to-all(f32[128,4,128]{2,1,0:T(4,128)S(1)} %bitcast.15), channel_id=1, replica_groups=mesh['z'=8,'y'=4,'x'=4,'c'=2] {'z','y','x'}, dimensions={0} | all-to-all | bytes 524288 | tf_op jit(solution)/shard_map/all_to_all | solution.py:522
  31.8 2.7 %collective-permute-start = (f32[512,128]{1,0:T(8,128)S(1)}, f32[512,128]{1,0:T(8,128)S(1)}, u32[]{:S(2)}, u32[]{:S(2)}) collective-permute-start(f32[512,128]{1,0:T(8,128)S(1)} %bitcast.12), channel_id=1, source_target_pairs={{0,1},{1,0},{2,3},{3,2},{4,5},{5,4},{6,7},{7,6},{8,9},{9,8},{10,11... | collective-permute-start | bytes 786440 | tf_op jit(solution)/shard_map/ppermute | solution.py:523
  34.5 1.2 %collective-permute-done.other_ref = f32[512,128]{1,0:T(8,128)S(1)} collective-permute-done((f32[512,128]{1,0:T(8,128)S(1)}, f32[512,128]{1,0:T(8,128)S(1)}, u32[]{:S(2)}, u32[]{:S(2)}) %collective-permute-start) | collective-permute-done | bytes 262176 | tf_op jit(solution)/shard_map/ppermute | solution.py:523
  35.7 0.8 shard_map.68
  36.6 0.4 collective-permute-start.2
  37.0 6.4 %collective-permute-done.1.one_ref = f32[2,3,8,8,128]{4,3,2,1,0:T(8,128)S(1)} collective-permute-done((f32[2,3,8,8,128]{4,3,2,1,0:T(8,128)S(1)}, f32[2,3,8,8,128]{4,3,2,1,0:T(8,128)S(1)}, u32[]{:S(2)}, u32[]{:S(2)}) %collective-permute-start.1) | collective-permute-done | bytes 196640 | tf_op jit(solution)/shard_map/ppermute | solution.py:550
  43.4 1.2 %shard_map.69 = (f32[2,3,8,8,128]{4,3,2,1,0:T(8,128)S(1)}, f32[3,8,8,128]{3,2,1,0:T(8,128)S(1)}) custom-call(s32[1]{0:T(128)} %bitcast.1.odd_ref, f32[2,3,8,8,128]{4,3,2,1,0:T(8,128)S(1)} %get-tuple-element.22.own_ref.refs_3_, f32[2,3,8,8,128]{4,3,2,1,0:T(8,128)S(1)} %collective-permute-done.1.one_ref, ...), custom_call_target="tpu_custom_call" | custom-call | tf_op jit(solution)/shard_map/pallas_call | solution.py:64
  44.6 1.9 %collective-permute-start.3 = (f32[3,8,8,128]{3,2,1,0:T(8,128)S(1)}, f32[3,8,8,128]{3,2,1,0:T(8,128)S(1)}, u32[]{:S(2)}, u32[]{:S(2)}) collective-permute-start(f32[3,8,8,128]{3,2,1,0:T(8,128)S(1)} %get-tuple-element.27), channel_id=1, source_target_pairs={{0,1},{1,0},{2,3},{3,2},{4,5},{5,4},{6,7},{7,6},{8,9},{9,8},{10,11... | collective-permute-start | bytes 294920 | tf_op jit(solution)/shard_map/ppermute | solution.py:566
  46.4 0.4 shard_map.70
  46.8 0.6 collective-permute-done.3.carry_ref
  48.1 6.7 %collective-permute-done.4.one_ref = f32[2,3,8,8,128]{4,3,2,1,0:T(8,128)S(1)} collective-permute-done((f32[2,3,8,8,128]{4,3,2,1,0:T(8,128)S(1)}, f32[2,3,8,8,128]{4,3,2,1,0:T(8,128)S(1)}, u32[]{:S(2)}, u32[]{:S(2)}) %collective-permute-start.4) | collective-permute-done | bytes 196640 | tf_op jit(solution)/shard_map/ppermute | solution.py:550
  54.8 1.2 %shard_map.72 = (f32[2,3,8,8,128]{4,3,2,1,0:T(8,128)S(1)}, f32[3,8,8,128]{3,2,1,0:T(8,128)S(1)}) custom-call(s32[1]{0:T(128)} %bitcast.1.odd_ref, f32[2,3,8,8,128]{4,3,2,1,0:T(8,128)S(1)} %get-tuple-element.29.own_ref.refs_4_, f32[2,3,8,8,128]{4,3,2,1,0:T(8,128)S(1)} %collective-permute-done.4.one_ref, ...), custom_call_target="tpu_custom_call" | custom-call | tf_op jit(solution)/shard_map/pallas_call | solution.py:64
  56.0 1.4 %collective-permute-start.6 = (f32[3,8,8,128]{3,2,1,0:T(8,128)S(1)}, f32[3,8,8,128]{3,2,1,0:T(8,128)S(1)}, u32[]{:S(2)}, u32[]{:S(2)}) collective-permute-start(f32[3,8,8,128]{3,2,1,0:T(8,128)S(1)} %get-tuple-element.33), channel_id=1, source_target_pairs={{0,1},{1,0},{2,3},{3,2},{4,5},{5,4},{6,7},{7,6},{8,9},{9,8},{10,11... | collective-permute-start | bytes 294920 | tf_op jit(solution)/shard_map/ppermute | solution.py:566
  57.5 0.4 shard_map.73
  57.9 0.4 collective-permute-done.6.carry_ref
  58.7 0.9 collective-permute-start.10
  59.6 6.1 %collective-permute-done.7.one_ref = f32[2,3,8,8,128]{4,3,2,1,0:T(8,128)S(1)} collective-permute-done((f32[2,3,8,8,128]{4,3,2,1,0:T(8,128)S(1)}, f32[2,3,8,8,128]{4,3,2,1,0:T(8,128)S(1)}, u32[]{:S(2)}, u32[]{:S(2)}) %collective-permute-start.7) | collective-permute-done | bytes 196640 | tf_op jit(solution)/shard_map/ppermute | solution.py:550
  65.7 1.0 %shard_map.75.pairs_ref = f32[2,3,8,8,128]{4,3,2,1,0:T(8,128)S(1)} custom-call(s32[1]{0:T(128)} %bitcast.1.odd_ref, f32[2,3,8,8,128]{4,3,2,1,0:T(8,128)S(1)} %get-tuple-element.34.own_ref.refs_5_, f32[2,3,8,8,128]{4,3,2,1,0:T(8,128)S(1)} %collective-permute-done.7.one_ref, f32[2,3,8,8,128]{4,3,2,1,0:T(8,128)S(1)} %collective-permute-done.8.two_ref, ...), custom_call_target="tpu_custom_call" | custom-call | tf_op jit(solution)/shard_map/pallas_call | solution.py:64
  66.7 1.4 %collective-permute-start.9 = (f32[2,3,8,8,128]{4,3,2,1,0:T(8,128)S(1)}, f32[2,3,8,8,128]{4,3,2,1,0:T(8,128)S(1)}, u32[]{:S(2)}, u32[]{:S(2)}) collective-permute-start(f32[2,3,8,8,128]{4,3,2,1,0:T(8,128)S(1)} %shard_map.75.pairs_ref), channel_id=1, source_target_pairs={{0,1},{1,0},{2,3},{3,2},{4,5},{5,4},{6,7},{7,6},{8,9},{9,8},{10,11... | collective-permute-start | bytes 589832 | tf_op jit(solution)/shard_map/ppermute | solution.py:576
  68.2 1.1 %collective-permute-done.9.other_pairs_ref = f32[2,3,8,8,128]{4,3,2,1,0:T(8,128)S(1)} collective-permute-done((f32[2,3,8,8,128]{4,3,2,1,0:T(8,128)S(1)}, f32[2,3,8,8,128]{4,3,2,1,0:T(8,128)S(1)}, u32[]{:S(2)}, u32[]{:S(2)}) %collective-permute-start.9) | collective-permute-done | bytes 196640 | tf_op jit(solution)/shard_map/ppermute | solution.py:576
  69.2 1.1 %shard_map.77 = f32[512,128]{1,0:T(8,128)S(1)} custom-call(s32[1]{0:T(128)} %bitcast.core_ref, f32[2,3,8,8,128]{4,3,2,1,0:T(8,128)S(1)} %shard_map.75.pairs_ref, f32[2,3,8,8,128]{4,3,2,1,0:T(8,128)S(1)} %collective-permute-done.9.other_pairs_ref, f32[53,8,128]{2,1,0:T(8,128)S(1)} %shard_map.76.total_ref, ...), custom_call_target="tpu_custom_call" | custom-call | tf_op jit(solution)/shard_map/pallas_call | solution.py:64
  70.3 19.5 %all_to_all.11 = f32[128,4,128]{2,1,0:T(4,128)S(1)} all-to-all(f32[128,4,128]{2,1,0:T(4,128)S(1)} %bitcast.16), channel_id=1, replica_groups=mesh['z'=8,'y'=4,'x'=4,'c'=2] {'z','y','x'}, dimensions={0} | all-to-all | bytes 524288 | tf_op jit(solution)/shard_map/all_to_all | solution.py:588
  89.8 1.1 %shard_map.78 = (f32[2,3,8,1024]{3,2,1,0:T(8,128)}, f32[1,1]{1,0:T(1,128)}, f32[1,3]{1,0:T(1,128)}) custom-call(f32[512,128]{1,0:T(8,128)S(1)} %bitcast.14), custom_call_target="tpu_custom_call" | custom-call | tf_op jit(solution)/shard_map/pallas_call | solution.py:64
  (20 shorter events, 1.3 us)
Async XLA Ops:
  31.8 3.8 %collective-permute-start = (f32[512,128]{1,0:T(8,128)S(1)}, f32[512,128]{1,0:T(8,128)S(1)}, u32[]{:S(2)}, u32[]{:S(2)}) collective-permute-start(f32[512,128]{1,0:T(8,128)S(1)} %bitcast.12), channel_id=1, source_target_pairs={{0,1},{1,0},{2,3},{3,2},{4,5},{5,4},{6,7},{7,6},{8,9},{9,8},{10,11... | collective-permute-start | bytes 786440 | tf_op jit(solution)/shard_map/ppermute | solution.py:523
  36.5 6.8 %collective-permute-start.1 = (f32[2,3,8,8,128]{4,3,2,1,0:T(8,128)S(1)}, f32[2,3,8,8,128]{4,3,2,1,0:T(8,128)S(1)}, u32[]{:S(2)}, u32[]{:S(2)}) collective-permute-start(f32[2,3,8,8,128]{4,3,2,1,0:T(8,128)S(1)} %get-tuple-element.22.own_ref.refs_3_), channel_id=1, source_target_pairs={{0,2},{2,0},{3,5},{5,3},{4,6},{6,4},{7,15},{15,7},{14,12},{12,14},... | collective-permute-start | bytes 589832 | tf_op jit(solution)/shard_map/ppermute | solution.py:550
  36.6 6.7 %collective-permute-start.2 = (f32[2,3,8,8,128]{4,3,2,1,0:T(8,128)S(1)}, f32[2,3,8,8,128]{4,3,2,1,0:T(8,128)S(1)}, u32[]{:S(2)}, u32[]{:S(2)}) collective-permute-start(f32[2,3,8,8,128]{4,3,2,1,0:T(8,128)S(1)} %get-tuple-element.22.own_ref.refs_3_), channel_id=1, source_target_pairs={{1,3},{3,1},{2,4},{4,2},{5,7},{7,5},{6,14},{14,6},{15,13},{13,15},... | collective-permute-start | bytes 589832 | tf_op jit(solution)/shard_map/ppermute | solution.py:551
  44.6 2.8 %collective-permute-start.3 = (f32[3,8,8,128]{3,2,1,0:T(8,128)S(1)}, f32[3,8,8,128]{3,2,1,0:T(8,128)S(1)}, u32[]{:S(2)}, u32[]{:S(2)}) collective-permute-start(f32[3,8,8,128]{3,2,1,0:T(8,128)S(1)} %get-tuple-element.27), channel_id=1, source_target_pairs={{0,1},{1,0},{2,3},{3,2},{4,5},{5,4},{6,7},{7,6},{8,9},{9,8},{10,11... | collective-permute-start | bytes 294920 | tf_op jit(solution)/shard_map/ppermute | solution.py:566
  47.4 0.7 copy-start.1
  47.5 9.9 %copy-start = (f32[2,16,3,1024]{3,1,2,0:T(8,128)S(1)}, f32[2,16,3,1024]{3,1,2,0:T(8,128)}, u32[]{:S(2)}) copy-start(f32[2,16,3,1024]{3,1,2,0:T(8,128)} %param.4) | copy-start | bytes 1179652
  47.5 7.3 %collective-permute-start.4 = (f32[2,3,8,8,128]{4,3,2,1,0:T(8,128)S(1)}, f32[2,3,8,8,128]{4,3,2,1,0:T(8,128)S(1)}, u32[]{:S(2)}, u32[]{:S(2)}) collective-permute-start(f32[2,3,8,8,128]{4,3,2,1,0:T(8,128)S(1)} %get-tuple-element.29.own_ref.refs_4_), channel_id=1, source_target_pairs={{0,2},{2,0},{3,5},{5,3},{4,6},{6,4},{7,15},{15,7},{14,12},{12,14},... | collective-permute-start | bytes 589832 | tf_op jit(solution)/shard_map/ppermute | solution.py:550
  47.6 7.2 %collective-permute-start.5 = (f32[2,3,8,8,128]{4,3,2,1,0:T(8,128)S(1)}, f32[2,3,8,8,128]{4,3,2,1,0:T(8,128)S(1)}, u32[]{:S(2)}, u32[]{:S(2)}) collective-permute-start(f32[2,3,8,8,128]{4,3,2,1,0:T(8,128)S(1)} %get-tuple-element.29.own_ref.refs_4_), channel_id=1, source_target_pairs={{1,3},{3,1},{2,4},{4,2},{5,7},{7,5},{6,14},{14,6},{15,13},{13,15},... | collective-permute-start | bytes 589832 | tf_op jit(solution)/shard_map/ppermute | solution.py:551
  56.0 2.3 %collective-permute-start.6 = (f32[3,8,8,128]{3,2,1,0:T(8,128)S(1)}, f32[3,8,8,128]{3,2,1,0:T(8,128)S(1)}, u32[]{:S(2)}, u32[]{:S(2)}) collective-permute-start(f32[3,8,8,128]{3,2,1,0:T(8,128)S(1)} %get-tuple-element.33), channel_id=1, source_target_pairs={{0,1},{1,0},{2,3},{3,2},{4,5},{5,4},{6,7},{7,6},{8,9},{9,8},{10,11... | collective-permute-start | bytes 294920 | tf_op jit(solution)/shard_map/ppermute | solution.py:566
  58.4 7.3 %collective-permute-start.7 = (f32[2,3,8,8,128]{4,3,2,1,0:T(8,128)S(1)}, f32[2,3,8,8,128]{4,3,2,1,0:T(8,128)S(1)}, u32[]{:S(2)}, u32[]{:S(2)}) collective-permute-start(f32[2,3,8,8,128]{4,3,2,1,0:T(8,128)S(1)} %get-tuple-element.34.own_ref.refs_5_), channel_id=1, source_target_pairs={{0,2},{2,0},{3,5},{5,3},{4,6},{6,4},{7,15},{15,7},{14,12},{12,14},... | collective-permute-start | bytes 589832 | tf_op jit(solution)/shard_map/ppermute | solution.py:550
  58.5 7.2 %collective-permute-start.8 = (f32[2,3,8,8,128]{4,3,2,1,0:T(8,128)S(1)}, f32[2,3,8,8,128]{4,3,2,1,0:T(8,128)S(1)}, u32[]{:S(2)}, u32[]{:S(2)}) collective-permute-start(f32[2,3,8,8,128]{4,3,2,1,0:T(8,128)S(1)} %get-tuple-element.34.own_ref.refs_5_), channel_id=1, source_target_pairs={{1,3},{3,1},{2,4},{4,2},{5,7},{7,5},{6,14},{14,6},{15,13},{13,15},... | collective-permute-start | bytes 589832 | tf_op jit(solution)/shard_map/ppermute | solution.py:551
  58.7 9.4 %collective-permute-start.10 = (f32[53,8,128]{2,1,0:T(8,128)S(1)}, f32[53,8,128]{2,1,0:T(8,128)S(1)}, u32[]{:S(2)}, u32[]{:S(2)}) collective-permute-start(f32[53,8,128]{2,1,0:T(8,128)S(1)} %shard_map.76.total_ref), channel_id=1, source_target_pairs={{0,1},{1,0},{2,3},{3,2},{4,5},{5,4},{6,7},{7,6},{8,9},{9,8},{10,11... | collective-permute-start | bytes 651272 | tf_op jit(solution)/shard_map/ppermute | solution.py:576
  66.7 2.5 %collective-permute-start.9 = (f32[2,3,8,8,128]{4,3,2,1,0:T(8,128)S(1)}, f32[2,3,8,8,128]{4,3,2,1,0:T(8,128)S(1)}, u32[]{:S(2)}, u32[]{:S(2)}) collective-permute-start(f32[2,3,8,8,128]{4,3,2,1,0:T(8,128)S(1)} %shard_map.75.pairs_ref), channel_id=1, source_target_pairs={{0,1},{1,0},{2,3},{3,2},{4,5},{5,4},{6,7},{7,6},{8,9},{9,8},{10,11... | collective-permute-start | bytes 589832 | tf_op jit(solution)/shard_map/ppermute | solution.py:576

commit v8 on v7

--- a/solution.py
+++ b/solution.py
@@ -97,15 +97,19 @@
     copies = [
         pltpu.make_async_copy(weight_ref, weights_ref, sems.at[0]),
         pltpu.make_async_copy(block_ref, blocks_ref, sems.at[1]),
-        pltpu.make_async_copy(departure_ref, values_ref, sems.at[2]),
-        pltpu.make_async_copy(decay_ref, decays_ref, sems.at[3]),
+        pltpu.make_async_copy(departure_ref.at[0], values_ref.at[0], sems.at[2]),
+        pltpu.make_async_copy(departure_ref.at[1], values_ref.at[1], sems.at[3]),
+        pltpu.make_async_copy(decay_ref, decays_ref, sems.at[4]),
     ]
     for copy in copies:
         copy.start()
-    for copy in copies:
+    for copy in copies[:3]:
         copy.wait()
     block = lax.broadcasted_iota(jnp.int32, (8, 16), 0)
     for j in range(2):
+        if j == 1:
+            for copy in copies[3:]:
+                copy.wait()
         emphasis = 1.0 + 2.0 * (place_ref[0] * 2 + j).astype(jnp.float32) / 63.0
         choose = jnp.where(
             blocks_ref[j : j + 1, :] == block, emphasis * weights_ref[j : j + 1, :], 0.0
@@ -204,12 +208,28 @@
     return power
 
 
+def send_halo(odd_ref, above_ref, one_ref, two_ref):
+    odd = odd_ref[0] == 1
+    for j in range(2):
+        for f in range(FIELDS - 1):
+            for col in range(LONS):
+                one_ref[j, LONS * f + col] = two_ref[j, LONS * f + col] = above_ref[j, f, col]
+        for col in range(LONS - 1):
+            near_west, near_east = above_ref[j, 2, col], above_ref[j, 2, col + 1]
+            at = LONS * (FIELDS - 1) + col
+            one_ref[j, at] = jnp.where(odd, near_west, near_east)
+            two_ref[j, at] = jnp.where(odd, near_east, near_west)
+
+
 def open_kernel(
     core_ref,
+    odd_ref,
     mine_ref,
     other_ref,
     zero_ref,
     above_ref,
+    one_ref,
+    two_ref,
     decay_ref,
     power_ref,
     turn_ref,
@@ -270,9 +290,21 @@
             zero_ref[f, col] = value
             above_ref[0, f, col] = second
             above_ref[1, f, col] = jnp.where(pair < 15, later(value, 1), carry)
-
-
-def close_kernel(core_ref, first_ref, second_ref, carry_ref, power_ref, zero_ref, above_ref):
+    send_halo(odd_ref, above_ref, one_ref, two_ref)
+
+
+def close_kernel(
+    core_ref,
+    odd_ref,
+    first_ref,
+    second_ref,
+    carry_ref,
+    power_ref,
+    zero_ref,
+    above_ref,
+    one_ref,
+    two_ref,
+):
     low = core_ref[0] == 0
     pair = iota(1) // 8
     for f in range(FIELDS):
@@ -282,6 +314,7 @@
             zero_ref[f, col] = value
             above_ref[0, f, col] = second_ref[f, col] + power_ref[1, f, col] * carry
             above_ref[1, f, col] = jnp.where(pair < 15, later(value, 1), carry)
+    send_halo(odd_ref, above_ref, one_ref, two_ref)
 
 
 def fine_kernel(
@@ -318,11 +351,16 @@
 
     for j in range(2):
         for f in range(FIELDS):
+            skipped = 1 if f == 2 else 0
+            for at in range(LONS - skipped):
+                one, two = one_ref[j, LONS * f + at], two_ref[j, LONS * f + at]
+                put(j, f, at + skipped, jnp.where(odd, one, two))
+                put(j, f, 2 * LONS + at, jnp.where(odd, two, one))
             for at in range(LONS):
-                one, two = one_ref[j, f, at], two_ref[j, f, at]
-                put(j, f, at, jnp.where(odd, one, two))
                 put(j, f, LONS + at, own_ref[j, f, at])
-                put(j, f, 2 * LONS + at, jnp.where(odd, two, one))
+            if skipped:
+                put(j, f, 0, jnp.zeros((8, 128), jnp.float32))
+                put(j, f, width - 1, jnp.zeros((8, 128), jnp.float32))
             edges(j, f, 0, width)
 
     keep = 1.0 / diffusion - 4.0
@@ -363,7 +401,8 @@
                 ) + (wave_new * (p_next - p_last) - turn * q[col])
                 if step < STEPS - 1:
                     put(j, 1, col, q1)
-                    put(j, 2, col, r1)
+                    if low < col < high - 1:
+                        put(j, 2, col, r1)
                 else:
                     for f, value in enumerate((p[col], q1, r1)):
                         result[j, f, col - LONS] = value
@@ -406,11 +445,14 @@
 
 def finish_kernel(
     core_ref,
+    first_ref,
+    second_ref,
     pairs_ref,
     other_pairs_ref,
     total_ref,
     other_total_ref,
     decay_ref,
+    power_ref,
     out_ref,
     weigh_ref,
     carry_ref,
@@ -419,37 +461,41 @@
 ):
     low = core_ref[0] == 0
     pair = iota(1) // 8
-    pairs = (pairs_ref, other_pairs_ref)
-    totals = (total_ref, other_total_ref)
-
-    def of_half(half, refs, *at):
-        mine, other = refs[0][at], refs[1][at]
-        return jnp.where(low, mine, other) if half == 0 else jnp.where(low, other, mine)
-
     chain_first(
         lambda f, col: None,
         decay_ref,
         None,
         carry_ref,
         weigh_ref,
-        both_of=lambda f, col: of_half(1, pairs, 0, f, col),
+        both_of=lambda f, col: jnp.where(low, other_pairs_ref[0, f, col], pairs_ref[0, f, col]),
     )
     change = size = jnp.zeros((8, 128), jnp.float32)
     result = {}
-    for half in range(2):
-        emphasis = emphases(half)
-        for f in range(FIELDS):
-            for col in range(LONS):
-                decay = decay_ref[f, col]
-                both, c1 = (of_half(half, pairs, i, f, col) for i in range(2))
-                if half == 0:
-                    enters = jnp.where(pair == 15, decay * carry_ref[f, col], 0.0)
-                    both, c1 = both + decay * enters, c1 + enters
-                for j, value in enumerate(chain_local(both, c1, decay, pair)):
-                    total = of_half(half, totals, (j * FIELDS + f) * LONS + col) + value
-                    change = change + emphasis[j] * (value * value)
-                    size = size + emphasis[j] * (total * total)
-                    result[half, j, f, col] = total
+    emphasis = emphases(core_ref[0]), emphases(1 - core_ref[0])
+    for f in range(FIELDS):
+        for col in range(LONS):
+            decay, carry = decay_ref[f, col], carry_ref[f, col]
+            mine, others = jnp.where(low, carry, 0.0), jnp.where(low, 0.0, carry)
+            enters = jnp.where(pair == 15, decay * others, 0.0)
+            values = (
+                (
+                    first_ref[f, col] + power_ref[0, f, col] * mine,
+                    second_ref[f, col] + power_ref[1, f, col] * mine,
+                ),
+                chain_local(
+                    other_pairs_ref[0, f, col] + decay * enters,
+                    other_pairs_ref[1, f, col] + enters,
+                    decay,
+                    pair,
+                ),
+            )
+            for side, ref in enumerate((total_ref, other_total_ref)):
+                for j in range(2):
+                    value = values[side][j]
+                    total = ref[(j * FIELDS + f) * LONS + col] + value
+                    change = change + emphasis[side][j] * (value * value)
+                    size = size + emphasis[side][j] * (total * total)
+                    result[side, j, f, col] = total
     row = iota(0)
     sums = [total_ref[CELLS + at] + other_total_ref[CELLS + at] for at in range(2 * ITERS - 1)]
     counted = sums[0 : ITERS - 1] + [change, sums[-1]] + sums[ITERS - 1 : 2 * ITERS - 2] + [size]
@@ -458,17 +504,20 @@
         parts = jnp.where(row == at, jnp.sum(part, axis=0, keepdims=True), parts)
     ones = jnp.ones((128, 128), jnp.float32)
     turn_ref[48:56, :] = jnp.dot(parts, ones, precision=lax.Precision.HIGHEST)
-    for half in range(2):
-        for s in range(4):
+    for s in range(4):
+        kept = []
+        for which in range(2):
             for side in range(2):
                 for j in range(2):
                     for f in range(FIELDS):
                         to = 64 * side + 24 * j + 8 * f
-                        turn_ref[to : to + 8, :] = result[half, j, f, s + 4 * side]
+                        turn_ref[to : to + 8, :] = result[which, j, f, s + 4 * side]
             back_ref[...] = turn_ref[...].T
             evens = back_ref[pl.ds(0, 64, stride=2), :]
             odds = back_ref[pl.ds(1, 64, stride=2), :]
-            out_ref[pl.ds(256 * half + s, 64, stride=4), :] = jnp.where(low, evens, odds)
+            kept.append(jnp.where(low, evens, odds))
+        out_ref[pl.ds(s, 64, stride=4), :] = jnp.where(low, kept[0], kept[1])
+        out_ref[pl.ds(256 + s, 64, stride=4), :] = jnp.where(low, kept[1], kept[0])
 
 
 def unpack_kernel(in_ref, out_ref, misfit_ref, changes_ref, rows_ref):
@@ -516,7 +565,7 @@
             pltpu.VMEM((2, 16), jnp.int32),
             pltpu.VMEM((FIELDS, 8, 1024), jnp.float32),
             pltpu.VMEM((512, 128), jnp.float32),
-            pltpu.SemaphoreType.DMA((4,)),
+            pltpu.SemaphoreType.DMA((5,)),
         ],
     )
     got = lax.all_to_all(sent.reshape(CHIPS, 4, 128), ZYX, 0, 0).reshape(512, 128)
@@ -526,10 +575,11 @@
     both = shape(2, FIELDS, LONS, 8, 128)
     square = pltpu.VMEM((128, 128), jnp.float32)
     weigh = pltpu.VMEM((FIELDS * LONS * 8, 128), jnp.float32)
-    zero, above, decay, power = call(
+    halo = shape(2, LONS * FIELDS - 1, 8, 128)
+    zero, above, to_one, to_two, decay, power = call(
         open_kernel,
-        (field, both, field, both),
-        (core_arg,),
+        (field, both, halo, halo, field, both),
+        (core_arg, tile_odd),
         got,
         other,
         scratch=[
@@ -542,13 +592,19 @@
     zeros, aboves = [], []
     for iteration in range(ITERS):
         if iteration > 0:
-            zero, above = call(
-                close_kernel, (field, both), (core_arg,), first, second, carry, power
+            zero, above, to_one, to_two = call(
+                close_kernel,
+                (field, both, halo, halo),
+                (core_arg, tile_odd),
+                first,
+                second,
+                carry,
+                power,
             )
         zeros.append(zero)
         aboves.append(above)
-        side_one = lax.ppermute(above, ALL, swap_pairs(0))
-        side_two = lax.ppermute(above, ALL, swap_pairs(1))
+        side_one = lax.ppermute(to_one, ALL, swap_pairs(0))
+        side_two = lax.ppermute(to_two, ALL, swap_pairs(1))
         last = iteration == ITERS - 1
         found = call(
             fine_kernel,
@@ -564,7 +620,7 @@
         pairs, carry = (found, None) if last else found
         if not last:
             carry = lax.ppermute(carry, "c", SIBLING)
-            first, second = call(scan_kernel, (field, field), (), pairs, decay)
+        first, second = call(scan_kernel, (field, field), (), pairs, decay)
     total = call(
         so_far_kernel,
         shape(CELLS + 2 * ITERS - 1, 8, 128),
@@ -578,11 +634,14 @@
         finish_kernel,
         shape(512, 128),
         (core_arg,),
+        first,
+        second,
         pairs,
         other_pairs,
         total,
         other_total,
         decay,
+        power,
         scratch=[weigh, pltpu.VMEM((FIELDS, LONS, 8, 128), jnp.float32), square, square],
     )
     home = lax.all_to_all(back.reshape(CHIPS, 4, 128), ZYX, 0, 0).reshape(512, 128)

time: 91.1 us -> 90.6 us (level)
    pallas_call x12 -> x13, Pallas kernels: 9.12 us -> 9.53 us  [call(): pl.pallas_call(kernel, out_shape=outs, in_specs=[smem] * len(scalars) + [...]
where the time goes in v8:
time: 90.6 us; the launch traced here: 90.4 us
  blocking collectives  49 us (54%)
  waiting for transfers between devices  21.5 us (24%)
  Pallas kernels  9.53 us (11%)
  starting transfers between devices  9.05 us (10%)
    all_to_all x1, blocking collectives, per_device(): lax.all_to_all(sent.reshape(CHIPS, 4, 128), ZYX, 0, 0).reshape(512, 128)  29.5 us
    all_to_all x1, blocking collectives, per_device(): lax.all_to_all(back.reshape(CHIPS, 4, 128), ZYX, 0, 0).reshape(512, 128)  19.5 us
    ppermute x3, waiting for transfers between devices, per_device(): side_one = lax.ppermute(to_one, ALL, swap_pairs(0))  18.6 us
    pallas_call x13, Pallas kernels, call(): pl.pallas_call(kernel, out_shape=outs, in_specs=[smem] * len(scalars) + [...  9.53 us
    ppermute x2, starting transfers between devices, per_device(): carry = lax.ppermute(carry, 'c', SIBLING)  3.26 us
    ppermute x1, starting transfers between devices, per_device(): other = lax.ppermute(got, 'c', SIBLING)  2.69 us
    ppermute x2, starting transfers between devices, per_device(): lax.ppermute(value, 'c', SIBLING)  2.28 us
  transfers between devices with their start and end apart: 11, of which 7 were waited for; matrix products, arithmetic and copies ran while one was open for 0% of the time, Pallas kernels for 2%

profile of v8, /device:TPU:1, one launch (start us, length us, event | category | flops | bytes accessed | tf_op | source)
XLA Modules:
  0.0 90.4 jit_solution(12390647797935866604)
XLA Ops:
  0.6 1.7 %shard_map.67 = f32[512,128]{1,0:T(8,128)S(1)} custom-call(s32[1]{0:T(128)} %bitcast.2.place_ref, f32[2,3,16,1024]{3,2,1,0:T(8,128)} %bitcast.17, f32[2,16]{1,0:T(2,128)} %weight_ref.1, s32[2,16]{1,0:T(2,128)} %block_ref.1, f32[3,8,1024]{2,1,0:T(8,128)} %decay_ref.1), custom_call_target="tpu_custom_call" | custom-call | tf_op jit(solution)/shard_map/pallas_call | solution.py:64
  2.3 29.5 %all_to_all.10 = f32[128,4,128]{2,1,0:T(4,128)S(1)} all-to-all(f32[128,4,128]{2,1,0:T(4,128)S(1)} %bitcast.15), channel_id=1, replica_groups=mesh['z'=8,'y'=4,'x'=4,'c'=2] {'z','y','x'}, dimensions={0} | all-to-all | bytes 524288 | tf_op jit(solution)/shard_map/all_to_all | solution.py:571
  31.9 2.7 %collective-permute-start = (f32[512,128]{1,0:T(8,128)S(1)}, f32[512,128]{1,0:T(8,128)S(1)}, u32[]{:S(2)}, u32[]{:S(2)}) collective-permute-start(f32[512,128]{1,0:T(8,128)S(1)} %bitcast.12), channel_id=1, source_target_pairs={{0,1},{1,0},{2,3},{3,2},{4,5},{5,4},{6,7},{7,6},{8,9},{9,8},{10,11... | collective-permute-start | bytes 786440 | tf_op jit(solution)/shard_map/ppermute | solution.py:572
  34.6 1.2 %collective-permute-done.other_ref = f32[512,128]{1,0:T(8,128)S(1)} collective-permute-done((f32[512,128]{1,0:T(8,128)S(1)}, f32[512,128]{1,0:T(8,128)S(1)}, u32[]{:S(2)}, u32[]{:S(2)}) %collective-permute-start) | collective-permute-done | bytes 262176 | tf_op jit(solution)/shard_map/ppermute | solution.py:572
  35.7 0.8 shard_map.68
  37.1 6.2 %collective-permute-done.1.one_ref = f32[2,23,8,128]{3,2,1,0:T(8,128)S(1)} collective-permute-done((f32[2,23,8,128]{3,2,1,0:T(8,128)S(1)}, f32[2,23,8,128]{3,2,1,0:T(8,128)S(1)}, u32[]{:S(2)}, u32[]{:S(2)}) %collective-permute-start.1) | collective-permute-done | bytes 188448 | tf_op jit(solution)/shard_map/ppermute | solution.py:606
  43.3 1.2 %shard_map.69 = (f32[2,3,8,8,128]{4,3,2,1,0:T(8,128)S(1)}, f32[3,8,8,128]{3,2,1,0:T(8,128)S(1)}) custom-call(s32[1]{0:T(128)} %bitcast.1.odd_ref, f32[2,3,8,8,128]{4,3,2,1,0:T(8,128)S(1)} %get-tuple-element.30.own_ref.refs_3_, f32[2,23,8,128]{3,2,1,0:T(8,128)S(1)} %collective-permute-done.1.one_ref, f32[2,23,8,128]{3,2,1,0:T(8,128)S(1)} %collective-permute-done.2.two_ref, ...), custom_call_target="tpu_custom_call" | custom-call | tf_op jit(solution)/shard_map/pallas_call | solution.py:64
  44.4 1.9 %collective-permute-start.3 = (f32[3,8,8,128]{3,2,1,0:T(8,128)S(1)}, f32[3,8,8,128]{3,2,1,0:T(8,128)S(1)}, u32[]{:S(2)}, u32[]{:S(2)}) collective-permute-start(f32[3,8,8,128]{3,2,1,0:T(8,128)S(1)} %get-tuple-element.37), channel_id=1, source_target_pairs={{0,1},{1,0},{2,3},{3,2},{4,5},{5,4},{6,7},{7,6},{8,9},{9,8},{10,11... | collective-permute-start | bytes 294920 | tf_op jit(solution)/shard_map/ppermute | solution.py:622
  46.3 0.4 shard_map.70
  46.7 0.6 collective-permute-done.3.carry_ref
  48.0 6.5 %collective-permute-done.4.one_ref = f32[2,23,8,128]{3,2,1,0:T(8,128)S(1)} collective-permute-done((f32[2,23,8,128]{3,2,1,0:T(8,128)S(1)}, f32[2,23,8,128]{3,2,1,0:T(8,128)S(1)}, u32[]{:S(2)}, u32[]{:S(2)}) %collective-permute-start.4) | collective-permute-done | bytes 188448 | tf_op jit(solution)/shard_map/ppermute | solution.py:606
  54.5 1.2 %shard_map.72 = (f32[2,3,8,8,128]{4,3,2,1,0:T(8,128)S(1)}, f32[3,8,8,128]{3,2,1,0:T(8,128)S(1)}) custom-call(s32[1]{0:T(128)} %bitcast.1.odd_ref, f32[2,3,8,8,128]{4,3,2,1,0:T(8,128)S(1)} %get-tuple-element.39.own_ref.refs_4_, f32[2,23,8,128]{3,2,1,0:T(8,128)S(1)} %collective-permute-done.4.one_ref, f32[2,23,8,128]{3,2,1,0:T(8,128)S(1)} %collective-permute-done.5.two_ref, ...), custom_call_target="tpu_custom_call" | custom-call | tf_op jit(solution)/shard_map/pallas_call | solution.py:64
  55.7 1.4 %collective-permute-start.6 = (f32[3,8,8,128]{3,2,1,0:T(8,128)S(1)}, f32[3,8,8,128]{3,2,1,0:T(8,128)S(1)}, u32[]{:S(2)}, u32[]{:S(2)}) collective-permute-start(f32[3,8,8,128]{3,2,1,0:T(8,128)S(1)} %get-tuple-element.45), channel_id=1, source_target_pairs={{0,1},{1,0},{2,3},{3,2},{4,5},{5,4},{6,7},{7,6},{8,9},{9,8},{10,11... | collective-permute-start | bytes 294920 | tf_op jit(solution)/shard_map/ppermute | solution.py:622
  57.2 0.4 shard_map.73
  57.6 0.4 collective-permute-done.6.carry_ref
  58.5 0.9 collective-permute-start.10
  59.3 5.9 %collective-permute-done.7.one_ref = f32[2,23,8,128]{3,2,1,0:T(8,128)S(1)} collective-permute-done((f32[2,23,8,128]{3,2,1,0:T(8,128)S(1)}, f32[2,23,8,128]{3,2,1,0:T(8,128)S(1)}, u32[]{:S(2)}, u32[]{:S(2)}) %collective-permute-start.7) | collective-permute-done | bytes 188448 | tf_op jit(solution)/shard_map/ppermute | solution.py:606
  65.3 1.0 %shard_map.75.pairs_ref = f32[2,3,8,8,128]{4,3,2,1,0:T(8,128)S(1)} custom-call(s32[1]{0:T(128)} %bitcast.1.odd_ref, f32[2,3,8,8,128]{4,3,2,1,0:T(8,128)S(1)} %get-tuple-element.46.own_ref.refs_5_, f32[2,23,8,128]{3,2,1,0:T(8,128)S(1)} %collective-permute-done.7.one_ref, f32[2,23,8,128]{3,2,1,0:T(8,128)S(1)} %collective-permute-done.8.two_ref, ...), custom_call_target="tpu_custom_call" | custom-call | tf_op jit(solution)/shard_map/pallas_call | solution.py:64
  66.3 1.4 %collective-permute-start.9 = (f32[2,3,8,8,128]{4,3,2,1,0:T(8,128)S(1)}, f32[2,3,8,8,128]{4,3,2,1,0:T(8,128)S(1)}, u32[]{:S(2)}, u32[]{:S(2)}) collective-permute-start(f32[2,3,8,8,128]{4,3,2,1,0:T(8,128)S(1)} %shard_map.75.pairs_ref), channel_id=1, source_target_pairs={{0,1},{1,0},{2,3},{3,2},{4,5},{5,4},{6,7},{7,6},{8,9},{9,8},{10,11... | collective-permute-start | bytes 589832 | tf_op jit(solution)/shard_map/ppermute | solution.py:632
  67.7 0.4 shard_map.76
  68.1 0.7 collective-permute-done.9.other_pairs_ref
  68.7 1.1 %shard_map.78 = f32[512,128]{1,0:T(8,128)S(1)} custom-call(s32[1]{0:T(128)} %bitcast.core_ref, f32[3,8,8,128]{3,2,1,0:T(8,128)S(1)} %get-tuple-element.49.first_ref, f32[3,8,8,128]{3,2,1,0:T(8,128)S(1)} %get-tuple-element.50.second_ref, f32[2,3,8,8,128]{4,3,2,1,0:T(8,128)S(1)} %shard_map.75.pairs_ref, ...), custom_call_target="tpu_custom_call" | custom-call | tf_op jit(solution)/shard_map/pallas_call | solution.py:64
  69.8 19.5 %all_to_all.11 = f32[128,4,128]{2,1,0:T(4,128)S(1)} all-to-all(f32[128,4,128]{2,1,0:T(4,128)S(1)} %bitcast.16), channel_id=1, replica_groups=mesh['z'=8,'y'=4,'x'=4,'c'=2] {'z','y','x'}, dimensions={0} | all-to-all | bytes 524288 | tf_op jit(solution)/shard_map/all_to_all | solution.py:647
  89.3 1.1 %shard_map.79 = (f32[2,3,8,1024]{3,2,1,0:T(8,128)}, f32[1,1]{1,0:T(1,128)}, f32[1,3]{1,0:T(1,128)}) custom-call(f32[512,128]{1,0:T(8,128)S(1)} %bitcast.14), custom_call_target="tpu_custom_call" | custom-call | tf_op jit(solution)/shard_map/pallas_call | solution.py:64
  (21 shorter events, 1.7 us)
Async XLA Ops:
  31.9 3.8 %collective-permute-start = (f32[512,128]{1,0:T(8,128)S(1)}, f32[512,128]{1,0:T(8,128)S(1)}, u32[]{:S(2)}, u32[]{:S(2)}) collective-permute-start(f32[512,128]{1,0:T(8,128)S(1)} %bitcast.12), channel_id=1, source_target_pairs={{0,1},{1,0},{2,3},{3,2},{4,5},{5,4},{6,7},{7,6},{8,9},{9,8},{10,11... | collective-permute-start | bytes 786440 | tf_op jit(solution)/shard_map/ppermute | solution.py:572
  36.6 6.7 %collective-permute-start.1 = (f32[2,23,8,128]{3,2,1,0:T(8,128)S(1)}, f32[2,23,8,128]{3,2,1,0:T(8,128)S(1)}, u32[]{:S(2)}, u32[]{:S(2)}) collective-permute-start(f32[2,23,8,128]{3,2,1,0:T(8,128)S(1)} %get-tuple-element.31), channel_id=1, source_target_pairs={{0,2},{2,0},{3,5},{5,3},{4,6},{6,4},{7,15},{15,7},{14,12},{12,14},... | collective-permute-start | bytes 565256 | tf_op jit(solution)/shard_map/ppermute | solution.py:606
  36.7 6.6 %collective-permute-start.2 = (f32[2,23,8,128]{3,2,1,0:T(8,128)S(1)}, f32[2,23,8,128]{3,2,1,0:T(8,128)S(1)}, u32[]{:S(2)}, u32[]{:S(2)}) collective-permute-start(f32[2,23,8,128]{3,2,1,0:T(8,128)S(1)} %get-tuple-element.32), channel_id=1, source_target_pairs={{1,3},{3,1},{2,4},{4,2},{5,7},{7,5},{6,14},{14,6},{15,13},{13,15},... | collective-permute-start | bytes 565256 | tf_op jit(solution)/shard_map/ppermute | solution.py:607
  44.4 2.8 %collective-permute-start.3 = (f32[3,8,8,128]{3,2,1,0:T(8,128)S(1)}, f32[3,8,8,128]{3,2,1,0:T(8,128)S(1)}, u32[]{:S(2)}, u32[]{:S(2)}) collective-permute-start(f32[3,8,8,128]{3,2,1,0:T(8,128)S(1)} %get-tuple-element.37), channel_id=1, source_target_pairs={{0,1},{1,0},{2,3},{3,2},{4,5},{5,4},{6,7},{7,6},{8,9},{9,8},{10,11... | collective-permute-start | bytes 294920 | tf_op jit(solution)/shard_map/ppermute | solution.py:622
  47.2 0.7 copy-start.1
  47.4 9.7 %copy-start = (f32[2,16,3,1024]{3,1,2,0:T(8,128)S(1)}, f32[2,16,3,1024]{3,1,2,0:T(8,128)}, u32[]{:S(2)}) copy-start(f32[2,16,3,1024]{3,1,2,0:T(8,128)} %param.4) | copy-start | bytes 1179652
  47.4 7.1 %collective-permute-start.4 = (f32[2,23,8,128]{3,2,1,0:T(8,128)S(1)}, f32[2,23,8,128]{3,2,1,0:T(8,128)S(1)}, u32[]{:S(2)}, u32[]{:S(2)}) collective-permute-start(f32[2,23,8,128]{3,2,1,0:T(8,128)S(1)} %get-tuple-element.40), channel_id=1, source_target_pairs={{0,2},{2,0},{3,5},{5,3},{4,6},{6,4},{7,15},{15,7},{14,12},{12,14},... | collective-permute-start | bytes 565256 | tf_op jit(solution)/shard_map/ppermute | solution.py:606
  47.5 7.0 %collective-permute-start.5 = (f32[2,23,8,128]{3,2,1,0:T(8,128)S(1)}, f32[2,23,8,128]{3,2,1,0:T(8,128)S(1)}, u32[]{:S(2)}, u32[]{:S(2)}) collective-permute-start(f32[2,23,8,128]{3,2,1,0:T(8,128)S(1)} %get-tuple-element.41), channel_id=1, source_target_pairs={{1,3},{3,1},{2,4},{4,2},{5,7},{7,5},{6,14},{14,6},{15,13},{13,15},... | collective-permute-start | bytes 565256 | tf_op jit(solution)/shard_map/ppermute | solution.py:607
  55.7 2.3 %collective-permute-start.6 = (f32[3,8,8,128]{3,2,1,0:T(8,128)S(1)}, f32[3,8,8,128]{3,2,1,0:T(8,128)S(1)}, u32[]{:S(2)}, u32[]{:S(2)}) collective-permute-start(f32[3,8,8,128]{3,2,1,0:T(8,128)S(1)} %get-tuple-element.45), channel_id=1, source_target_pairs={{0,1},{1,0},{2,3},{3,2},{4,5},{5,4},{6,7},{7,6},{8,9},{9,8},{10,11... | collective-permute-start | bytes 294920 | tf_op jit(solution)/shard_map/ppermute | solution.py:622
  58.1 7.1 %collective-permute-start.7 = (f32[2,23,8,128]{3,2,1,0:T(8,128)S(1)}, f32[2,23,8,128]{3,2,1,0:T(8,128)S(1)}, u32[]{:S(2)}, u32[]{:S(2)}) collective-permute-start(f32[2,23,8,128]{3,2,1,0:T(8,128)S(1)} %get-tuple-element.47), channel_id=1, source_target_pairs={{0,2},{2,0},{3,5},{5,3},{4,6},{6,4},{7,15},{15,7},{14,12},{12,14},... | collective-permute-start | bytes 565256 | tf_op jit(solution)/shard_map/ppermute | solution.py:606
  58.2 7.0 %collective-permute-start.8 = (f32[2,23,8,128]{3,2,1,0:T(8,128)S(1)}, f32[2,23,8,128]{3,2,1,0:T(8,128)S(1)}, u32[]{:S(2)}, u32[]{:S(2)}) collective-permute-start(f32[2,23,8,128]{3,2,1,0:T(8,128)S(1)} %get-tuple-element.48), channel_id=1, source_target_pairs={{1,3},{3,1},{2,4},{4,2},{5,7},{7,5},{6,14},{14,6},{15,13},{13,15},... | collective-permute-start | bytes 565256 | tf_op jit(solution)/shard_map/ppermute | solution.py:607
  58.5 9.6 %collective-permute-start.10 = (f32[53,8,128]{2,1,0:T(8,128)S(1)}, f32[53,8,128]{2,1,0:T(8,128)S(1)}, u32[]{:S(2)}, u32[]{:S(2)}) collective-permute-start(f32[53,8,128]{2,1,0:T(8,128)S(1)} %shard_map.77.total_ref), channel_id=1, source_target_pairs={{0,1},{1,0},{2,3},{3,2},{4,5},{5,4},{6,7},{7,6},{8,9},{9,8},{10,11... | collective-permute-start | bytes 651272 | tf_op jit(solution)/shard_map/ppermute | solution.py:632
  66.3 2.5 %collective-permute-start.9 = (f32[2,3,8,8,128]{4,3,2,1,0:T(8,128)S(1)}, f32[2,3,8,8,128]{4,3,2,1,0:T(8,128)S(1)}, u32[]{:S(2)}, u32[]{:S(2)}) collective-permute-start(f32[2,3,8,8,128]{4,3,2,1,0:T(8,128)S(1)} %shard_map.75.pairs_ref), channel_id=1, source_target_pairs={{0,1},{1,0},{2,3},{3,2},{4,5},{5,4},{6,7},{7,6},{8,9},{9,8},{10,11... | collective-permute-start | bytes 589832 | tf_op jit(solution)/shard_map/ppermute | solution.py:632

commit v9 on v8

--- a/solution.py
+++ b/solution.py
@@ -97,19 +97,15 @@
     copies = [
         pltpu.make_async_copy(weight_ref, weights_ref, sems.at[0]),
         pltpu.make_async_copy(block_ref, blocks_ref, sems.at[1]),
-        pltpu.make_async_copy(departure_ref.at[0], values_ref.at[0], sems.at[2]),
-        pltpu.make_async_copy(departure_ref.at[1], values_ref.at[1], sems.at[3]),
-        pltpu.make_async_copy(decay_ref, decays_ref, sems.at[4]),
+        pltpu.make_async_copy(departure_ref, values_ref, sems.at[2]),
+        pltpu.make_async_copy(decay_ref, decays_ref, sems.at[3]),
     ]
     for copy in copies:
         copy.start()
-    for copy in copies[:3]:
+    for copy in copies:
         copy.wait()
     block = lax.broadcasted_iota(jnp.int32, (8, 16), 0)
     for j in range(2):
-        if j == 1:
-            for copy in copies[3:]:
-                copy.wait()
         emphasis = 1.0 + 2.0 * (place_ref[0] * 2 + j).astype(jnp.float32) / 63.0
         choose = jnp.where(
             blocks_ref[j : j + 1, :] == block, emphasis * weights_ref[j : j + 1, :], 0.0
@@ -521,10 +517,10 @@
 
 
 def unpack_kernel(in_ref, out_ref, misfit_ref, changes_ref, rows_ref):
-    sums = [in_ref[8 * v : 8 * v + 8, :] for v in range(64)]
+    sums = [in_ref[pl.ds(32 * v, 8, stride=4), :] for v in range(16)]
     while len(sums) > 1:
         sums = [a + b for a, b in zip(sums[::2], sums[1::2])]
-    total = pltpu.roll(sums[0] + pltpu.roll(sums[0], 4, 0), 80, 1)
+    total = pltpu.roll(jnp.broadcast_to(jnp.sum(sums[0], axis=0, keepdims=True), (8, 128)), 80, 1)
     misfit_ref[...] = total[0:1, 3:4]
     changes_ref[...] = (total / (pltpu.roll(total, 124, 1) + epsilon))[0:1, 0:ITERS]
     second = (lax.broadcasted_iota(jnp.int32, (128, 128), 0) & 7) >= 4
@@ -565,7 +561,7 @@
             pltpu.VMEM((2, 16), jnp.int32),
             pltpu.VMEM((FIELDS, 8, 1024), jnp.float32),
             pltpu.VMEM((512, 128), jnp.float32),
-            pltpu.SemaphoreType.DMA((5,)),
+            pltpu.SemaphoreType.DMA((4,)),
         ],
     )
     got = lax.all_to_all(sent.reshape(CHIPS, 4, 128), ZYX, 0, 0).reshape(512, 128)

time: 90.6 us -> 90.6 us (level)
  no operation moved by 1% of the time
where the time goes in v9:
time: 90.6 us; the launch traced here: 90.4 us
  blocking collectives  49 us (54%)
  waiting for transfers between devices  21.5 us (24%)
  Pallas kernels  9.47 us (10%)
  starting transfers between devices  9.05 us (10%)
    all_to_all x1, blocking collectives, per_device(): lax.all_to_all(sent.reshape(CHIPS, 4, 128), ZYX, 0, 0).reshape(512, 128)  29.5 us
    all_to_all x1, blocking collectives, per_device(): lax.all_to_all(back.reshape(CHIPS, 4, 128), ZYX, 0, 0).reshape(512, 128)  19.5 us
    ppermute x3, waiting for transfers between devices, per_device(): side_one = lax.ppermute(to_one, ALL, swap_pairs(0))  18.6 us
    pallas_call x13, Pallas kernels, call(): pl.pallas_call(kernel, out_shape=outs, in_specs=[smem] * len(scalars) + [...  9.47 us
    ppermute x2, starting transfers between devices, per_device(): carry = lax.ppermute(carry, 'c', SIBLING)  3.26 us
    ppermute x1, starting transfers between devices, per_device(): other = lax.ppermute(got, 'c', SIBLING)  2.69 us
    ppermute x2, starting transfers between devices, per_device(): lax.ppermute(value, 'c', SIBLING)  2.28 us
  transfers between devices with their start and end apart: 11, of which 7 were waited for; matrix products, arithmetic and copies ran while one was open for 0% of the time, Pallas kernels for 2%

profile of v9, /device:TPU:1, one launch (start us, length us, event | category | flops | bytes accessed | tf_op | source)
XLA Modules:
  0.0 90.4 jit_solution(7558927075388986833)
XLA Ops:
  0.6 1.6 %shard_map.67 = f32[512,128]{1,0:T(8,128)S(1)} custom-call(s32[1]{0:T(128)} %bitcast.2.place_ref, f32[2,3,16,1024]{3,2,1,0:T(8,128)} %bitcast.17, f32[2,16]{1,0:T(2,128)} %weight_ref.1, s32[2,16]{1,0:T(2,128)} %block_ref.1, f32[3,8,1024]{2,1,0:T(8,128)} %decay_ref.1), custom_call_target="tpu_custom_call" | custom-call | tf_op jit(solution)/shard_map/pallas_call | solution.py:64
  2.3 29.5 %all_to_all.10 = f32[128,4,128]{2,1,0:T(4,128)S(1)} all-to-all(f32[128,4,128]{2,1,0:T(4,128)S(1)} %bitcast.15), channel_id=1, replica_groups=mesh['z'=8,'y'=4,'x'=4,'c'=2] {'z','y','x'}, dimensions={0} | all-to-all | bytes 524288 | tf_op jit(solution)/shard_map/all_to_all | solution.py:567
  31.8 2.7 %collective-permute-start = (f32[512,128]{1,0:T(8,128)S(1)}, f32[512,128]{1,0:T(8,128)S(1)}, u32[]{:S(2)}, u32[]{:S(2)}) collective-permute-start(f32[512,128]{1,0:T(8,128)S(1)} %bitcast.12), channel_id=1, source_target_pairs={{0,1},{1,0},{2,3},{3,2},{4,5},{5,4},{6,7},{7,6},{8,9},{9,8},{10,11... | collective-permute-start | bytes 786440 | tf_op jit(solution)/shard_map/ppermute | solution.py:568
  34.5 1.2 %collective-permute-done.other_ref = f32[512,128]{1,0:T(8,128)S(1)} collective-permute-done((f32[512,128]{1,0:T(8,128)S(1)}, f32[512,128]{1,0:T(8,128)S(1)}, u32[]{:S(2)}, u32[]{:S(2)}) %collective-permute-start) | collective-permute-done | bytes 262176 | tf_op jit(solution)/shard_map/ppermute | solution.py:568
  35.7 0.8 shard_map.68
  37.0 6.2 %collective-permute-done.1.one_ref = f32[2,23,8,128]{3,2,1,0:T(8,128)S(1)} collective-permute-done((f32[2,23,8,128]{3,2,1,0:T(8,128)S(1)}, f32[2,23,8,128]{3,2,1,0:T(8,128)S(1)}, u32[]{:S(2)}, u32[]{:S(2)}) %collective-permute-start.1) | collective-permute-done | bytes 188448 | tf_op jit(solution)/shard_map/ppermute | solution.py:602
  43.2 1.2 %shard_map.69 = (f32[2,3,8,8,128]{4,3,2,1,0:T(8,128)S(1)}, f32[3,8,8,128]{3,2,1,0:T(8,128)S(1)}) custom-call(s32[1]{0:T(128)} %bitcast.1.odd_ref, f32[2,3,8,8,128]{4,3,2,1,0:T(8,128)S(1)} %get-tuple-element.30.own_ref.refs_3_, f32[2,23,8,128]{3,2,1,0:T(8,128)S(1)} %collective-permute-done.1.one_ref, f32[2,23,8,128]{3,2,1,0:T(8,128)S(1)} %collective-permute-done.2.two_ref, ...), custom_call_target="tpu_custom_call" | custom-call | tf_op jit(solution)/shard_map/pallas_call | solution.py:64
  44.4 1.9 %collective-permute-start.3 = (f32[3,8,8,128]{3,2,1,0:T(8,128)S(1)}, f32[3,8,8,128]{3,2,1,0:T(8,128)S(1)}, u32[]{:S(2)}, u32[]{:S(2)}) collective-permute-start(f32[3,8,8,128]{3,2,1,0:T(8,128)S(1)} %get-tuple-element.37), channel_id=1, source_target_pairs={{0,1},{1,0},{2,3},{3,2},{4,5},{5,4},{6,7},{7,6},{8,9},{9,8},{10,11... | collective-permute-start | bytes 294920 | tf_op jit(solution)/shard_map/ppermute | solution.py:618
  46.3 0.4 shard_map.70
  46.6 0.6 collective-permute-done.3.carry_ref
  47.9 6.5 %collective-permute-done.4.one_ref = f32[2,23,8,128]{3,2,1,0:T(8,128)S(1)} collective-permute-done((f32[2,23,8,128]{3,2,1,0:T(8,128)S(1)}, f32[2,23,8,128]{3,2,1,0:T(8,128)S(1)}, u32[]{:S(2)}, u32[]{:S(2)}) %collective-permute-start.4) | collective-permute-done | bytes 188448 | tf_op jit(solution)/shard_map/ppermute | solution.py:602
  54.4 1.2 %shard_map.72 = (f32[2,3,8,8,128]{4,3,2,1,0:T(8,128)S(1)}, f32[3,8,8,128]{3,2,1,0:T(8,128)S(1)}) custom-call(s32[1]{0:T(128)} %bitcast.1.odd_ref, f32[2,3,8,8,128]{4,3,2,1,0:T(8,128)S(1)} %get-tuple-element.39.own_ref.refs_4_, f32[2,23,8,128]{3,2,1,0:T(8,128)S(1)} %collective-permute-done.4.one_ref, f32[2,23,8,128]{3,2,1,0:T(8,128)S(1)} %collective-permute-done.5.two_ref, ...), custom_call_target="tpu_custom_call" | custom-call | tf_op jit(solution)/shard_map/pallas_call | solution.py:64
  55.6 1.4 %collective-permute-start.6 = (f32[3,8,8,128]{3,2,1,0:T(8,128)S(1)}, f32[3,8,8,128]{3,2,1,0:T(8,128)S(1)}, u32[]{:S(2)}, u32[]{:S(2)}) collective-permute-start(f32[3,8,8,128]{3,2,1,0:T(8,128)S(1)} %get-tuple-element.45), channel_id=1, source_target_pairs={{0,1},{1,0},{2,3},{3,2},{4,5},{5,4},{6,7},{7,6},{8,9},{9,8},{10,11... | collective-permute-start | bytes 294920 | tf_op jit(solution)/shard_map/ppermute | solution.py:618
  57.1 0.4 shard_map.73
  57.5 0.4 collective-permute-done.6.carry_ref
  58.4 0.9 collective-permute-start.10
  59.3 5.9 %collective-permute-done.7.one_ref = f32[2,23,8,128]{3,2,1,0:T(8,128)S(1)} collective-permute-done((f32[2,23,8,128]{3,2,1,0:T(8,128)S(1)}, f32[2,23,8,128]{3,2,1,0:T(8,128)S(1)}, u32[]{:S(2)}, u32[]{:S(2)}) %collective-permute-start.7) | collective-permute-done | bytes 188448 | tf_op jit(solution)/shard_map/ppermute | solution.py:602
  65.2 1.0 %shard_map.75.pairs_ref = f32[2,3,8,8,128]{4,3,2,1,0:T(8,128)S(1)} custom-call(s32[1]{0:T(128)} %bitcast.1.odd_ref, f32[2,3,8,8,128]{4,3,2,1,0:T(8,128)S(1)} %get-tuple-element.46.own_ref.refs_5_, f32[2,23,8,128]{3,2,1,0:T(8,128)S(1)} %collective-permute-done.7.one_ref, f32[2,23,8,128]{3,2,1,0:T(8,128)S(1)} %collective-permute-done.8.two_ref, ...), custom_call_target="tpu_custom_call" | custom-call | tf_op jit(solution)/shard_map/pallas_call | solution.py:64
  66.2 1.4 %collective-permute-start.9 = (f32[2,3,8,8,128]{4,3,2,1,0:T(8,128)S(1)}, f32[2,3,8,8,128]{4,3,2,1,0:T(8,128)S(1)}, u32[]{:S(2)}, u32[]{:S(2)}) collective-permute-start(f32[2,3,8,8,128]{4,3,2,1,0:T(8,128)S(1)} %shard_map.75.pairs_ref), channel_id=1, source_target_pairs={{0,1},{1,0},{2,3},{3,2},{4,5},{5,4},{6,7},{7,6},{8,9},{9,8},{10,11... | collective-permute-start | bytes 589832 | tf_op jit(solution)/shard_map/ppermute | solution.py:628
  67.6 0.4 shard_map.76
  68.0 0.7 collective-permute-done.9.other_pairs_ref
  68.7 1.1 %shard_map.78 = f32[512,128]{1,0:T(8,128)S(1)} custom-call(s32[1]{0:T(128)} %bitcast.core_ref, f32[3,8,8,128]{3,2,1,0:T(8,128)S(1)} %get-tuple-element.49.first_ref, f32[3,8,8,128]{3,2,1,0:T(8,128)S(1)} %get-tuple-element.50.second_ref, f32[2,3,8,8,128]{4,3,2,1,0:T(8,128)S(1)} %shard_map.75.pairs_ref, ...), custom_call_target="tpu_custom_call" | custom-call | tf_op jit(solution)/shard_map/pallas_call | solution.py:64
  69.8 19.5 %all_to_all.11 = f32[128,4,128]{2,1,0:T(4,128)S(1)} all-to-all(f32[128,4,128]{2,1,0:T(4,128)S(1)} %bitcast.16), channel_id=1, replica_groups=mesh['z'=8,'y'=4,'x'=4,'c'=2] {'z','y','x'}, dimensions={0} | all-to-all | bytes 524288 | tf_op jit(solution)/shard_map/all_to_all | solution.py:643
  89.3 1.1 %shard_map.79 = (f32[2,3,8,1024]{3,2,1,0:T(8,128)}, f32[1,1]{1,0:T(1,128)}, f32[1,3]{1,0:T(1,128)}) custom-call(f32[512,128]{1,0:T(8,128)S(1)} %bitcast.14), custom_call_target="tpu_custom_call" | custom-call | tf_op jit(solution)/shard_map/pallas_call | solution.py:64
  (21 shorter events, 1.7 us)
Async XLA Ops:
  31.8 3.8 %collective-permute-start = (f32[512,128]{1,0:T(8,128)S(1)}, f32[512,128]{1,0:T(8,128)S(1)}, u32[]{:S(2)}, u32[]{:S(2)}) collective-permute-start(f32[512,128]{1,0:T(8,128)S(1)} %bitcast.12), channel_id=1, source_target_pairs={{0,1},{1,0},{2,3},{3,2},{4,5},{5,4},{6,7},{7,6},{8,9},{9,8},{10,11... | collective-permute-start | bytes 786440 | tf_op jit(solution)/shard_map/ppermute | solution.py:568
  36.5 6.7 %collective-permute-start.1 = (f32[2,23,8,128]{3,2,1,0:T(8,128)S(1)}, f32[2,23,8,128]{3,2,1,0:T(8,128)S(1)}, u32[]{:S(2)}, u32[]{:S(2)}) collective-permute-start(f32[2,23,8,128]{3,2,1,0:T(8,128)S(1)} %get-tuple-element.31), channel_id=1, source_target_pairs={{0,2},{2,0},{3,5},{5,3},{4,6},{6,4},{7,15},{15,7},{14,12},{12,14},... | collective-permute-start | bytes 565256 | tf_op jit(solution)/shard_map/ppermute | solution.py:602
  36.6 6.6 %collective-permute-start.2 = (f32[2,23,8,128]{3,2,1,0:T(8,128)S(1)}, f32[2,23,8,128]{3,2,1,0:T(8,128)S(1)}, u32[]{:S(2)}, u32[]{:S(2)}) collective-permute-start(f32[2,23,8,128]{3,2,1,0:T(8,128)S(1)} %get-tuple-element.32), channel_id=1, source_target_pairs={{1,3},{3,1},{2,4},{4,2},{5,7},{7,5},{6,14},{14,6},{15,13},{13,15},... | collective-permute-start | bytes 565256 | tf_op jit(solution)/shard_map/ppermute | solution.py:603
  44.4 2.8 %collective-permute-start.3 = (f32[3,8,8,128]{3,2,1,0:T(8,128)S(1)}, f32[3,8,8,128]{3,2,1,0:T(8,128)S(1)}, u32[]{:S(2)}, u32[]{:S(2)}) collective-permute-start(f32[3,8,8,128]{3,2,1,0:T(8,128)S(1)} %get-tuple-element.37), channel_id=1, source_target_pairs={{0,1},{1,0},{2,3},{3,2},{4,5},{5,4},{6,7},{7,6},{8,9},{9,8},{10,11... | collective-permute-start | bytes 294920 | tf_op jit(solution)/shard_map/ppermute | solution.py:618
  47.2 0.7 copy-start.1
  47.3 9.7 %copy-start = (f32[2,16,3,1024]{3,1,2,0:T(8,128)S(1)}, f32[2,16,3,1024]{3,1,2,0:T(8,128)}, u32[]{:S(2)}) copy-start(f32[2,16,3,1024]{3,1,2,0:T(8,128)} %param.4) | copy-start | bytes 1179652
  47.3 7.1 %collective-permute-start.4 = (f32[2,23,8,128]{3,2,1,0:T(8,128)S(1)}, f32[2,23,8,128]{3,2,1,0:T(8,128)S(1)}, u32[]{:S(2)}, u32[]{:S(2)}) collective-permute-start(f32[2,23,8,128]{3,2,1,0:T(8,128)S(1)} %get-tuple-element.40), channel_id=1, source_target_pairs={{0,2},{2,0},{3,5},{5,3},{4,6},{6,4},{7,15},{15,7},{14,12},{12,14},... | collective-permute-start | bytes 565256 | tf_op jit(solution)/shard_map/ppermute | solution.py:602
  47.4 7.0 %collective-permute-start.5 = (f32[2,23,8,128]{3,2,1,0:T(8,128)S(1)}, f32[2,23,8,128]{3,2,1,0:T(8,128)S(1)}, u32[]{:S(2)}, u32[]{:S(2)}) collective-permute-start(f32[2,23,8,128]{3,2,1,0:T(8,128)S(1)} %get-tuple-element.41), channel_id=1, source_target_pairs={{1,3},{3,1},{2,4},{4,2},{5,7},{7,5},{6,14},{14,6},{15,13},{13,15},... | collective-permute-start | bytes 565256 | tf_op jit(solution)/shard_map/ppermute | solution.py:603
  55.6 2.3 %collective-permute-start.6 = (f32[3,8,8,128]{3,2,1,0:T(8,128)S(1)}, f32[3,8,8,128]{3,2,1,0:T(8,128)S(1)}, u32[]{:S(2)}, u32[]{:S(2)}) collective-permute-start(f32[3,8,8,128]{3,2,1,0:T(8,128)S(1)} %get-tuple-element.45), channel_id=1, source_target_pairs={{0,1},{1,0},{2,3},{3,2},{4,5},{5,4},{6,7},{7,6},{8,9},{9,8},{10,11... | collective-permute-start | bytes 294920 | tf_op jit(solution)/shard_map/ppermute | solution.py:618
  58.1 7.1 %collective-permute-start.7 = (f32[2,23,8,128]{3,2,1,0:T(8,128)S(1)}, f32[2,23,8,128]{3,2,1,0:T(8,128)S(1)}, u32[]{:S(2)}, u32[]{:S(2)}) collective-permute-start(f32[2,23,8,128]{3,2,1,0:T(8,128)S(1)} %get-tuple-element.47), channel_id=1, source_target_pairs={{0,2},{2,0},{3,5},{5,3},{4,6},{6,4},{7,15},{15,7},{14,12},{12,14},... | collective-permute-start | bytes 565256 | tf_op jit(solution)/shard_map/ppermute | solution.py:602
  58.2 7.0 %collective-permute-start.8 = (f32[2,23,8,128]{3,2,1,0:T(8,128)S(1)}, f32[2,23,8,128]{3,2,1,0:T(8,128)S(1)}, u32[]{:S(2)}, u32[]{:S(2)}) collective-permute-start(f32[2,23,8,128]{3,2,1,0:T(8,128)S(1)} %get-tuple-element.48), channel_id=1, source_target_pairs={{1,3},{3,1},{2,4},{4,2},{5,7},{7,5},{6,14},{14,6},{15,13},{13,15},... | collective-permute-start | bytes 565256 | tf_op jit(solution)/shard_map/ppermute | solution.py:603
  58.4 9.6 %collective-permute-start.10 = (f32[53,8,128]{2,1,0:T(8,128)S(1)}, f32[53,8,128]{2,1,0:T(8,128)S(1)}, u32[]{:S(2)}, u32[]{:S(2)}) collective-permute-start(f32[53,8,128]{2,1,0:T(8,128)S(1)} %shard_map.77.total_ref), channel_id=1, source_target_pairs={{0,1},{1,0},{2,3},{3,2},{4,5},{5,4},{6,7},{7,6},{8,9},{9,8},{10,11... | collective-permute-start | bytes 651272 | tf_op jit(solution)/shard_map/ppermute | solution.py:628
  66.2 2.5 %collective-permute-start.9 = (f32[2,3,8,8,128]{4,3,2,1,0:T(8,128)S(1)}, f32[2,3,8,8,128]{4,3,2,1,0:T(8,128)S(1)}, u32[]{:S(2)}, u32[]{:S(2)}) collective-permute-start(f32[2,3,8,8,128]{4,3,2,1,0:T(8,128)S(1)} %shard_map.75.pairs_ref), channel_id=1, source_target_pairs={{0,1},{1,0},{2,3},{3,2},{4,5},{5,4},{6,7},{7,6},{8,9},{9,8},{10,11... | collective-permute-start | bytes 589832 | tf_op jit(solution)/shard_map/ppermute | solution.py:628
